TPU v7x, 256 devices: a whole 4x4x8 slice. The times are simulated.
256 devices in a mesh: dp: 32 (over x, z), mp: 8 (over y, core).
Axes of the slice: x: 4, y: 4, z: 8, core: 2. Of those that a mesh axis runs over, the one named last changes fastest.
Arguments:
- query_emb: bfloat16 [8192, 768], P('dp'), may hold values from -6 to 6
- positive_list: int32 [8192], replicated, may hold values from 0 to 32767
- centroids: float32 [32768, 768], P(('dp', 'mp')), may hold values from -0.6 to 0.6
- first_moment: float32 [32768, 768], P(('dp', 'mp')), may hold values from -3 to 3
- second_moment: float32 [32768, 768], P(('dp', 'mp')), may hold values from 0.05 to 2
Outputs:
- new_centroids: float32 [32768, 768], P(('dp', 'mp'))
- new_first: float32 [32768, 768], P(('dp', 'mp'))
- new_second: float32 [32768, 768], P(('dp', 'mp'))
- mean_loss: float32 [], replicated
All inputs are finite; a program needn't handle non-finite values.
Results may differ from a plain program's by a relative error of at most 0.00097.
Values may be sent and summed in bfloat16 or wider, within the bound.
No kernel may reach another device: no remote copies, remote signals or barrier semaphores. Data moves between devices by JAX's collectives and lax.ppermute only.
A program may use at most 64 MiB of HBM per device.

v0:
```python
import functools

import jax
import jax.numpy as jnp
import numpy as np
from jax import lax
from jax.sharding import Mesh
from jax.sharding import PartitionSpec as P


DP = ("x", "z")
DP_MP = ("x", "z", "y", "c")

beta_first = 0.9
beta_second = 0.95
learn_rate = 0.01
epsilon = 1e-08
ROWS = 8192
HALF = 128
OWN = 128
HOPS = (1, 2, 3, 0)
ZERO = np.uint32(0)
SCALE = 4.0


def turn(size, step):
    return [(i, (i + step) % size) for i in range(size)]


SWAP = [(0, 1), (1, 0)]
OPPOSITE = [(z * 2 + c, (z + (1, -1)[c]) % 8 * 2 + c) for z in range(8) for c in range(2)]


def adam_update(centroids, first_moment, second_moment, gradient):
    new_first = beta_first * first_moment + (1.0 - beta_first) * gradient
    new_second = beta_second * second_moment + (1.0 - beta_second) * gradient * gradient
    new_centroids = centroids - learn_rate * new_first / (jnp.sqrt(new_second) + epsilon)
    return (new_centroids, new_first, new_second)


def join(*parts):
    top = functools.reduce(jnp.maximum, parts)
    joined = top + jnp.log(sum(jnp.exp(part - top) for part in parts))
    return jnp.where(lax.broadcasted_iota(jnp.int32, top.shape, 0) < 16, joined, sum(parts))


def over_lists(state, at_first):
    state = join(state, lax.ppermute(state, "c", SWAP))
    pair = join(state, lax.ppermute(state, ("z", "c"), OPPOSITE))
    some = lax.ppermute(pair, ("z", "c"), [(z * 2 + c, (z + (2, -1)[c]) % 8 * 2 + c) for z in range(8) for c in range(2)])
    rest = lax.ppermute(pair, ("z", "c"), [(z * 2 + 1, (z - 3) % 8 * 2 + 1) for z in range(8)])
    state = join(some, jnp.where(at_first, pair, rest))
    state = join(state, *[lax.ppermute(state, "y", turn(4, step)) for step in (2, 1, -1)])
    return join(state, lax.ppermute(state, "c", SWAP))


def is_target(targets):
    return lax.broadcasted_iota(jnp.int32, (4 * OWN, targets.shape[0]), 0) == targets[None, :]


def logits_of(rows, lists):
    return jnp.einsum("kd,rd->kr", lists, rows, preferred_element_type=jnp.float32)


def logits_of(rows, lists):
    return jnp.einsum("kd,rd->kr", lists, rows, preferred_element_type=jnp.float32)


def forward(rows, lists, targets):
    logits = logits_of(rows, lists)
    peak = jnp.max(logits, axis=0)
    logits, peak = lax.optimization_barrier((logits, peak))
    total = jnp.sum(jnp.exp(logits - peak[None, :]), axis=0)
    hit = jnp.sum(jnp.where(is_target(targets), logits, 0.0), axis=0)
    return (peak + jnp.log(total)).reshape(-1, HALF), jnp.sum(hit.reshape(-1, HALF), axis=0, keepdims=True)


def put(into, part, row):
    return lax.dynamic_update_slice(into, part.reshape(-1, HALF, part.shape[1]), (row, ZERO, ZERO))


def body(query_emb, positive_list, centroids):
    x, z, y, core = (lax.axis_index(name) for name in DP_MP)
    sign = 1 - 2 * core
    width = query_emb.shape[1]

    steps = [0, -1, 1, -2, 2, -3, 3, 4]
    firsts = [((z + sign * step) & 7) * 2 for step in steps]
    firsts = firsts[:7] + [firsts[7] + core, firsts[7] + 1 - core]
    firsts = [first.astype(jnp.uint32) for first in firsts]
    own_base, x_at, cut, at_first = (z * 8 + y * 2 + core) * OWN, x.astype(jnp.uint32), core.astype(jnp.uint32), core == 0

    part, blocks = query_emb, [query_emb]
    for k in range(3):
        part = lax.ppermute(part, ("z", "c"), OPPOSITE)
        if k == 0:
            part, positive_list, own_base, x, x_at, cut, at_first, *firsts = lax.optimization_barrier(
                (part, positive_list, own_base, x, x_at, cut, at_first, *firsts)
            )
        swapped = lax.ppermute(part, "c", SWAP)
        blocks += [part, swapped]
    part = lax.dynamic_slice(part.reshape(2, HALF, width), (cut, ZERO, ZERO), (1, HALF, width))[0]
    last = lax.ppermute(part, ("z", "c"), OPPOSITE)
    swapped = lax.ppermute(last, "c", SWAP)
    blocks = list(zip(blocks + [last, swapped], firsts))

    half = centroids.astype(jnp.bfloat16)
    lists = jnp.concatenate([lax.ppermute(half, "x", turn(4, -hop)) if hop else half for hop in HOPS])
    lists = lax.optimization_barrier(lists)

    targets = lax.dynamic_slice(positive_list.reshape(4, 2048), (x_at, ZERO), (1, 2048))[0] - own_base
    place = (((targets >> 13) - x + 3) & 3) * OWN + (targets & (OWN - 1))
    targets = jnp.where((targets & 8191) < OWN, place, -1)
    late = [lax.dynamic_slice(targets.reshape(16, HALF), (row, ZERO), (block.shape[0] // HALF, HALF)) for block, row in blocks[5:]]
    targets, *late = lax.optimization_barrier((targets, *[some.reshape(-1) for some in late]))
    rows = jnp.zeros((16, HALF, width), query_emb.dtype)
    for block, row in blocks[:5]:
        rows = put(rows, block, row)
    state, hit = forward(rows.reshape(-1, width), lists, targets)
    at = lax.broadcasted_iota(jnp.uint32, (16, HALF), 0)
    for i, (block, row) in enumerate(blocks[5:]):
        local, more = forward(block, lists, late[i])
        state, hit = jnp.where(at == row, local[:1], state), hit + more
        if i < 2:
            state = jnp.where(at - 1 == row, local[1:], state)
            rows = put(rows, block, row)
    state = jnp.concatenate([state, hit, jnp.zeros((7, HALF), jnp.float32)])
    for block, row in blocks[7:]:
        rows = put(rows, block, row)
    rows = rows.reshape(-1, width)
    state = over_lists(state, at_first)

    rows, lists, log_norm = lax.optimization_barrier((rows, lists, state[:16].reshape(-1)))
    hot = is_target(targets).astype(jnp.float32)
    weights = (jnp.exp(logits_of(rows, lists) - log_norm[None, :]) - hot).astype(jnp.bfloat16)
    weights = lax.optimization_barrier(weights)
    sent = jnp.dot(weights[: 3 * OWN], rows, preferred_element_type=jnp.float32)
    sent = (sent * SCALE).astype(jnp.float16)
    back = []
    for some, step in ((slice(128, 192), 2), (slice(192, 256), -2), (slice(0, 128), 1), (slice(256, 384), -1)):
        back.append(lax.ppermute(sent[some], "x", turn(4, step)).astype(jnp.float32))
    own = jnp.dot(weights[3 * OWN :], rows, preferred_element_type=jnp.float32)
    own = lax.optimization_barrier(own)
    at = lax.broadcasted_iota(jnp.int32, state.shape, 0)
    loss = jnp.full((8, 128), jnp.sum(jnp.where(at < 16, state, -state)))
    others = []
    for step in (2, 1, -1):
        others.append(lax.ppermute(loss, "x", turn(4, step)))
    gradient = own + (jnp.concatenate(back[:2]) + back[2] + back[3]) * (1.0 / SCALE)
    return (gradient, loss + others[0] + others[1] + others[2])


def shards(query_emb, positive_list, centroids, first_moment, second_moment):
    gradient, loss = body(query_emb, positive_list, centroids)
    new_centroids, new_first, new_second = adam_update(centroids, first_moment, second_moment, gradient)
    return (new_centroids, new_first, new_second, loss[0, 0] / ROWS)


def solution(mesh):
    split = Mesh(mesh.devices.reshape(4, 8, 4, 2), DP_MP)
    placed = (P(DP, None), P(), P(DP_MP, None), P(DP_MP, None), P(DP_MP, None))
    return jax.shard_map(
        shards,
        mesh=split,
        in_specs=placed,
        out_specs=(P(DP_MP, None), P(DP_MP, None), P(DP_MP, None), P()),
        check_vma=False,
    )
```

profile of v0, /device:TPU:1, one launch (start us, length us, event | category | flops | bytes accessed | tf_op | source)
XLA Modules:
  0.0 91.5 jit_solution(12328005782887820703)
XLA Ops:
  0.6 6.5 %collective-permute-start = (bf16[256,768]{1,0:T(8,128)(2,1)}, bf16[256,768]{1,0:T(8,128)(2,1)S(1)}, u32[]{:S(2)}, u32[]{:S(2)}) collective-permute-start(bf16[256,768]{1,0:T(8,128)(2,1)} %param.5), channel_id=1, source_target_pairs={{0,8},{1,57},{8,16},{9,1},{16,24},{17,9},{24,32},{25,17},{32,40},{... | collective-permute-start | bytes 1179656 | tf_op jit(solution)/shard_map/ppermute | solution.py:95
  7.1 1.0 %convert_element_type.64 = bf16[128,768]{1,0:T(8,128)(2,1)S(1)} convert(f32[128,768]{1,0:T(8,128)} %param.7) | non-fusion elementwise | flops 98304 | bytes 589824 | tf_op jit(solution)/shard_map/convert_element_type | solution.py:107
  8.1 1.3 %collective-permute-start.10 = (bf16[128,768]{1,0:T(8,128)(2,1)S(1)}, bf16[128,768]{1,0:T(8,128)(2,1)S(1)}, u32[]{:S(2)}, u32[]{:S(2)}) collective-permute-start(bf16[128,768]{1,0:T(8,128)(2,1)S(1)} %convert_element_type.64), channel_id=1, source_target_pairs={{0,64},{64,128},{128,192},{192,0},{1,65},{65,129},{129,193},{193,1... | collective-permute-start | bytes 589832 | tf_op jit(solution)/shard_map/ppermute | solution.py:108
  9.4 1.5 %collective-permute-start.8 = (bf16[128,768]{1,0:T(8,128)(2,1)S(1)}, bf16[128,768]{1,0:T(8,128)(2,1)S(1)}, u32[]{:S(2)}, u32[]{:S(2)}) collective-permute-start(bf16[128,768]{1,0:T(8,128)(2,1)S(1)} %convert_element_type.64), channel_id=1, source_target_pairs={{0,192},{64,0},{128,64},{192,128},{1,193},{65,1},{129,65},{193,129... | collective-permute-start | bytes 589832 | tf_op jit(solution)/shard_map/ppermute | solution.py:108
  10.9 1.5 %collective-permute-start.9 = (bf16[128,768]{1,0:T(8,128)(2,1)S(1)}, bf16[128,768]{1,0:T(8,128)(2,1)S(1)}, u32[]{:S(2)}, u32[]{:S(2)}) collective-permute-start(bf16[128,768]{1,0:T(8,128)(2,1)S(1)} %convert_element_type.64), channel_id=1, source_target_pairs={{0,128},{64,192},{128,0},{192,64},{1,129},{65,193},{129,1},{193,65... | collective-permute-start | bytes 589832 | tf_op jit(solution)/shard_map/ppermute | solution.py:108
  12.5 2.8 %collective-permute-done.10 = bf16[128,768]{1,0:T(8,128)(2,1)S(1)} collective-permute-done((bf16[128,768]{1,0:T(8,128)(2,1)S(1)}, bf16[128,768]{1,0:T(8,128)(2,1)S(1)}, u32[]{:S(2)}, u32[]{:S(2)}) %collective-permute-start.10) | collective-permute-done | bytes 196640 | tf_op jit(solution)/shard_map/ppermute | solution.py:108
  15.3 2.3 %collective-permute-done.8 = bf16[128,768]{1,0:T(8,128)(2,1)S(1)} collective-permute-done((bf16[128,768]{1,0:T(8,128)(2,1)S(1)}, bf16[128,768]{1,0:T(8,128)(2,1)S(1)}, u32[]{:S(2)}, u32[]{:S(2)}) %collective-permute-start.8) | collective-permute-done | bytes 196640 | tf_op jit(solution)/shard_map/ppermute | solution.py:108
  17.6 1.6 %collective-permute-done.9 = bf16[128,768]{1,0:T(8,128)(2,1)S(1)} collective-permute-done((bf16[128,768]{1,0:T(8,128)(2,1)S(1)}, bf16[128,768]{1,0:T(8,128)(2,1)S(1)}, u32[]{:S(2)}, u32[]{:S(2)}) %collective-permute-start.9) | collective-permute-done | bytes 196640 | tf_op jit(solution)/shard_map/ppermute | solution.py:108
  19.2 2.8 %collective-permute-start.2 = (bf16[256,768]{1,0:T(8,128)(2,1)S(1)}, bf16[256,768]{1,0:T(8,128)(2,1)S(1)}, u32[]{:S(2)}, u32[]{:S(2)}) collective-permute-start(bf16[256,768]{1,0:T(8,128)(2,1)S(1)} %collective-permute-done), channel_id=1, source_target_pairs={{0,8},{1,57},{8,16},{9,1},{16,24},{17,9},{24,32},{25,17},{32,40},{... | collective-permute-start | bytes 1179656 | tf_op jit(solution)/shard_map/ppermute | solution.py:95
  23.2 3.5 %collective-permute-done.2 = bf16[256,768]{1,0:T(8,128)(2,1)S(1)} collective-permute-done((bf16[256,768]{1,0:T(8,128)(2,1)S(1)}, bf16[256,768]{1,0:T(8,128)(2,1)S(1)}, u32[]{:S(2)}, u32[]{:S(2)}) %collective-permute-start.2) | collective-permute-done | bytes 393248 | tf_op jit(solution)/shard_map/ppermute | solution.py:95
  26.7 3.1 %collective-permute-start.4 = (bf16[256,768]{1,0:T(8,128)(2,1)S(1)}, bf16[256,768]{1,0:T(8,128)(2,1)S(1)}, u32[]{:S(2)}, u32[]{:S(2)}) collective-permute-start(bf16[256,768]{1,0:T(8,128)(2,1)S(1)} %collective-permute-done.2), channel_id=1, source_target_pairs={{0,8},{1,57},{8,16},{9,1},{16,24},{17,9},{24,32},{25,17},{32,40},{... | collective-permute-start | bytes 1179656 | tf_op jit(solution)/shard_map/ppermute | solution.py:95
  29.9 4.6 %collective-permute-done.4 = bf16[256,768]{1,0:T(8,128)(2,1)S(1)} collective-permute-done((bf16[256,768]{1,0:T(8,128)(2,1)S(1)}, bf16[256,768]{1,0:T(8,128)(2,1)S(1)}, u32[]{:S(2)}, u32[]{:S(2)}) %collective-permute-start.4) | collective-permute-done | bytes 393248 | tf_op jit(solution)/shard_map/ppermute | solution.py:95
  34.5 3.2 %collective-permute-start.6 = (bf16[128,768]{1,0:T(8,128)(2,1)S(1)}, bf16[128,768]{1,0:T(8,128)(2,1)S(1)}, u32[]{:S(2)}, u32[]{:S(2)}) collective-permute-start(bf16[128,768]{1,0:T(8,128)(2,1)S(1)} %dynamic-slice_bitcast_fusion), channel_id=1, source_target_pairs={{0,8},{1,57},{8,16},{9,1},{16,24},{17,9},{24,32},{25,17},{32,40},{... | collective-permute-start | bytes 589832 | tf_op jit(solution)/shard_map/ppermute | solution.py:103
  37.8 1.8 %fusion.35 = (f32[2048]{0:T(1024)S(1)}, f32[512,2048]{1,0:T(8,128)S(1)}) fusion(bf16[512,768]{1,0:T(8,128)(2,1)S(1)} %pad_maximum_fusion, bf16[2048,768]{1,0:T(8,128)(2,1)S(1)} %bitcast.62), kind=kOutput, calls=%fused_computation.94 | convolution fusion | flops 1611659264 | bytes 8134656 | tf_op jit(solution)/shard_map/kd,rd->kr/dot_general | solution.py:66
  39.6 1.1 %exponential_reduce_fusion = (f32[2048]{0:T(1024)S(1)}, f32[2048]{0:T(1024)S(1)}) fusion(f32[512,2048]{1,0:T(8,128)S(1)} %get-tuple-element.58, f32[2048]{0:T(1024)S(1)} %get-tuple-element.57, s32[2048]{0:T(1024)S(1)} %bitcast.76), kind=kLoop, calls=%fused_computation.3 | loop fusion | flops 5238784 | bytes 4227072 | tf_op jit(solution)/shard_map/reduce_sum | solution.py:73
  41.5 3.3 %collective-permute-start.7 = (bf16[128,768]{1,0:T(8,128)(2,1)S(1)}, bf16[128,768]{1,0:T(8,128)(2,1)S(1)}, u32[]{:S(2)}, u32[]{:S(2)}) collective-permute-start(bf16[128,768]{1,0:T(8,128)(2,1)S(1)} %collective-permute-done.6), channel_id=1, source_target_pairs={{0,1},{1,0},{2,3},{3,2},{4,5},{5,4},{6,7},{7,6},{8,9},{9,8},{10,11... | collective-permute-start | bytes 589832 | tf_op jit(solution)/shard_map/ppermute | solution.py:104
  49.0 2.3 %collective-permute-done.12 = f32[24,128]{1,0:T(8,128)S(1)} collective-permute-done((f32[24,128]{1,0:T(8,128)S(1)}, f32[24,128]{1,0:T(8,128)S(1)}, u32[]{:S(2)}, u32[]{:S(2)}) %collective-permute-start.12) | collective-permute-done | bytes 12320 | tf_op jit(solution)/shard_map/ppermute | solution.py:49
  51.4 1.4 %collective-permute-start.13 = (f32[24,128]{1,0:T(8,128)S(1)}, f32[24,128]{1,0:T(8,128)S(1)}, u32[]{:S(2)}, u32[]{:S(2)}) collective-permute-start(f32[24,128]{1,0:T(8,128)S(1)} %add_select_fusion.3), channel_id=1, source_target_pairs={{0,16},{1,57},{8,24},{9,1},{16,32},{17,9},{24,40},{25,17},{32,48},... | collective-permute-start | bytes 36872 | tf_op jit(solution)/shard_map/ppermute | solution.py:50
  52.9 4.4 %collective-permute-start.14 = (f32[24,128]{1,0:T(8,128)S(1)}, f32[24,128]{1,0:T(8,128)S(1)}, u32[]{:S(2)}, u32[]{:S(2)}) collective-permute-start(f32[24,128]{1,0:T(8,128)S(1)} %add_select_fusion.3), channel_id=1, source_target_pairs={{1,41},{9,49},{17,57},{25,1},{33,9},{41,17},{49,25},{57,33},{3,43}... | collective-permute-start | bytes 36872 | tf_op jit(solution)/shard_map/ppermute | solution.py:51
  57.3 1.8 %collective-permute-done.14 = f32[24,128]{1,0:T(8,128)S(1)} collective-permute-done((f32[24,128]{1,0:T(8,128)S(1)}, f32[24,128]{1,0:T(8,128)S(1)}, u32[]{:S(2)}, u32[]{:S(2)}) %collective-permute-start.14) | collective-permute-done | bytes 12320 | tf_op jit(solution)/shard_map/ppermute | solution.py:51
  59.1 3.0 %collective-permute-start.15 = (f32[24,128]{1,0:T(8,128)S(1)}, f32[24,128]{1,0:T(8,128)S(1)}, u32[]{:S(2)}, u32[]{:S(2)}) collective-permute-start(f32[24,128]{1,0:T(8,128)S(1)} %add_select_fusion.2), channel_id=1, source_target_pairs={{0,4},{2,6},{4,0},{6,2},{1,5},{3,7},{5,1},{7,3},{8,12},{10,14},{12... | collective-permute-start | bytes 36872 | tf_op jit(solution)/shard_map/ppermute | solution.py:53
  62.5 2.3 %collective-permute-start.17 = (f32[24,128]{1,0:T(8,128)S(1)}, f32[24,128]{1,0:T(8,128)S(1)}, u32[]{:S(2)}, u32[]{:S(2)}) collective-permute-start(f32[24,128]{1,0:T(8,128)S(1)} %add_select_fusion.2), channel_id=1, source_target_pairs={{0,6},{2,0},{4,2},{6,4},{1,7},{3,1},{5,3},{7,5},{8,14},{10,8},{12,... | collective-permute-start | bytes 36872 | tf_op jit(solution)/shard_map/ppermute | solution.py:53
  64.8 1.1 %collective-permute-done.16 = f32[24,128]{1,0:T(8,128)S(1)} collective-permute-done((f32[24,128]{1,0:T(8,128)S(1)}, f32[24,128]{1,0:T(8,128)S(1)}, u32[]{:S(2)}, u32[]{:S(2)}) %collective-permute-start.16) | collective-permute-done | bytes 12320 | tf_op jit(solution)/shard_map/ppermute | solution.py:53
  65.9 2.4 %collective-permute-start.18 = (f32[24,128]{1,0:T(8,128)S(1)}, f32[24,128]{1,0:T(8,128)S(1)}, u32[]{:S(2)}, u32[]{:S(2)}) collective-permute-start(f32[24,128]{1,0:T(8,128)S(1)} %add_select_fusion.1), channel_id=1, source_target_pairs={{0,1},{1,0},{2,3},{3,2},{4,5},{5,4},{6,7},{7,6},{8,9},{9,8},{10,11... | collective-permute-start | bytes 36872 | tf_op jit(solution)/shard_map/ppermute | solution.py:54
  71.1 1.7 %collective-permute-start.24 = (f32[8,128]{1,0:T(8,128)S(1)}, f32[8,128]{1,0:T(8,128)S(1)}, u32[]{:S(2)}, u32[]{:S(2)}) collective-permute-start(f32[8,128]{1,0:T(8,128)S(1)} %broadcast_in_dim.92), channel_id=1, source_target_pairs={{0,64},{64,128},{128,192},{192,0},{1,65},{65,129},{129,193},{193,1... | collective-permute-start | bytes 12296 | tf_op jit(solution)/shard_map/ppermute | solution.py:148
  73.8 2.0 %subtract_convert_fusion = bf16[512,2048]{1,0:T(8,128)(2,1)S(1)} fusion(bf16[512,768]{1,0:T(8,128)(2,1)S(1)} %pad_maximum_fusion, bf16[2048,768]{1,0:T(8,128)(2,1)S(1)} %bitcast.63, f32[2048]{0:T(1024)S(1)} %slice_bitcast_fusion, s32[2048]{0:T(1024)S(1)} %bitcast.77), kind=kOutput, calls=%fused_computation | convolution fusion | flops 1615855616 | bytes 6045696 | tf_op jit(solution)/shard_map/kd,rd->kr/dot_general | solution.py:66
  75.8 1.4 %fusion.5 = f16[384,768]{1,0:T(8,128)(2,1)S(1)} fusion(bf16[2048,768]{1,0:T(8,128)(2,1)S(1)} %bitcast.64, bf16[512,2048]{1,0:T(8,128)(2,1)S(1)} %subtract_convert_fusion), kind=kOutput, calls=%fused_computation.7 | convolution fusion | flops 1208549376 | bytes 5308416 | tf_op jit(solution)/shard_map/dot_general | solution.py:137
  78.5 2.2 %collective-permute-start.22 = (f16[128,768]{1,0:T(8,128)(2,1)S(1)}, f16[128,768]{1,0:T(8,128)(2,1)S(1)}, u32[]{:S(2)}, u32[]{:S(2)}) collective-permute-start(f16[128,768]{1,0:T(8,128)(2,1)S(1)} %get-tuple-element.90), channel_id=1, source_target_pairs={{0,192},{64,0},{128,64},{192,128},{1,193},{65,1},{129,65},{193,129... | collective-permute-start | bytes 589832 | tf_op jit(solution)/shard_map/ppermute | solution.py:141
  80.7 3.0 %collective-permute-start.20 = (f16[64,768]{1,0:T(8,128)(2,1)S(1)}, f16[64,768]{1,0:T(8,128)(2,1)S(1)}, u32[]{:S(2)}, u32[]{:S(2)}) collective-permute-start(f16[64,768]{1,0:T(8,128)(2,1)S(1)} %get-tuple-element.88), channel_id=1, source_target_pairs={{0,128},{64,192},{128,0},{192,64},{1,129},{65,193},{129,1},{193,65... | collective-permute-start | bytes 294920 | tf_op jit(solution)/shard_map/ppermute | solution.py:141
  85.5 1.2 %collective-permute-done.19 = f16[64,768]{1,0:T(8,128)(2,1)S(1)} collective-permute-done((f16[64,768]{1,0:T(8,128)(2,1)S(1)}, f16[64,768]{1,0:T(8,128)(2,1)S(1)}, u32[]{:S(2)}, u32[]{:S(2)}) %collective-permute-start.19) | collective-permute-done | bytes 98336 | tf_op jit(solution)/shard_map/ppermute | solution.py:141
  86.7 2.4 %collective-permute-done.20 = f16[64,768]{1,0:T(8,128)(2,1)S(1)} collective-permute-done((f16[64,768]{1,0:T(8,128)(2,1)S(1)}, f16[64,768]{1,0:T(8,128)(2,1)S(1)}, u32[]{:S(2)}, u32[]{:S(2)}) %collective-permute-start.20) | collective-permute-done | bytes 98336 | tf_op jit(solution)/shard_map/ppermute | solution.py:141
  89.1 1.2 %divide_subtract_fusion = (f32[128,768]{1,0:T(8,128)}, f32[128,768]{1,0:T(8,128)}, f32[128,768]{1,0:T(8,128)}) fusion(f32[128,768]{1,0:T(8,128)S(1)} %copy-done, f32[128,768]{1,0:T(8,128)S(1)} %fusion.8, f16[128,768]{1,0:T(8,128)(2,1)S(1)} %collective-permute-done.22, f16[128,768]{1,0:T(8,128)(2,1)S(1)} %collective-permute-done.21, ...), kind=kLoop, calls=%fused_computation.19 | loop fusion | flops 1867776 | bytes 3342336 | tf_op jit(solution)/shard_map/sub | solution.py:37
  (86 shorter events, 13.2 us)
Async XLA Ops:
  0.6 22.5 %copy-start.3 = (bf16[256,768]{1,0:T(8,128)(2,1)S(1)}, bf16[256,768]{1,0:T(8,128)(2,1)}, u32[]{:S(2)}) copy-start(bf16[256,768]{1,0:T(8,128)(2,1)} %param.5) | copy-start | bytes 1179652
  0.6 18.6 %collective-permute-start = (bf16[256,768]{1,0:T(8,128)(2,1)}, bf16[256,768]{1,0:T(8,128)(2,1)S(1)}, u32[]{:S(2)}, u32[]{:S(2)}) collective-permute-start(bf16[256,768]{1,0:T(8,128)(2,1)} %param.5), channel_id=1, source_target_pairs={{0,8},{1,57},{8,16},{9,1},{16,24},{17,9},{24,32},{25,17},{32,40},{... | collective-permute-start | bytes 1179656 | tf_op jit(solution)/shard_map/ppermute | solution.py:95
  8.1 7.2 %collective-permute-start.10 = (bf16[128,768]{1,0:T(8,128)(2,1)S(1)}, bf16[128,768]{1,0:T(8,128)(2,1)S(1)}, u32[]{:S(2)}, u32[]{:S(2)}) collective-permute-start(bf16[128,768]{1,0:T(8,128)(2,1)S(1)} %convert_element_type.64), channel_id=1, source_target_pairs={{0,64},{64,128},{128,192},{192,0},{1,65},{65,129},{129,193},{193,1... | collective-permute-start | bytes 589832 | tf_op jit(solution)/shard_map/ppermute | solution.py:108
  9.4 8.2 %collective-permute-start.8 = (bf16[128,768]{1,0:T(8,128)(2,1)S(1)}, bf16[128,768]{1,0:T(8,128)(2,1)S(1)}, u32[]{:S(2)}, u32[]{:S(2)}) collective-permute-start(bf16[128,768]{1,0:T(8,128)(2,1)S(1)} %convert_element_type.64), channel_id=1, source_target_pairs={{0,192},{64,0},{128,64},{192,128},{1,193},{65,1},{129,65},{193,129... | collective-permute-start | bytes 589832 | tf_op jit(solution)/shard_map/ppermute | solution.py:108
  10.9 8.3 %collective-permute-start.9 = (bf16[128,768]{1,0:T(8,128)(2,1)S(1)}, bf16[128,768]{1,0:T(8,128)(2,1)S(1)}, u32[]{:S(2)}, u32[]{:S(2)}) collective-permute-start(bf16[128,768]{1,0:T(8,128)(2,1)S(1)} %convert_element_type.64), channel_id=1, source_target_pairs={{0,128},{64,192},{128,0},{192,64},{1,129},{65,193},{129,1},{193,65... | collective-permute-start | bytes 589832 | tf_op jit(solution)/shard_map/ppermute | solution.py:108
  19.2 7.5 %collective-permute-start.2 = (bf16[256,768]{1,0:T(8,128)(2,1)S(1)}, bf16[256,768]{1,0:T(8,128)(2,1)S(1)}, u32[]{:S(2)}, u32[]{:S(2)}) collective-permute-start(bf16[256,768]{1,0:T(8,128)(2,1)S(1)} %collective-permute-done), channel_id=1, source_target_pairs={{0,8},{1,57},{8,16},{9,1},{16,24},{17,9},{24,32},{25,17},{32,40},{... | collective-permute-start | bytes 1179656 | tf_op jit(solution)/shard_map/ppermute | solution.py:95
  22.0 7.9 %collective-permute-start.1 = (bf16[256,768]{1,0:T(8,128)(2,1)S(1)}, bf16[256,768]{1,0:T(8,128)(2,1)S(1)}, u32[]{:S(2)}, u32[]{:S(2)}) collective-permute-start(bf16[256,768]{1,0:T(8,128)(2,1)S(1)} %collective-permute-done), channel_id=1, source_target_pairs={{0,1},{1,0},{2,3},{3,2},{4,5},{5,4},{6,7},{7,6},{8,9},{9,8},{10,11... | collective-permute-start | bytes 1179656 | tf_op jit(solution)/shard_map/ppermute | solution.py:100
  26.7 7.8 %collective-permute-start.4 = (bf16[256,768]{1,0:T(8,128)(2,1)S(1)}, bf16[256,768]{1,0:T(8,128)(2,1)S(1)}, u32[]{:S(2)}, u32[]{:S(2)}) collective-permute-start(bf16[256,768]{1,0:T(8,128)(2,1)S(1)} %collective-permute-done.2), channel_id=1, source_target_pairs={{0,8},{1,57},{8,16},{9,1},{16,24},{17,9},{24,32},{25,17},{32,40},{... | collective-permute-start | bytes 1179656 | tf_op jit(solution)/shard_map/ppermute | solution.py:95
  29.8 7.9 %collective-permute-start.3 = (bf16[256,768]{1,0:T(8,128)(2,1)S(1)}, bf16[256,768]{1,0:T(8,128)(2,1)S(1)}, u32[]{:S(2)}, u32[]{:S(2)}) collective-permute-start(bf16[256,768]{1,0:T(8,128)(2,1)S(1)} %collective-permute-done.2), channel_id=1, source_target_pairs={{0,1},{1,0},{2,3},{3,2},{4,5},{5,4},{6,7},{7,6},{8,9},{9,8},{10,11... | collective-permute-start | bytes 1179656 | tf_op jit(solution)/shard_map/ppermute | solution.py:100
  34.5 6.9 %collective-permute-start.6 = (bf16[128,768]{1,0:T(8,128)(2,1)S(1)}, bf16[128,768]{1,0:T(8,128)(2,1)S(1)}, u32[]{:S(2)}, u32[]{:S(2)}) collective-permute-start(bf16[128,768]{1,0:T(8,128)(2,1)S(1)} %dynamic-slice_bitcast_fusion), channel_id=1, source_target_pairs={{0,8},{1,57},{8,16},{9,1},{16,24},{17,9},{24,32},{25,17},{32,40},{... | collective-permute-start | bytes 589832 | tf_op jit(solution)/shard_map/ppermute | solution.py:103
  41.1 5.3 %collective-permute-start.5 = (bf16[256,768]{1,0:T(8,128)(2,1)S(1)}, bf16[256,768]{1,0:T(8,128)(2,1)S(1)}, u32[]{:S(2)}, u32[]{:S(2)}) collective-permute-start(bf16[256,768]{1,0:T(8,128)(2,1)S(1)} %collective-permute-done.4), channel_id=1, source_target_pairs={{0,1},{1,0},{2,3},{3,2},{4,5},{5,4},{6,7},{7,6},{8,9},{9,8},{10,11... | collective-permute-start | bytes 1179656 | tf_op jit(solution)/shard_map/ppermute | solution.py:100
  41.5 4.4 %collective-permute-start.7 = (bf16[128,768]{1,0:T(8,128)(2,1)S(1)}, bf16[128,768]{1,0:T(8,128)(2,1)S(1)}, u32[]{:S(2)}, u32[]{:S(2)}) collective-permute-start(bf16[128,768]{1,0:T(8,128)(2,1)S(1)} %collective-permute-done.6), channel_id=1, source_target_pairs={{0,1},{1,0},{2,3},{3,2},{4,5},{5,4},{6,7},{7,6},{8,9},{9,8},{10,11... | collective-permute-start | bytes 589832 | tf_op jit(solution)/shard_map/ppermute | solution.py:104
  47.4 1.2 %collective-permute-start.11 = (f32[24,128]{1,0:T(8,128)S(1)}, f32[24,128]{1,0:T(8,128)S(1)}, u32[]{:S(2)}, u32[]{:S(2)}) collective-permute-start(f32[24,128]{1,0:T(8,128)S(1)} %maximum_maximum_fusion), channel_id=1, source_target_pairs={{0,1},{1,0},{2,3},{3,2},{4,5},{5,4},{6,7},{7,6},{8,9},{9,8},{10,11... | collective-permute-start | bytes 36872 | tf_op jit(solution)/shard_map/ppermute | solution.py:48
  48.7 2.6 %collective-permute-start.12 = (f32[24,128]{1,0:T(8,128)S(1)}, f32[24,128]{1,0:T(8,128)S(1)}, u32[]{:S(2)}, u32[]{:S(2)}) collective-permute-start(f32[24,128]{1,0:T(8,128)S(1)} %add_select_fusion.4), channel_id=1, source_target_pairs={{0,8},{1,57},{8,16},{9,1},{16,24},{17,9},{24,32},{25,17},{32,40},{... | collective-permute-start | bytes 36872 | tf_op jit(solution)/shard_map/ppermute | solution.py:49
  51.4 5.9 %collective-permute-start.13 = (f32[24,128]{1,0:T(8,128)S(1)}, f32[24,128]{1,0:T(8,128)S(1)}, u32[]{:S(2)}, u32[]{:S(2)}) collective-permute-start(f32[24,128]{1,0:T(8,128)S(1)} %add_select_fusion.3), channel_id=1, source_target_pairs={{0,16},{1,57},{8,24},{9,1},{16,32},{17,9},{24,40},{25,17},{32,48},... | collective-permute-start | bytes 36872 | tf_op jit(solution)/shard_map/ppermute | solution.py:50
  52.9 6.2 %collective-permute-start.14 = (f32[24,128]{1,0:T(8,128)S(1)}, f32[24,128]{1,0:T(8,128)S(1)}, u32[]{:S(2)}, u32[]{:S(2)}) collective-permute-start(f32[24,128]{1,0:T(8,128)S(1)} %add_select_fusion.3), channel_id=1, source_target_pairs={{1,41},{9,49},{17,57},{25,1},{33,9},{41,17},{49,25},{57,33},{3,43}... | collective-permute-start | bytes 36872 | tf_op jit(solution)/shard_map/ppermute | solution.py:51
  59.1 5.7 %collective-permute-start.15 = (f32[24,128]{1,0:T(8,128)S(1)}, f32[24,128]{1,0:T(8,128)S(1)}, u32[]{:S(2)}, u32[]{:S(2)}) collective-permute-start(f32[24,128]{1,0:T(8,128)S(1)} %add_select_fusion.2), channel_id=1, source_target_pairs={{0,4},{2,6},{4,0},{6,2},{1,5},{3,7},{5,1},{7,3},{8,12},{10,14},{12... | collective-permute-start | bytes 36872 | tf_op jit(solution)/shard_map/ppermute | solution.py:53
  62.1 3.8 %collective-permute-start.16 = (f32[24,128]{1,0:T(8,128)S(1)}, f32[24,128]{1,0:T(8,128)S(1)}, u32[]{:S(2)}, u32[]{:S(2)}) collective-permute-start(f32[24,128]{1,0:T(8,128)S(1)} %add_select_fusion.2), channel_id=1, source_target_pairs={{0,2},{2,4},{4,6},{6,0},{1,3},{3,5},{5,7},{7,1},{8,10},{10,12},{12... | collective-permute-start | bytes 36872 | tf_op jit(solution)/shard_map/ppermute | solution.py:53
  62.5 3.4 %collective-permute-start.17 = (f32[24,128]{1,0:T(8,128)S(1)}, f32[24,128]{1,0:T(8,128)S(1)}, u32[]{:S(2)}, u32[]{:S(2)}) collective-permute-start(f32[24,128]{1,0:T(8,128)S(1)} %add_select_fusion.2), channel_id=1, source_target_pairs={{0,6},{2,0},{4,2},{6,4},{1,7},{3,1},{5,3},{7,5},{8,14},{10,8},{12,... | collective-permute-start | bytes 36872 | tf_op jit(solution)/shard_map/ppermute | solution.py:53
  65.9 3.2 %collective-permute-start.18 = (f32[24,128]{1,0:T(8,128)S(1)}, f32[24,128]{1,0:T(8,128)S(1)}, u32[]{:S(2)}, u32[]{:S(2)}) collective-permute-start(f32[24,128]{1,0:T(8,128)S(1)} %add_select_fusion.1), channel_id=1, source_target_pairs={{0,1},{1,0},{2,3},{3,2},{4,5},{5,4},{6,7},{7,6},{8,9},{9,8},{10,11... | collective-permute-start | bytes 36872 | tf_op jit(solution)/shard_map/ppermute | solution.py:54
  70.5 10.2 %collective-permute-start.23 = (f32[8,128]{1,0:T(8,128)S(1)}, f32[8,128]{1,0:T(8,128)S(1)}, u32[]{:S(2)}, u32[]{:S(2)}) collective-permute-start(f32[8,128]{1,0:T(8,128)S(1)} %broadcast_in_dim.92), channel_id=1, source_target_pairs={{0,128},{64,192},{128,0},{192,64},{1,129},{65,193},{129,1},{193,65... | collective-permute-start | bytes 12296 | tf_op jit(solution)/shard_map/ppermute | solution.py:148
  71.1 9.6 %collective-permute-start.24 = (f32[8,128]{1,0:T(8,128)S(1)}, f32[8,128]{1,0:T(8,128)S(1)}, u32[]{:S(2)}, u32[]{:S(2)}) collective-permute-start(f32[8,128]{1,0:T(8,128)S(1)} %broadcast_in_dim.92), channel_id=1, source_target_pairs={{0,64},{64,128},{128,192},{192,0},{1,65},{65,129},{129,193},{193,1... | collective-permute-start | bytes 12296 | tf_op jit(solution)/shard_map/ppermute | solution.py:148
  72.8 10.8 %collective-permute-start.25 = (f32[8,128]{1,0:T(8,128)S(1)}, f32[8,128]{1,0:T(8,128)S(1)}, u32[]{:S(2)}, u32[]{:S(2)}) collective-permute-start(f32[8,128]{1,0:T(8,128)S(1)} %broadcast_in_dim.92), channel_id=1, source_target_pairs={{0,192},{64,0},{128,64},{192,128},{1,193},{65,1},{129,65},{193,129... | collective-permute-start | bytes 12296 | tf_op jit(solution)/shard_map/ppermute | solution.py:148
  77.2 11.9 %copy-start = (f32[128,768]{1,0:T(8,128)S(1)}, f32[128,768]{1,0:T(8,128)}, u32[]{:S(2)}) copy-start(f32[128,768]{1,0:T(8,128)} %param.7) | copy-start | bytes 1179652
  77.2 11.9 %copy-start.1 = (f32[128,768]{1,0:T(8,128)S(1)}, f32[128,768]{1,0:T(8,128)}, u32[]{:S(2)}) copy-start(f32[128,768]{1,0:T(8,128)} %param.8) | copy-start | bytes 1179652
  77.2 11.9 %copy-start.2 = (f32[128,768]{1,0:T(8,128)S(1)}, f32[128,768]{1,0:T(8,128)}, u32[]{:S(2)}) copy-start(f32[128,768]{1,0:T(8,128)} %param.9) | copy-start | bytes 1179652
  77.9 11.2 %collective-permute-start.21 = (f16[128,768]{1,0:T(8,128)(2,1)S(1)}, f16[128,768]{1,0:T(8,128)(2,1)S(1)}, u32[]{:S(2)}, u32[]{:S(2)}) collective-permute-start(f16[128,768]{1,0:T(8,128)(2,1)S(1)} %get-tuple-element.89), channel_id=1, source_target_pairs={{0,64},{64,128},{128,192},{192,0},{1,65},{65,129},{129,193},{193,1... | collective-permute-start | bytes 589832 | tf_op jit(solution)/shard_map/ppermute | solution.py:141
  78.5 10.6 %collective-permute-start.22 = (f16[128,768]{1,0:T(8,128)(2,1)S(1)}, f16[128,768]{1,0:T(8,128)(2,1)S(1)}, u32[]{:S(2)}, u32[]{:S(2)}) collective-permute-start(f16[128,768]{1,0:T(8,128)(2,1)S(1)} %get-tuple-element.90), channel_id=1, source_target_pairs={{0,192},{64,0},{128,64},{192,128},{1,193},{65,1},{129,65},{193,129... | collective-permute-start | bytes 589832 | tf_op jit(solution)/shard_map/ppermute | solution.py:141
  80.7 6.0 %collective-permute-start.19 = (f16[64,768]{1,0:T(8,128)(2,1)S(1)}, f16[64,768]{1,0:T(8,128)(2,1)S(1)}, u32[]{:S(2)}, u32[]{:S(2)}) collective-permute-start(f16[64,768]{1,0:T(8,128)(2,1)S(1)} %get-tuple-element.87), channel_id=1, source_target_pairs={{0,128},{64,192},{128,0},{192,64},{1,129},{65,193},{129,1},{193,65... | collective-permute-start | bytes 294920 | tf_op jit(solution)/shard_map/ppermute | solution.py:141
  80.7 8.4 %collective-permute-start.20 = (f16[64,768]{1,0:T(8,128)(2,1)S(1)}, f16[64,768]{1,0:T(8,128)(2,1)S(1)}, u32[]{:S(2)}, u32[]{:S(2)}) collective-permute-start(f16[64,768]{1,0:T(8,128)(2,1)S(1)} %get-tuple-element.88), channel_id=1, source_target_pairs={{0,128},{64,192},{128,0},{192,64},{1,129},{65,193},{129,1},{193,65... | collective-permute-start | bytes 294920 | tf_op jit(solution)/shard_map/ppermute | solution.py:141
where the time goes:
time: 92.3 us; the launch traced here: 91.5 us
  starting transfers between devices  47 us (51%)
  waiting for transfers between devices  25.8 us (28%)
  matrix products  7.33 us (8%)
  other arithmetic  5.76 us (6%)
  between operations  2.79 us (3%)
  local copies, waits for them, and re-layouts  2.73 us (3%)
    ppermute x3, starting transfers between devices, body(): part = lax.ppermute(part, ('z', 'c'), OPPOSITE)  12.3 us
    ppermute x3, waiting for transfers between devices, body(): part = lax.ppermute(part, ('z', 'c'), OPPOSITE)  8.05 us
    ppermute x3, waiting for transfers between devices, body(): lax.ppermute(half, 'x', turn(4, -hop))  6.64 us
    ppermute x4, starting transfers between devices, body(): lax.ppermute(sent[some], 'x', turn(4, step)).astype(jnp.float32)  5.72 us
    ppermute x3, starting transfers between devices, over_lists(): lax.ppermute(state, 'y', turn(4, step))  5.64 us
    dot_general x6, matrix products, logits_of(): jnp.einsum('kd,rd->kr', lists, rows, preferred_element_type=jnp.float32)  5.36 us
    ppermute x1, starting transfers between devices, over_lists(): lax.ppermute(pair, ('z', 'c'), [(z * 2 + 1, (z - 3) % 8 * 2 + 1) for z in...  4.39 us
    ppermute x3, starting transfers between devices, body(): lax.ppermute(half, 'x', turn(4, -hop))  4.29 us
  transfers between devices with their start and end apart: 26, of which 13 were waited for; matrix products, arithmetic and copies ran while one was open for 13% of the time, Pallas kernels for 0%

commit v1 on v0

--- a/solution.py
+++ b/solution.py
@@ -47,8 +47,8 @@
 def over_lists(state, at_first):
     state = join(state, lax.ppermute(state, "c", SWAP))
     pair = join(state, lax.ppermute(state, ("z", "c"), OPPOSITE))
-    some = lax.ppermute(pair, ("z", "c"), [(z * 2 + c, (z + (2, -1)[c]) % 8 * 2 + c) for z in range(8) for c in range(2)])
-    rest = lax.ppermute(pair, ("z", "c"), [(z * 2 + 1, (z - 3) % 8 * 2 + 1) for z in range(8)])
+    some = lax.ppermute(pair, ("z", "c"), [(z * 2 + c, (z + (2, -3)[c]) % 8 * 2 + c) for z in range(8) for c in range(2)])
+    rest = lax.ppermute(pair, ("z", "c"), [(z * 2 + 1, (z - 1) % 8 * 2 + 1) for z in range(8)])
     state = join(some, jnp.where(at_first, pair, rest))
     state = join(state, *[lax.ppermute(state, "y", turn(4, step)) for step in (2, 1, -1)])
     return join(state, lax.ppermute(state, "c", SWAP))
@@ -84,49 +84,53 @@
     sign = 1 - 2 * core
     width = query_emb.shape[1]
 
-    steps = [0, -1, 1, -2, 2, -3, 3, 4]
-    firsts = [((z + sign * step) & 7) * 2 for step in steps]
-    firsts = firsts[:7] + [firsts[7] + core, firsts[7] + 1 - core]
-    firsts = [first.astype(jnp.uint32) for first in firsts]
+    def slot(step, half):
+        return ((((z + sign * step) & 7) * 2) + half).astype(jnp.uint32)
+
+    own_at, one = slot(0, 0), [slot(-1, 0), slot(1, 0)]
+    two, three = [[slot(step, half) for step, half in ((-k, core), (-k, 1 - core), (k, 1 - core), (k, core))] for k in (2, 3)]
+    four = [slot(4, core), slot(4, 1 - core)]
     own_base, x_at, cut, at_first = (z * 8 + y * 2 + core) * OWN, x.astype(jnp.uint32), core.astype(jnp.uint32), core == 0
 
-    part, blocks = query_emb, [query_emb]
-    for k in range(3):
-        part = lax.ppermute(part, ("z", "c"), OPPOSITE)
-        if k == 0:
-            part, positive_list, own_base, x, x_at, cut, at_first, *firsts = lax.optimization_barrier(
-                (part, positive_list, own_base, x, x_at, cut, at_first, *firsts)
-            )
-        swapped = lax.ppermute(part, "c", SWAP)
-        blocks += [part, swapped]
-    part = lax.dynamic_slice(part.reshape(2, HALF, width), (cut, ZERO, ZERO), (1, HALF, width))[0]
-    last = lax.ppermute(part, ("z", "c"), OPPOSITE)
+    targets = lax.dynamic_slice(positive_list.reshape(4, 2048), (x_at, ZERO), (1, 2048))[0] - own_base
+    place = (((targets >> 13) - x + 3) & 3) * OWN + (targets & (OWN - 1))
+    targets = jnp.where((targets & 8191) < OWN, place, -1)
+    late = [lax.dynamic_slice(targets.reshape(16, HALF), (row, ZERO), (1, HALF))[0] for row in four]
+
+    part = lax.ppermute(query_emb, ("z", "c"), OPPOSITE)
+    part, own_at, one, two, three, four, cut, at_first, targets, late = lax.optimization_barrier(
+        (part, own_at, one, two, three, four, cut, at_first, targets, late)
+    )
+    swapped = lax.ppermute(part, "c", SWAP)
+    rows = jnp.zeros((16, HALF, width), query_emb.dtype)
+    for block, row in zip((query_emb, part, swapped), [own_at] + one):
+        rows = put(rows, block, row)
+    part = part.reshape(2, HALF, width)
+    parts = [lax.dynamic_slice(part, (at, ZERO, ZERO), (1, HALF, width))[0] for at in (cut, 1 - cut)]
+    arrived = []
+    for _ in range(2):
+        for i in range(2):
+            parts[i] = lax.ppermute(parts[i], ("z", "c"), OPPOSITE)
+        swapped = []
+        for i in range(2):
+            swapped.append(lax.ppermute(parts[i], "c", SWAP))
+        arrived.append(parts + swapped)
+    last = lax.ppermute(parts[0], ("z", "c"), OPPOSITE)
     swapped = lax.ppermute(last, "c", SWAP)
-    blocks = list(zip(blocks + [last, swapped], firsts))
+    for block, row in zip(arrived[0] + arrived[1], two + three):
+        rows = put(rows, block, row)
 
     half = centroids.astype(jnp.bfloat16)
     lists = jnp.concatenate([lax.ppermute(half, "x", turn(4, -hop)) if hop else half for hop in HOPS])
     lists = lax.optimization_barrier(lists)
 
-    targets = lax.dynamic_slice(positive_list.reshape(4, 2048), (x_at, ZERO), (1, 2048))[0] - own_base
-    place = (((targets >> 13) - x + 3) & 3) * OWN + (targets & (OWN - 1))
-    targets = jnp.where((targets & 8191) < OWN, place, -1)
-    late = [lax.dynamic_slice(targets.reshape(16, HALF), (row, ZERO), (block.shape[0] // HALF, HALF)) for block, row in blocks[5:]]
-    targets, *late = lax.optimization_barrier((targets, *[some.reshape(-1) for some in late]))
-    rows = jnp.zeros((16, HALF, width), query_emb.dtype)
-    for block, row in blocks[:5]:
-        rows = put(rows, block, row)
     state, hit = forward(rows.reshape(-1, width), lists, targets)
     at = lax.broadcasted_iota(jnp.uint32, (16, HALF), 0)
-    for i, (block, row) in enumerate(blocks[5:]):
+    for i, (block, row) in enumerate(zip((last, swapped), four)):
         local, more = forward(block, lists, late[i])
-        state, hit = jnp.where(at == row, local[:1], state), hit + more
-        if i < 2:
-            state = jnp.where(at - 1 == row, local[1:], state)
-            rows = put(rows, block, row)
+        state, hit = jnp.where(at == row, local, state), hit + more
+        rows = put(rows, block, row)
     state = jnp.concatenate([state, hit, jnp.zeros((7, HALF), jnp.float32)])
-    for block, row in blocks[7:]:
-        rows = put(rows, block, row)
     rows = rows.reshape(-1, width)
     state = over_lists(state, at_first)
 
@@ -142,18 +146,19 @@
     own = jnp.dot(weights[3 * OWN :], rows, preferred_element_type=jnp.float32)
     own = lax.optimization_barrier(own)
     at = lax.broadcasted_iota(jnp.int32, state.shape, 0)
-    loss = jnp.full((8, 128), jnp.sum(jnp.where(at < 16, state, -state)))
+    loss = jnp.sum(jnp.where(at < 16, state, -state)).reshape(1, 1)
     others = []
     for step in (2, 1, -1):
         others.append(lax.ppermute(loss, "x", turn(4, step)))
     gradient = own + (jnp.concatenate(back[:2]) + back[2] + back[3]) * (1.0 / SCALE)
-    return (gradient, loss + others[0] + others[1] + others[2])
+    return (gradient, [loss] + others)
 
 
 def shards(query_emb, positive_list, centroids, first_moment, second_moment):
     gradient, loss = body(query_emb, positive_list, centroids)
     new_centroids, new_first, new_second = adam_update(centroids, first_moment, second_moment, gradient)
-    return (new_centroids, new_first, new_second, loss[0, 0] / ROWS)
+    new_first, *loss = lax.optimization_barrier((new_first, *loss))
+    return (new_centroids, new_first, new_second, sum(loss).reshape(()) / ROWS)
 
 
 def solution(mesh):

time: 92.3 us -> 87 us (0.943)
  waiting for transfers between devices: 25.8 us -> 15 us
  starting transfers between devices: 47 us -> 53.2 us
  between operations: 2.79 us -> 4.6 us
  local copies, waits for them, and re-layouts: 2.73 us -> 1.59 us
  other arithmetic: 5.76 us -> 4.79 us
    ppermute x6 -> x12, waiting for transfers between devices: 9.83 us -> 3.12 us  [the longest x4 1.45 us: body(): parts[i] = lax.ppermute(parts[i], ('z', 'c'), OPPOSITE)]
    ppermute x6 -> x12, starting transfers between devices: 21.4 us -> 26.7 us  [the longest x4 8.94 us: body(): parts[i] = lax.ppermute(parts[i], ('z', 'c'), OPPOSITE)]
    ppermute x1, starting transfers between devices: 3.35 us -> 0.46 us  [body(): swapped = lax.ppermute(last, 'c', SWAP)]
    ppermute x4, waiting for transfers between devices: 3.63 us -> 1.5 us  [body(): lax.ppermute(sent[some], 'x', turn(4, step)).astype(jnp.float32)]
    ppermute x3, starting transfers between devices: 3.35 us -> 5.13 us  [body(): others.append(lax.ppermute(loss, 'x', turn(4, step)))]
    ppermute x3, waiting for transfers between devices: 6.64 us -> 4.95 us  [body(): lax.ppermute(half, 'x', turn(4, -hop))]
    ppermute x1, starting transfers between devices: 2.36 us -> 3.34 us  [over_lists(): return join(state, lax.ppermute(state, 'c', SWAP))]
    ppermute x3 -> x1, starting transfers between devices: 0.32 us -> 1.27 us  [body(): swapped = lax.ppermute(part, 'c', SWAP)]
  transfers between devices with their start and end apart: 26 -> 30, of which waited for: 13 -> 12; matrix products, arithmetic and copies ran while one was open for 13% -> 9% of each run, Pallas kernels for 0% -> 0%
where the time goes in v1:
time: 87 us; the launch traced here: 85.7 us
  starting transfers between devices  53.2 us (61%)
  waiting for transfers between devices  15 us (17%)
  matrix products  6.5 us (7%)
  other arithmetic  4.79 us (6%)
  between operations  4.6 us (5%)
  local copies, waits for them, and re-layouts  1.59 us (2%)
    ppermute x4, starting transfers between devices, body(): parts[i] = lax.ppermute(parts[i], ('z', 'c'), OPPOSITE)  8.94 us
    ppermute x1, starting transfers between devices, body(): part = lax.ppermute(query_emb, ('z', 'c'), OPPOSITE)  6.47 us
    ppermute x4, starting transfers between devices, body(): lax.ppermute(sent[some], 'x', turn(4, step)).astype(jnp.float32)  5.94 us
    ppermute x3, starting transfers between devices, over_lists(): lax.ppermute(state, 'y', turn(4, step))  5.63 us
    ppermute x3, starting transfers between devices, body(): others.append(lax.ppermute(loss, 'x', turn(4, step)))  5.13 us
    ppermute x3, waiting for transfers between devices, body(): lax.ppermute(half, 'x', turn(4, -hop))  4.95 us
    dot_general x4, matrix products, logits_of(): jnp.einsum('kd,rd->kr', lists, rows, preferred_element_type=jnp.float32)  4.54 us
    ppermute x4, starting transfers between devices, body(): swapped.append(lax.ppermute(parts[i], 'c', SWAP))  3.75 us
  transfers between devices with their start and end apart: 30, of which 12 were waited for; matrix products, arithmetic and copies ran while one was open for 9% of the time, Pallas kernels for 0%

profile of v1, /device:TPU:1, one launch (start us, length us, event | category | flops | bytes accessed | tf_op | source)
XLA Modules:
  0.0 85.7 jit_solution(14395613266762897473)
XLA Ops:
  0.6 6.5 %collective-permute-start = (bf16[256,768]{1,0:T(8,128)(2,1)}, bf16[256,768]{1,0:T(8,128)(2,1)S(1)}, u32[]{:S(2)}, u32[]{:S(2)}) collective-permute-start(bf16[256,768]{1,0:T(8,128)(2,1)} %param.5), channel_id=1, source_target_pairs={{0,8},{1,57},{8,16},{9,1},{16,24},{17,9},{24,32},{25,17},{32,40},{... | collective-permute-start | bytes 1179656 | tf_op jit(solution)/shard_map/ppermute | solution.py:100
  7.1 1.0 %convert_element_type.80 = bf16[128,768]{1,0:T(8,128)(2,1)S(1)} convert(f32[128,768]{1,0:T(8,128)} %param.7) | non-fusion elementwise | flops 98304 | bytes 589824 | tf_op jit(solution)/shard_map/convert_element_type | solution.py:123
  8.1 2.6 %collective-permute-start.12 = (bf16[128,768]{1,0:T(8,128)(2,1)S(1)}, bf16[128,768]{1,0:T(8,128)(2,1)S(1)}, u32[]{:S(2)}, u32[]{:S(2)}) collective-permute-start(bf16[128,768]{1,0:T(8,128)(2,1)S(1)} %convert_element_type.80), channel_id=1, source_target_pairs={{0,192},{64,0},{128,64},{192,128},{1,193},{65,1},{129,65},{193,129... | collective-permute-start | bytes 589832 | tf_op jit(solution)/shard_map/ppermute | solution.py:124
  12.8 1.3 %collective-permute-start.1 = (bf16[256,768]{1,0:T(8,128)(2,1)S(1)}, bf16[256,768]{1,0:T(8,128)(2,1)S(1)}, u32[]{:S(2)}, u32[]{:S(2)}) collective-permute-start(bf16[256,768]{1,0:T(8,128)(2,1)S(1)} %collective-permute-done), channel_id=1, source_target_pairs={{0,1},{1,0},{2,3},{3,2},{4,5},{5,4},{6,7},{7,6},{8,9},{9,8},{10,11... | collective-permute-start | bytes 1179656 | tf_op jit(solution)/shard_map/ppermute | solution.py:104
  14.1 1.8 %collective-permute-start.2 = (bf16[128,768]{1,0:T(8,128)(2,1)S(1)}, bf16[128,768]{1,0:T(8,128)(2,1)S(1)}, u32[]{:S(2)}, u32[]{:S(2)}) collective-permute-start(bf16[128,768]{1,0:T(8,128)(2,1)S(1)} %get-tuple-element.86), channel_id=1, source_target_pairs={{0,8},{1,57},{8,16},{9,1},{16,24},{17,9},{24,32},{25,17},{32,40},{... | collective-permute-start | bytes 589832 | tf_op jit(solution)/shard_map/ppermute | solution.py:113
  15.9 1.2 %collective-permute-done.12 = bf16[128,768]{1,0:T(8,128)(2,1)S(1)} collective-permute-done((bf16[128,768]{1,0:T(8,128)(2,1)S(1)}, bf16[128,768]{1,0:T(8,128)(2,1)S(1)}, u32[]{:S(2)}, u32[]{:S(2)}) %collective-permute-start.12) | collective-permute-done | bytes 196640 | tf_op jit(solution)/shard_map/ppermute | solution.py:124
  17.1 1.6 %collective-permute-done.13 = bf16[128,768]{1,0:T(8,128)(2,1)S(1)} collective-permute-done((bf16[128,768]{1,0:T(8,128)(2,1)S(1)}, bf16[128,768]{1,0:T(8,128)(2,1)S(1)}, u32[]{:S(2)}, u32[]{:S(2)}) %collective-permute-start.13) | collective-permute-done | bytes 196640 | tf_op jit(solution)/shard_map/ppermute | solution.py:124
  18.7 2.1 %collective-permute-done.14 = bf16[128,768]{1,0:T(8,128)(2,1)S(1)} collective-permute-done((bf16[128,768]{1,0:T(8,128)(2,1)S(1)}, bf16[128,768]{1,0:T(8,128)(2,1)S(1)}, u32[]{:S(2)}, u32[]{:S(2)}) %collective-permute-start.14) | collective-permute-done | bytes 196640 | tf_op jit(solution)/shard_map/ppermute | solution.py:124
  20.9 3.2 %collective-permute-start.3 = (bf16[128,768]{1,0:T(8,128)(2,1)S(1)}, bf16[128,768]{1,0:T(8,128)(2,1)S(1)}, u32[]{:S(2)}, u32[]{:S(2)}) collective-permute-start(bf16[128,768]{1,0:T(8,128)(2,1)S(1)} %get-tuple-element.85), channel_id=1, source_target_pairs={{0,8},{1,57},{8,16},{9,1},{16,24},{17,9},{24,32},{25,17},{32,40},{... | collective-permute-start | bytes 589832 | tf_op jit(solution)/shard_map/ppermute | solution.py:113
  25.3 1.4 %collective-permute-done.3 = bf16[128,768]{1,0:T(8,128)(2,1)S(1)} collective-permute-done((bf16[128,768]{1,0:T(8,128)(2,1)S(1)}, bf16[128,768]{1,0:T(8,128)(2,1)S(1)}, u32[]{:S(2)}, u32[]{:S(2)}) %collective-permute-start.3) | collective-permute-done | bytes 196640 | tf_op jit(solution)/shard_map/ppermute | solution.py:113
  26.7 3.1 %collective-permute-start.7 = (bf16[128,768]{1,0:T(8,128)(2,1)S(1)}, bf16[128,768]{1,0:T(8,128)(2,1)S(1)}, u32[]{:S(2)}, u32[]{:S(2)}) collective-permute-start(bf16[128,768]{1,0:T(8,128)(2,1)S(1)} %collective-permute-done.3), channel_id=1, source_target_pairs={{0,8},{1,57},{8,16},{9,1},{16,24},{17,9},{24,32},{25,17},{32,40},{... | collective-permute-start | bytes 589832 | tf_op jit(solution)/shard_map/ppermute | solution.py:113
  30.6 1.7 %collective-permute-start.10 = (bf16[128,768]{1,0:T(8,128)(2,1)S(1)}, bf16[128,768]{1,0:T(8,128)(2,1)S(1)}, u32[]{:S(2)}, u32[]{:S(2)}) collective-permute-start(bf16[128,768]{1,0:T(8,128)(2,1)S(1)} %collective-permute-done.6), channel_id=1, source_target_pairs={{0,8},{1,57},{8,16},{9,1},{16,24},{17,9},{24,32},{25,17},{32,40},{... | collective-permute-start | bytes 589832 | tf_op jit(solution)/shard_map/ppermute | solution.py:118
  32.4 3.0 %collective-permute-start.9 = (bf16[128,768]{1,0:T(8,128)(2,1)S(1)}, bf16[128,768]{1,0:T(8,128)(2,1)S(1)}, u32[]{:S(2)}, u32[]{:S(2)}) collective-permute-start(bf16[128,768]{1,0:T(8,128)(2,1)S(1)} %collective-permute-done.7), channel_id=1, source_target_pairs={{0,1},{1,0},{2,3},{3,2},{4,5},{5,4},{6,7},{7,6},{8,9},{9,8},{10,11... | collective-permute-start | bytes 589832 | tf_op jit(solution)/shard_map/ppermute | solution.py:116
  35.6 0.9 collective-permute-done.9
  36.5 1.8 %fusion.23 = (f32[2048]{0:T(1024)S(1)}, f32[512,2048]{1,0:T(8,128)S(1)}) fusion(bf16[512,768]{1,0:T(8,128)(2,1)S(1)} %pad_maximum_fusion, bf16[2048,768]{1,0:T(8,128)(2,1)S(1)} %bitcast.57), kind=kOutput, calls=%fused_computation.71 | convolution fusion | flops 1611659264 | bytes 8134656 | tf_op jit(solution)/shard_map/kd,rd->kr/dot_general | solution.py:66
  38.3 1.1 %exponential_reduce_fusion = (f32[2048]{0:T(1024)S(1)}, f32[2048]{0:T(1024)S(1)}) fusion(f32[512,2048]{1,0:T(8,128)S(1)} %get-tuple-element.57, f32[2048]{0:T(1024)S(1)} %get-tuple-element.56, s32[2048]{0:T(1024)S(1)} %bitcast.66), kind=kLoop, calls=%fused_computation.3 | loop fusion | flops 5238784 | bytes 4227072 | tf_op jit(solution)/shard_map/reduce_sum | solution.py:73
  42.1 0.8 collective-permute-done.15
  43.6 2.0 %collective-permute-done.16 = f32[24,128]{1,0:T(8,128)S(1)} collective-permute-done((f32[24,128]{1,0:T(8,128)S(1)}, f32[24,128]{1,0:T(8,128)S(1)}, u32[]{:S(2)}, u32[]{:S(2)}) %collective-permute-start.16) | collective-permute-done | bytes 12320 | tf_op jit(solution)/shard_map/ppermute | solution.py:49
  45.7 2.2 %collective-permute-start.17 = (f32[24,128]{1,0:T(8,128)S(1)}, f32[24,128]{1,0:T(8,128)S(1)}, u32[]{:S(2)}, u32[]{:S(2)}) collective-permute-start(f32[24,128]{1,0:T(8,128)S(1)} %add_select_fusion.3), channel_id=1, source_target_pairs={{0,16},{1,41},{8,24},{9,49},{16,32},{17,57},{24,40},{25,1},{32,48}... | collective-permute-start | bytes 36872 | tf_op jit(solution)/shard_map/ppermute | solution.py:50
  47.9 3.6 %collective-permute-start.18 = (f32[24,128]{1,0:T(8,128)S(1)}, f32[24,128]{1,0:T(8,128)S(1)}, u32[]{:S(2)}, u32[]{:S(2)}) collective-permute-start(f32[24,128]{1,0:T(8,128)S(1)} %add_select_fusion.3), channel_id=1, source_target_pairs={{1,57},{9,1},{17,9},{25,17},{33,25},{41,33},{49,41},{57,49},{3,59}... | collective-permute-start | bytes 36872 | tf_op jit(solution)/shard_map/ppermute | solution.py:51
  52.4 3.0 %collective-permute-start.19 = (f32[24,128]{1,0:T(8,128)S(1)}, f32[24,128]{1,0:T(8,128)S(1)}, u32[]{:S(2)}, u32[]{:S(2)}) collective-permute-start(f32[24,128]{1,0:T(8,128)S(1)} %add_select_fusion.2), channel_id=1, source_target_pairs={{0,4},{2,6},{4,0},{6,2},{1,5},{3,7},{5,1},{7,3},{8,12},{10,14},{12... | collective-permute-start | bytes 36872 | tf_op jit(solution)/shard_map/ppermute | solution.py:53
  55.8 2.3 %collective-permute-start.21 = (f32[24,128]{1,0:T(8,128)S(1)}, f32[24,128]{1,0:T(8,128)S(1)}, u32[]{:S(2)}, u32[]{:S(2)}) collective-permute-start(f32[24,128]{1,0:T(8,128)S(1)} %add_select_fusion.2), channel_id=1, source_target_pairs={{0,6},{2,0},{4,2},{6,4},{1,7},{3,1},{5,3},{7,5},{8,14},{10,8},{12,... | collective-permute-start | bytes 36872 | tf_op jit(solution)/shard_map/ppermute | solution.py:53
  58.1 1.1 %collective-permute-done.20 = f32[24,128]{1,0:T(8,128)S(1)} collective-permute-done((f32[24,128]{1,0:T(8,128)S(1)}, f32[24,128]{1,0:T(8,128)S(1)}, u32[]{:S(2)}, u32[]{:S(2)}) %collective-permute-start.20) | collective-permute-done | bytes 12320 | tf_op jit(solution)/shard_map/ppermute | solution.py:53
  59.3 3.3 %collective-permute-start.22 = (f32[24,128]{1,0:T(8,128)S(1)}, f32[24,128]{1,0:T(8,128)S(1)}, u32[]{:S(2)}, u32[]{:S(2)}) collective-permute-start(f32[24,128]{1,0:T(8,128)S(1)} %add_select_fusion.1), channel_id=1, source_target_pairs={{0,1},{1,0},{2,3},{3,2},{4,5},{5,4},{6,7},{7,6},{8,9},{9,8},{10,11... | collective-permute-start | bytes 36872 | tf_op jit(solution)/shard_map/ppermute | solution.py:54
  64.1 2.0 %subtract_convert_fusion = bf16[512,2048]{1,0:T(8,128)(2,1)S(1)} fusion(bf16[512,768]{1,0:T(8,128)(2,1)S(1)} %pad_maximum_fusion, bf16[2048,768]{1,0:T(8,128)(2,1)S(1)} %bitcast.58, f32[2048]{0:T(1024)S(1)} %slice_bitcast_fusion, s32[2048]{0:T(1024)S(1)} %bitcast.67), kind=kOutput, calls=%fused_computation | convolution fusion | flops 1615855616 | bytes 6045696 | tf_op jit(solution)/shard_map/kd,rd->kr/dot_general | solution.py:66
  66.1 1.4 %fusion.5 = f16[384,768]{1,0:T(8,128)(2,1)S(1)} fusion(bf16[2048,768]{1,0:T(8,128)(2,1)S(1)} %bitcast.59, bf16[512,2048]{1,0:T(8,128)(2,1)S(1)} %subtract_convert_fusion), kind=kOutput, calls=%fused_computation.7 | convolution fusion | flops 1208549376 | bytes 5308416 | tf_op jit(solution)/shard_map/dot_general | solution.py:141
  67.9 2.7 %collective-permute-start.26 = (f16[128,768]{1,0:T(8,128)(2,1)S(1)}, f16[128,768]{1,0:T(8,128)(2,1)S(1)}, u32[]{:S(2)}, u32[]{:S(2)}) collective-permute-start(f16[128,768]{1,0:T(8,128)(2,1)S(1)} %get-tuple-element.84), channel_id=1, source_target_pairs={{0,192},{64,0},{128,64},{192,128},{1,193},{65,1},{129,65},{193,129... | collective-permute-start | bytes 589832 | tf_op jit(solution)/shard_map/ppermute | solution.py:145
  70.6 3.0 %collective-permute-start.24 = (f16[64,768]{1,0:T(8,128)(2,1)S(1)}, f16[64,768]{1,0:T(8,128)(2,1)S(1)}, u32[]{:S(2)}, u32[]{:S(2)}) collective-permute-start(f16[64,768]{1,0:T(8,128)(2,1)S(1)} %get-tuple-element.82), channel_id=1, source_target_pairs={{0,128},{64,192},{128,0},{192,64},{1,129},{65,193},{129,1},{193,65... | collective-permute-start | bytes 294920 | tf_op jit(solution)/shard_map/ppermute | solution.py:145
  74.2 1.5 %collective-permute-done.23 = f16[64,768]{1,0:T(8,128)(2,1)S(1)} collective-permute-done((f16[64,768]{1,0:T(8,128)(2,1)S(1)}, f16[64,768]{1,0:T(8,128)(2,1)S(1)}, u32[]{:S(2)}, u32[]{:S(2)}) %collective-permute-start.23) | collective-permute-done | bytes 98336 | tf_op jit(solution)/shard_map/ppermute | solution.py:145
  75.7 2.2 %collective-permute-start.28 = (f32[1,1]{1,0:T(1,128)}, f32[1,1]{1,0:T(1,128)}, u32[]{:S(2)}, u32[]{:S(2)}) collective-permute-start(f32[1,1]{1,0:T(1,128)} %bitcast.25), channel_id=1, source_target_pairs={{0,64},{64,128},{128,192},{192,0},{1,65},{65,129},{129,193},{193,1... | collective-permute-start | bytes 20 | tf_op jit(solution)/shard_map/ppermute | solution.py:152
  77.9 2.8 %collective-permute-start.29 = (f32[1,1]{1,0:T(1,128)}, f32[1,1]{1,0:T(1,128)}, u32[]{:S(2)}, u32[]{:S(2)}) collective-permute-start(f32[1,1]{1,0:T(1,128)} %bitcast.25), channel_id=1, source_target_pairs={{0,192},{64,0},{128,64},{192,128},{1,193},{65,1},{129,65},{193,129... | collective-permute-start | bytes 20 | tf_op jit(solution)/shard_map/ppermute | solution.py:152
  80.8 1.3 %divide_subtract_fusion = (f32[128,768]{1,0:T(8,128)}, f32[128,768]{1,0:T(8,128)}, f32[128,768]{1,0:T(8,128)}) fusion(f32[128,768]{1,0:T(8,128)S(1)} %copy-done, f32[128,768]{1,0:T(8,128)S(1)} %fusion.8, f16[128,768]{1,0:T(8,128)(2,1)S(1)} %collective-permute-done.26, f16[128,768]{1,0:T(8,128)(2,1)S(1)} %collective-permute-done.25, ...), kind=kLoop, calls=%fused_computation.13 | loop fusion | flops 1867776 | bytes 3342336 | tf_op jit(solution)/shard_map/sub | solution.py:37
  (83 shorter events, 11.7 us)
Async XLA Ops:
  0.6 23.8 %copy-start.3 = (bf16[256,768]{1,0:T(8,128)(2,1)S(1)}, bf16[256,768]{1,0:T(8,128)(2,1)}, u32[]{:S(2)}) copy-start(bf16[256,768]{1,0:T(8,128)(2,1)} %param.5) | copy-start | bytes 1179652
  0.6 12.1 %collective-permute-start = (bf16[256,768]{1,0:T(8,128)(2,1)}, bf16[256,768]{1,0:T(8,128)(2,1)S(1)}, u32[]{:S(2)}, u32[]{:S(2)}) collective-permute-start(bf16[256,768]{1,0:T(8,128)(2,1)} %param.5), channel_id=1, source_target_pairs={{0,8},{1,57},{8,16},{9,1},{16,24},{17,9},{24,32},{25,17},{32,40},{... | collective-permute-start | bytes 1179656 | tf_op jit(solution)/shard_map/ppermute | solution.py:100
  8.1 9.0 %collective-permute-start.12 = (bf16[128,768]{1,0:T(8,128)(2,1)S(1)}, bf16[128,768]{1,0:T(8,128)(2,1)S(1)}, u32[]{:S(2)}, u32[]{:S(2)}) collective-permute-start(bf16[128,768]{1,0:T(8,128)(2,1)S(1)} %convert_element_type.80), channel_id=1, source_target_pairs={{0,192},{64,0},{128,64},{192,128},{1,193},{65,1},{129,65},{193,129... | collective-permute-start | bytes 589832 | tf_op jit(solution)/shard_map/ppermute | solution.py:124
  10.7 8.0 %collective-permute-start.13 = (bf16[128,768]{1,0:T(8,128)(2,1)S(1)}, bf16[128,768]{1,0:T(8,128)(2,1)S(1)}, u32[]{:S(2)}, u32[]{:S(2)}) collective-permute-start(bf16[128,768]{1,0:T(8,128)(2,1)S(1)} %convert_element_type.80), channel_id=1, source_target_pairs={{0,128},{64,192},{128,0},{192,64},{1,129},{65,193},{129,1},{193,65... | collective-permute-start | bytes 589832 | tf_op jit(solution)/shard_map/ppermute | solution.py:124
  11.2 9.6 %collective-permute-start.14 = (bf16[128,768]{1,0:T(8,128)(2,1)S(1)}, bf16[128,768]{1,0:T(8,128)(2,1)S(1)}, u32[]{:S(2)}, u32[]{:S(2)}) collective-permute-start(bf16[128,768]{1,0:T(8,128)(2,1)S(1)} %convert_element_type.80), channel_id=1, source_target_pairs={{0,64},{64,128},{128,192},{192,0},{1,65},{65,129},{129,193},{193,1... | collective-permute-start | bytes 589832 | tf_op jit(solution)/shard_map/ppermute | solution.py:124
  12.8 17.9 %collective-permute-start.1 = (bf16[256,768]{1,0:T(8,128)(2,1)S(1)}, bf16[256,768]{1,0:T(8,128)(2,1)S(1)}, u32[]{:S(2)}, u32[]{:S(2)}) collective-permute-start(bf16[256,768]{1,0:T(8,128)(2,1)S(1)} %collective-permute-done), channel_id=1, source_target_pairs={{0,1},{1,0},{2,3},{3,2},{4,5},{5,4},{6,7},{7,6},{8,9},{9,8},{10,11... | collective-permute-start | bytes 1179656 | tf_op jit(solution)/shard_map/ppermute | solution.py:104
  14.1 10.4 %collective-permute-start.2 = (bf16[128,768]{1,0:T(8,128)(2,1)S(1)}, bf16[128,768]{1,0:T(8,128)(2,1)S(1)}, u32[]{:S(2)}, u32[]{:S(2)}) collective-permute-start(bf16[128,768]{1,0:T(8,128)(2,1)S(1)} %get-tuple-element.86), channel_id=1, source_target_pairs={{0,8},{1,57},{8,16},{9,1},{16,24},{17,9},{24,32},{25,17},{32,40},{... | collective-permute-start | bytes 589832 | tf_op jit(solution)/shard_map/ppermute | solution.py:113
  20.9 5.8 %collective-permute-start.3 = (bf16[128,768]{1,0:T(8,128)(2,1)S(1)}, bf16[128,768]{1,0:T(8,128)(2,1)S(1)}, u32[]{:S(2)}, u32[]{:S(2)}) collective-permute-start(bf16[128,768]{1,0:T(8,128)(2,1)S(1)} %get-tuple-element.85), channel_id=1, source_target_pairs={{0,8},{1,57},{8,16},{9,1},{16,24},{17,9},{24,32},{25,17},{32,40},{... | collective-permute-start | bytes 589832 | tf_op jit(solution)/shard_map/ppermute | solution.py:113
  24.5 5.9 %collective-permute-start.6 = (bf16[128,768]{1,0:T(8,128)(2,1)S(1)}, bf16[128,768]{1,0:T(8,128)(2,1)S(1)}, u32[]{:S(2)}, u32[]{:S(2)}) collective-permute-start(bf16[128,768]{1,0:T(8,128)(2,1)S(1)} %collective-permute-done.2), channel_id=1, source_target_pairs={{0,8},{1,57},{8,16},{9,1},{16,24},{17,9},{24,32},{25,17},{32,40},{... | collective-permute-start | bytes 589832 | tf_op jit(solution)/shard_map/ppermute | solution.py:113
  26.7 5.7 %collective-permute-start.7 = (bf16[128,768]{1,0:T(8,128)(2,1)S(1)}, bf16[128,768]{1,0:T(8,128)(2,1)S(1)}, u32[]{:S(2)}, u32[]{:S(2)}) collective-permute-start(bf16[128,768]{1,0:T(8,128)(2,1)S(1)} %collective-permute-done.3), channel_id=1, source_target_pairs={{0,8},{1,57},{8,16},{9,1},{16,24},{17,9},{24,32},{25,17},{32,40},{... | collective-permute-start | bytes 589832 | tf_op jit(solution)/shard_map/ppermute | solution.py:113
  29.8 5.6 %collective-permute-start.4 = (bf16[128,768]{1,0:T(8,128)(2,1)S(1)}, bf16[128,768]{1,0:T(8,128)(2,1)S(1)}, u32[]{:S(2)}, u32[]{:S(2)}) collective-permute-start(bf16[128,768]{1,0:T(8,128)(2,1)S(1)} %collective-permute-done.2), channel_id=1, source_target_pairs={{0,1},{1,0},{2,3},{3,2},{4,5},{5,4},{6,7},{7,6},{8,9},{9,8},{10,11... | collective-permute-start | bytes 589832 | tf_op jit(solution)/shard_map/ppermute | solution.py:116
  29.8 5.7 %collective-permute-start.5 = (bf16[128,768]{1,0:T(8,128)(2,1)S(1)}, bf16[128,768]{1,0:T(8,128)(2,1)S(1)}, u32[]{:S(2)}, u32[]{:S(2)}) collective-permute-start(bf16[128,768]{1,0:T(8,128)(2,1)S(1)} %collective-permute-done.3), channel_id=1, source_target_pairs={{0,1},{1,0},{2,3},{3,2},{4,5},{5,4},{6,7},{7,6},{8,9},{9,8},{10,11... | collective-permute-start | bytes 589832 | tf_op jit(solution)/shard_map/ppermute | solution.py:116
  30.3 5.2 %collective-permute-start.8 = (bf16[128,768]{1,0:T(8,128)(2,1)S(1)}, bf16[128,768]{1,0:T(8,128)(2,1)S(1)}, u32[]{:S(2)}, u32[]{:S(2)}) collective-permute-start(bf16[128,768]{1,0:T(8,128)(2,1)S(1)} %collective-permute-done.6), channel_id=1, source_target_pairs={{0,1},{1,0},{2,3},{3,2},{4,5},{5,4},{6,7},{7,6},{8,9},{9,8},{10,11... | collective-permute-start | bytes 589832 | tf_op jit(solution)/shard_map/ppermute | solution.py:116
  30.6 8.8 %collective-permute-start.10 = (bf16[128,768]{1,0:T(8,128)(2,1)S(1)}, bf16[128,768]{1,0:T(8,128)(2,1)S(1)}, u32[]{:S(2)}, u32[]{:S(2)}) collective-permute-start(bf16[128,768]{1,0:T(8,128)(2,1)S(1)} %collective-permute-done.6), channel_id=1, source_target_pairs={{0,8},{1,57},{8,16},{9,1},{16,24},{17,9},{24,32},{25,17},{32,40},{... | collective-permute-start | bytes 589832 | tf_op jit(solution)/shard_map/ppermute | solution.py:118
  32.4 4.0 %collective-permute-start.9 = (bf16[128,768]{1,0:T(8,128)(2,1)S(1)}, bf16[128,768]{1,0:T(8,128)(2,1)S(1)}, u32[]{:S(2)}, u32[]{:S(2)}) collective-permute-start(bf16[128,768]{1,0:T(8,128)(2,1)S(1)} %collective-permute-done.7), channel_id=1, source_target_pairs={{0,1},{1,0},{2,3},{3,2},{4,5},{5,4},{6,7},{7,6},{8,9},{9,8},{10,11... | collective-permute-start | bytes 589832 | tf_op jit(solution)/shard_map/ppermute | solution.py:116
  39.4 1.5 %collective-permute-start.11 = (bf16[128,768]{1,0:T(8,128)(2,1)S(1)}, bf16[128,768]{1,0:T(8,128)(2,1)S(1)}, u32[]{:S(2)}, u32[]{:S(2)}) collective-permute-start(bf16[128,768]{1,0:T(8,128)(2,1)S(1)} %collective-permute-done.10), channel_id=1, source_target_pairs={{0,1},{1,0},{2,3},{3,2},{4,5},{5,4},{6,7},{7,6},{8,9},{9,8},{10,11... | collective-permute-start | bytes 589832 | tf_op jit(solution)/shard_map/ppermute | solution.py:119
  41.7 1.2 %collective-permute-start.15 = (f32[24,128]{1,0:T(8,128)S(1)}, f32[24,128]{1,0:T(8,128)S(1)}, u32[]{:S(2)}, u32[]{:S(2)}) collective-permute-start(f32[24,128]{1,0:T(8,128)S(1)} %maximum_maximum_fusion), channel_id=1, source_target_pairs={{0,1},{1,0},{2,3},{3,2},{4,5},{5,4},{6,7},{7,6},{8,9},{9,8},{10,11... | collective-permute-start | bytes 36872 | tf_op jit(solution)/shard_map/ppermute | solution.py:48
  43.0 2.6 %collective-permute-start.16 = (f32[24,128]{1,0:T(8,128)S(1)}, f32[24,128]{1,0:T(8,128)S(1)}, u32[]{:S(2)}, u32[]{:S(2)}) collective-permute-start(f32[24,128]{1,0:T(8,128)S(1)} %add_select_fusion.4), channel_id=1, source_target_pairs={{0,8},{1,57},{8,16},{9,1},{16,24},{17,9},{24,32},{25,17},{32,40},{... | collective-permute-start | bytes 36872 | tf_op jit(solution)/shard_map/ppermute | solution.py:49
  45.7 5.8 %collective-permute-start.17 = (f32[24,128]{1,0:T(8,128)S(1)}, f32[24,128]{1,0:T(8,128)S(1)}, u32[]{:S(2)}, u32[]{:S(2)}) collective-permute-start(f32[24,128]{1,0:T(8,128)S(1)} %add_select_fusion.3), channel_id=1, source_target_pairs={{0,16},{1,41},{8,24},{9,49},{16,32},{17,57},{24,40},{25,1},{32,48}... | collective-permute-start | bytes 36872 | tf_op jit(solution)/shard_map/ppermute | solution.py:50
  47.9 4.4 %collective-permute-start.18 = (f32[24,128]{1,0:T(8,128)S(1)}, f32[24,128]{1,0:T(8,128)S(1)}, u32[]{:S(2)}, u32[]{:S(2)}) collective-permute-start(f32[24,128]{1,0:T(8,128)S(1)} %add_select_fusion.3), channel_id=1, source_target_pairs={{1,57},{9,1},{17,9},{25,17},{33,25},{41,33},{49,41},{57,49},{3,59}... | collective-permute-start | bytes 36872 | tf_op jit(solution)/shard_map/ppermute | solution.py:51
  52.4 5.7 %collective-permute-start.19 = (f32[24,128]{1,0:T(8,128)S(1)}, f32[24,128]{1,0:T(8,128)S(1)}, u32[]{:S(2)}, u32[]{:S(2)}) collective-permute-start(f32[24,128]{1,0:T(8,128)S(1)} %add_select_fusion.2), channel_id=1, source_target_pairs={{0,4},{2,6},{4,0},{6,2},{1,5},{3,7},{5,1},{7,3},{8,12},{10,14},{12... | collective-permute-start | bytes 36872 | tf_op jit(solution)/shard_map/ppermute | solution.py:53
  55.4 3.8 %collective-permute-start.20 = (f32[24,128]{1,0:T(8,128)S(1)}, f32[24,128]{1,0:T(8,128)S(1)}, u32[]{:S(2)}, u32[]{:S(2)}) collective-permute-start(f32[24,128]{1,0:T(8,128)S(1)} %add_select_fusion.2), channel_id=1, source_target_pairs={{0,2},{2,4},{4,6},{6,0},{1,3},{3,5},{5,7},{7,1},{8,10},{10,12},{12... | collective-permute-start | bytes 36872 | tf_op jit(solution)/shard_map/ppermute | solution.py:53
  55.8 3.4 %collective-permute-start.21 = (f32[24,128]{1,0:T(8,128)S(1)}, f32[24,128]{1,0:T(8,128)S(1)}, u32[]{:S(2)}, u32[]{:S(2)}) collective-permute-start(f32[24,128]{1,0:T(8,128)S(1)} %add_select_fusion.2), channel_id=1, source_target_pairs={{0,6},{2,0},{4,2},{6,4},{1,7},{3,1},{5,3},{7,5},{8,14},{10,8},{12,... | collective-permute-start | bytes 36872 | tf_op jit(solution)/shard_map/ppermute | solution.py:53
  59.3 4.2 %collective-permute-start.22 = (f32[24,128]{1,0:T(8,128)S(1)}, f32[24,128]{1,0:T(8,128)S(1)}, u32[]{:S(2)}, u32[]{:S(2)}) collective-permute-start(f32[24,128]{1,0:T(8,128)S(1)} %add_select_fusion.1), channel_id=1, source_target_pairs={{0,1},{1,0},{2,3},{3,2},{4,5},{5,4},{6,7},{7,6},{8,9},{9,8},{10,11... | collective-permute-start | bytes 36872 | tf_op jit(solution)/shard_map/ppermute | solution.py:54
  67.5 13.3 %copy-start = (f32[128,768]{1,0:T(8,128)S(1)}, f32[128,768]{1,0:T(8,128)}, u32[]{:S(2)}) copy-start(f32[128,768]{1,0:T(8,128)} %param.7) | copy-start | bytes 1179652
  67.6 13.2 %collective-permute-start.25 = (f16[128,768]{1,0:T(8,128)(2,1)S(1)}, f16[128,768]{1,0:T(8,128)(2,1)S(1)}, u32[]{:S(2)}, u32[]{:S(2)}) collective-permute-start(f16[128,768]{1,0:T(8,128)(2,1)S(1)} %get-tuple-element.83), channel_id=1, source_target_pairs={{0,64},{64,128},{128,192},{192,0},{1,65},{65,129},{129,193},{193,1... | collective-permute-start | bytes 589832 | tf_op jit(solution)/shard_map/ppermute | solution.py:145
  67.9 12.9 %collective-permute-start.26 = (f16[128,768]{1,0:T(8,128)(2,1)S(1)}, f16[128,768]{1,0:T(8,128)(2,1)S(1)}, u32[]{:S(2)}, u32[]{:S(2)}) collective-permute-start(f16[128,768]{1,0:T(8,128)(2,1)S(1)} %get-tuple-element.84), channel_id=1, source_target_pairs={{0,192},{64,0},{128,64},{192,128},{1,193},{65,1},{129,65},{193,129... | collective-permute-start | bytes 589832 | tf_op jit(solution)/shard_map/ppermute | solution.py:145
  70.6 5.2 %collective-permute-start.23 = (f16[64,768]{1,0:T(8,128)(2,1)S(1)}, f16[64,768]{1,0:T(8,128)(2,1)S(1)}, u32[]{:S(2)}, u32[]{:S(2)}) collective-permute-start(f16[64,768]{1,0:T(8,128)(2,1)S(1)} %get-tuple-element.81), channel_id=1, source_target_pairs={{0,128},{64,192},{128,0},{192,64},{1,129},{65,193},{129,1},{193,65... | collective-permute-start | bytes 294920 | tf_op jit(solution)/shard_map/ppermute | solution.py:145
  70.6 7.3 %collective-permute-start.24 = (f16[64,768]{1,0:T(8,128)(2,1)S(1)}, f16[64,768]{1,0:T(8,128)(2,1)S(1)}, u32[]{:S(2)}, u32[]{:S(2)}) collective-permute-start(f16[64,768]{1,0:T(8,128)(2,1)S(1)} %get-tuple-element.82), channel_id=1, source_target_pairs={{0,128},{64,192},{128,0},{192,64},{1,129},{65,193},{129,1},{193,65... | collective-permute-start | bytes 294920 | tf_op jit(solution)/shard_map/ppermute | solution.py:145
  74.1 7.9 %collective-permute-start.27 = (f32[1,1]{1,0:T(1,128)}, f32[1,1]{1,0:T(1,128)}, u32[]{:S(2)}, u32[]{:S(2)}) collective-permute-start(f32[1,1]{1,0:T(1,128)} %bitcast.25), channel_id=1, source_target_pairs={{0,128},{64,192},{128,0},{192,64},{1,129},{65,193},{129,1},{193,65... | collective-permute-start | bytes 20 | tf_op jit(solution)/shard_map/ppermute | solution.py:152
  75.7 6.3 %collective-permute-start.28 = (f32[1,1]{1,0:T(1,128)}, f32[1,1]{1,0:T(1,128)}, u32[]{:S(2)}, u32[]{:S(2)}) collective-permute-start(f32[1,1]{1,0:T(1,128)} %bitcast.25), channel_id=1, source_target_pairs={{0,64},{64,128},{128,192},{192,0},{1,65},{65,129},{129,193},{193,1... | collective-permute-start | bytes 20 | tf_op jit(solution)/shard_map/ppermute | solution.py:152
  77.9 4.1 %collective-permute-start.29 = (f32[1,1]{1,0:T(1,128)}, f32[1,1]{1,0:T(1,128)}, u32[]{:S(2)}, u32[]{:S(2)}) collective-permute-start(f32[1,1]{1,0:T(1,128)} %bitcast.25), channel_id=1, source_target_pairs={{0,192},{64,0},{128,64},{192,128},{1,193},{65,1},{129,65},{193,129... | collective-permute-start | bytes 20 | tf_op jit(solution)/shard_map/ppermute | solution.py:152
  (2 other events, 26.6 us)

commit v2 on v1

--- a/solution.py
+++ b/solution.py
@@ -29,6 +29,10 @@
 
 SWAP = [(0, 1), (1, 0)]
 OPPOSITE = [(z * 2 + c, (z + (1, -1)[c]) % 8 * 2 + c) for z in range(8) for c in range(2)]
+
+
+def after(x, *others):
+    return lax.optimization_barrier((x, *others))[0]
 
 
 def adam_update(centroids, first_moment, second_moment, gradient):
@@ -141,16 +145,17 @@
     sent = jnp.dot(weights[: 3 * OWN], rows, preferred_element_type=jnp.float32)
     sent = (sent * SCALE).astype(jnp.float16)
     back = []
-    for some, step in ((slice(128, 192), 2), (slice(192, 256), -2), (slice(0, 128), 1), (slice(256, 384), -1)):
+    for some, step in ((slice(128, 256), 2), (slice(0, 128), 1), (slice(256, 384), -1)):
         back.append(lax.ppermute(sent[some], "x", turn(4, step)).astype(jnp.float32))
     own = jnp.dot(weights[3 * OWN :], rows, preferred_element_type=jnp.float32)
     own = lax.optimization_barrier(own)
     at = lax.broadcasted_iota(jnp.int32, state.shape, 0)
+    state = after(state, sent)
     loss = jnp.sum(jnp.where(at < 16, state, -state)).reshape(1, 1)
     others = []
     for step in (2, 1, -1):
         others.append(lax.ppermute(loss, "x", turn(4, step)))
-    gradient = own + (jnp.concatenate(back[:2]) + back[2] + back[3]) * (1.0 / SCALE)
+    gradient = own + (back[0] + back[1] + back[2]) * (1.0 / SCALE)
     return (gradient, [loss] + others)
 
 

time: 87 us -> 86.4 us (level); the launches traced: 85.7 us -> 86.1 us
  waiting for transfers between devices: 15 us -> 18.4 us
  starting transfers between devices: 53.2 us -> 50.1 us
    ppermute x4 -> x3, waiting for transfers between devices: 1.5 us -> 4.89 us  [body(): lax.ppermute(sent[some], 'x', turn(4, step)).astype(jnp.float32)]
    ppermute x3, starting transfers between devices: 5.13 us -> 3.2 us  [body(): others.append(lax.ppermute(loss, 'x', turn(4, step)))]
    ppermute x4 -> x3, starting transfers between devices: 5.94 us -> 4.83 us  [body(): lax.ppermute(sent[some], 'x', turn(4, step)).astype(jnp.float32)]
  transfers between devices with their start and end apart: 30 -> 29, of which waited for: 12 -> 13; matrix products, arithmetic and copies ran while one was open for 9% -> 9% of each run, Pallas kernels for 0% -> 0%
where the time goes in v2:
time: 86.4 us; the launch traced here: 86.1 us
  starting transfers between devices  50.1 us (58%)
  waiting for transfers between devices  18.4 us (21%)
  matrix products  6.51 us (8%)
  other arithmetic  4.82 us (6%)
  between operations  4.65 us (5%)
  local copies, waits for them, and re-layouts  1.59 us (2%)
    ppermute x4, starting transfers between devices, body(): parts[i] = lax.ppermute(parts[i], ('z', 'c'), OPPOSITE)  8.94 us
    ppermute x1, starting transfers between devices, body(): part = lax.ppermute(query_emb, ('z', 'c'), OPPOSITE)  6.47 us
    ppermute x3, starting transfers between devices, over_lists(): lax.ppermute(state, 'y', turn(4, step))  5.63 us
    ppermute x3, waiting for transfers between devices, body(): lax.ppermute(half, 'x', turn(4, -hop))  4.95 us
    ppermute x3, waiting for transfers between devices, body(): lax.ppermute(sent[some], 'x', turn(4, step)).astype(jnp.float32)  4.89 us
    ppermute x3, starting transfers between devices, body(): lax.ppermute(sent[some], 'x', turn(4, step)).astype(jnp.float32)  4.83 us
    dot_general x4, matrix products, logits_of(): jnp.einsum('kd,rd->kr', lists, rows, preferred_element_type=jnp.float32)  4.55 us
    ppermute x4, starting transfers between devices, body(): swapped.append(lax.ppermute(parts[i], 'c', SWAP))  3.75 us
  transfers between devices with their start and end apart: 29, of which 13 were waited for; matrix products, arithmetic and copies ran while one was open for 9% of the time, Pallas kernels for 0%

profile of v2, /device:TPU:1, one launch (start us, length us, event | category | flops | bytes accessed | tf_op | source)
XLA Modules:
  0.0 86.1 jit_solution(17201042542578461169)
XLA Ops:
  0.6 6.5 %collective-permute-start = (bf16[256,768]{1,0:T(8,128)(2,1)}, bf16[256,768]{1,0:T(8,128)(2,1)S(1)}, u32[]{:S(2)}, u32[]{:S(2)}) collective-permute-start(bf16[256,768]{1,0:T(8,128)(2,1)} %param.5), channel_id=1, source_target_pairs={{0,8},{1,57},{8,16},{9,1},{16,24},{17,9},{24,32},{25,17},{32,40},{... | collective-permute-start | bytes 1179656 | tf_op jit(solution)/shard_map/ppermute | solution.py:104
  7.1 1.0 %convert_element_type.81 = bf16[128,768]{1,0:T(8,128)(2,1)S(1)} convert(f32[128,768]{1,0:T(8,128)} %param.7) | non-fusion elementwise | flops 98304 | bytes 589824 | tf_op jit(solution)/shard_map/convert_element_type | solution.py:127
  8.1 2.6 %collective-permute-start.12 = (bf16[128,768]{1,0:T(8,128)(2,1)S(1)}, bf16[128,768]{1,0:T(8,128)(2,1)S(1)}, u32[]{:S(2)}, u32[]{:S(2)}) collective-permute-start(bf16[128,768]{1,0:T(8,128)(2,1)S(1)} %convert_element_type.81), channel_id=1, source_target_pairs={{0,192},{64,0},{128,64},{192,128},{1,193},{65,1},{129,65},{193,129... | collective-permute-start | bytes 589832 | tf_op jit(solution)/shard_map/ppermute | solution.py:128
  12.8 1.3 %collective-permute-start.1 = (bf16[256,768]{1,0:T(8,128)(2,1)S(1)}, bf16[256,768]{1,0:T(8,128)(2,1)S(1)}, u32[]{:S(2)}, u32[]{:S(2)}) collective-permute-start(bf16[256,768]{1,0:T(8,128)(2,1)S(1)} %collective-permute-done), channel_id=1, source_target_pairs={{0,1},{1,0},{2,3},{3,2},{4,5},{5,4},{6,7},{7,6},{8,9},{9,8},{10,11... | collective-permute-start | bytes 1179656 | tf_op jit(solution)/shard_map/ppermute | solution.py:108
  14.1 1.8 %collective-permute-start.2 = (bf16[128,768]{1,0:T(8,128)(2,1)S(1)}, bf16[128,768]{1,0:T(8,128)(2,1)S(1)}, u32[]{:S(2)}, u32[]{:S(2)}) collective-permute-start(bf16[128,768]{1,0:T(8,128)(2,1)S(1)} %get-tuple-element.85), channel_id=1, source_target_pairs={{0,8},{1,57},{8,16},{9,1},{16,24},{17,9},{24,32},{25,17},{32,40},{... | collective-permute-start | bytes 589832 | tf_op jit(solution)/shard_map/ppermute | solution.py:117
  15.9 1.2 %collective-permute-done.12 = bf16[128,768]{1,0:T(8,128)(2,1)S(1)} collective-permute-done((bf16[128,768]{1,0:T(8,128)(2,1)S(1)}, bf16[128,768]{1,0:T(8,128)(2,1)S(1)}, u32[]{:S(2)}, u32[]{:S(2)}) %collective-permute-start.12) | collective-permute-done | bytes 196640 | tf_op jit(solution)/shard_map/ppermute | solution.py:128
  17.1 1.6 %collective-permute-done.13 = bf16[128,768]{1,0:T(8,128)(2,1)S(1)} collective-permute-done((bf16[128,768]{1,0:T(8,128)(2,1)S(1)}, bf16[128,768]{1,0:T(8,128)(2,1)S(1)}, u32[]{:S(2)}, u32[]{:S(2)}) %collective-permute-start.13) | collective-permute-done | bytes 196640 | tf_op jit(solution)/shard_map/ppermute | solution.py:128
  18.7 2.1 %collective-permute-done.14 = bf16[128,768]{1,0:T(8,128)(2,1)S(1)} collective-permute-done((bf16[128,768]{1,0:T(8,128)(2,1)S(1)}, bf16[128,768]{1,0:T(8,128)(2,1)S(1)}, u32[]{:S(2)}, u32[]{:S(2)}) %collective-permute-start.14) | collective-permute-done | bytes 196640 | tf_op jit(solution)/shard_map/ppermute | solution.py:128
  20.9 3.2 %collective-permute-start.3 = (bf16[128,768]{1,0:T(8,128)(2,1)S(1)}, bf16[128,768]{1,0:T(8,128)(2,1)S(1)}, u32[]{:S(2)}, u32[]{:S(2)}) collective-permute-start(bf16[128,768]{1,0:T(8,128)(2,1)S(1)} %get-tuple-element.84), channel_id=1, source_target_pairs={{0,8},{1,57},{8,16},{9,1},{16,24},{17,9},{24,32},{25,17},{32,40},{... | collective-permute-start | bytes 589832 | tf_op jit(solution)/shard_map/ppermute | solution.py:117
  25.3 1.4 %collective-permute-done.3 = bf16[128,768]{1,0:T(8,128)(2,1)S(1)} collective-permute-done((bf16[128,768]{1,0:T(8,128)(2,1)S(1)}, bf16[128,768]{1,0:T(8,128)(2,1)S(1)}, u32[]{:S(2)}, u32[]{:S(2)}) %collective-permute-start.3) | collective-permute-done | bytes 196640 | tf_op jit(solution)/shard_map/ppermute | solution.py:117
  26.7 3.1 %collective-permute-start.7 = (bf16[128,768]{1,0:T(8,128)(2,1)S(1)}, bf16[128,768]{1,0:T(8,128)(2,1)S(1)}, u32[]{:S(2)}, u32[]{:S(2)}) collective-permute-start(bf16[128,768]{1,0:T(8,128)(2,1)S(1)} %collective-permute-done.3), channel_id=1, source_target_pairs={{0,8},{1,57},{8,16},{9,1},{16,24},{17,9},{24,32},{25,17},{32,40},{... | collective-permute-start | bytes 589832 | tf_op jit(solution)/shard_map/ppermute | solution.py:117
  30.6 1.7 %collective-permute-start.10 = (bf16[128,768]{1,0:T(8,128)(2,1)S(1)}, bf16[128,768]{1,0:T(8,128)(2,1)S(1)}, u32[]{:S(2)}, u32[]{:S(2)}) collective-permute-start(bf16[128,768]{1,0:T(8,128)(2,1)S(1)} %collective-permute-done.6), channel_id=1, source_target_pairs={{0,8},{1,57},{8,16},{9,1},{16,24},{17,9},{24,32},{25,17},{32,40},{... | collective-permute-start | bytes 589832 | tf_op jit(solution)/shard_map/ppermute | solution.py:122
  32.4 3.0 %collective-permute-start.9 = (bf16[128,768]{1,0:T(8,128)(2,1)S(1)}, bf16[128,768]{1,0:T(8,128)(2,1)S(1)}, u32[]{:S(2)}, u32[]{:S(2)}) collective-permute-start(bf16[128,768]{1,0:T(8,128)(2,1)S(1)} %collective-permute-done.7), channel_id=1, source_target_pairs={{0,1},{1,0},{2,3},{3,2},{4,5},{5,4},{6,7},{7,6},{8,9},{9,8},{10,11... | collective-permute-start | bytes 589832 | tf_op jit(solution)/shard_map/ppermute | solution.py:120
  35.6 0.9 collective-permute-done.9
  36.5 1.8 %fusion.22 = (f32[2048]{0:T(1024)S(1)}, f32[512,2048]{1,0:T(8,128)S(1)}) fusion(bf16[512,768]{1,0:T(8,128)(2,1)S(1)} %pad_maximum_fusion, bf16[2048,768]{1,0:T(8,128)(2,1)S(1)} %bitcast.57), kind=kOutput, calls=%fused_computation.70 | convolution fusion | flops 1611659264 | bytes 8134656 | tf_op jit(solution)/shard_map/kd,rd->kr/dot_general | solution.py:70
  38.3 1.1 %exponential_reduce_fusion = (f32[2048]{0:T(1024)S(1)}, f32[2048]{0:T(1024)S(1)}) fusion(f32[512,2048]{1,0:T(8,128)S(1)} %get-tuple-element.58, f32[2048]{0:T(1024)S(1)} %get-tuple-element.57, s32[2048]{0:T(1024)S(1)} %bitcast.66), kind=kLoop, calls=%fused_computation.3 | loop fusion | flops 5238784 | bytes 4227072 | tf_op jit(solution)/shard_map/reduce_sum | solution.py:77
  42.1 0.8 collective-permute-done.15
  43.6 2.0 %collective-permute-done.16 = f32[24,128]{1,0:T(8,128)S(1)} collective-permute-done((f32[24,128]{1,0:T(8,128)S(1)}, f32[24,128]{1,0:T(8,128)S(1)}, u32[]{:S(2)}, u32[]{:S(2)}) %collective-permute-start.16) | collective-permute-done | bytes 12320 | tf_op jit(solution)/shard_map/ppermute | solution.py:53
  45.7 2.2 %collective-permute-start.17 = (f32[24,128]{1,0:T(8,128)S(1)}, f32[24,128]{1,0:T(8,128)S(1)}, u32[]{:S(2)}, u32[]{:S(2)}) collective-permute-start(f32[24,128]{1,0:T(8,128)S(1)} %add_select_fusion.3), channel_id=1, source_target_pairs={{0,16},{1,41},{8,24},{9,49},{16,32},{17,57},{24,40},{25,1},{32,48}... | collective-permute-start | bytes 36872 | tf_op jit(solution)/shard_map/ppermute | solution.py:54
  47.9 3.6 %collective-permute-start.18 = (f32[24,128]{1,0:T(8,128)S(1)}, f32[24,128]{1,0:T(8,128)S(1)}, u32[]{:S(2)}, u32[]{:S(2)}) collective-permute-start(f32[24,128]{1,0:T(8,128)S(1)} %add_select_fusion.3), channel_id=1, source_target_pairs={{1,57},{9,1},{17,9},{25,17},{33,25},{41,33},{49,41},{57,49},{3,59}... | collective-permute-start | bytes 36872 | tf_op jit(solution)/shard_map/ppermute | solution.py:55
  52.4 3.0 %collective-permute-start.19 = (f32[24,128]{1,0:T(8,128)S(1)}, f32[24,128]{1,0:T(8,128)S(1)}, u32[]{:S(2)}, u32[]{:S(2)}) collective-permute-start(f32[24,128]{1,0:T(8,128)S(1)} %add_select_fusion.2), channel_id=1, source_target_pairs={{0,4},{2,6},{4,0},{6,2},{1,5},{3,7},{5,1},{7,3},{8,12},{10,14},{12... | collective-permute-start | bytes 36872 | tf_op jit(solution)/shard_map/ppermute | solution.py:57
  55.8 2.3 %collective-permute-start.21 = (f32[24,128]{1,0:T(8,128)S(1)}, f32[24,128]{1,0:T(8,128)S(1)}, u32[]{:S(2)}, u32[]{:S(2)}) collective-permute-start(f32[24,128]{1,0:T(8,128)S(1)} %add_select_fusion.2), channel_id=1, source_target_pairs={{0,6},{2,0},{4,2},{6,4},{1,7},{3,1},{5,3},{7,5},{8,14},{10,8},{12,... | collective-permute-start | bytes 36872 | tf_op jit(solution)/shard_map/ppermute | solution.py:57
  58.1 1.1 %collective-permute-done.20 = f32[24,128]{1,0:T(8,128)S(1)} collective-permute-done((f32[24,128]{1,0:T(8,128)S(1)}, f32[24,128]{1,0:T(8,128)S(1)}, u32[]{:S(2)}, u32[]{:S(2)}) %collective-permute-start.20) | collective-permute-done | bytes 12320 | tf_op jit(solution)/shard_map/ppermute | solution.py:57
  59.3 3.3 %collective-permute-start.22 = (f32[24,128]{1,0:T(8,128)S(1)}, f32[24,128]{1,0:T(8,128)S(1)}, u32[]{:S(2)}, u32[]{:S(2)}) collective-permute-start(f32[24,128]{1,0:T(8,128)S(1)} %add_select_fusion.1), channel_id=1, source_target_pairs={{0,1},{1,0},{2,3},{3,2},{4,5},{5,4},{6,7},{7,6},{8,9},{9,8},{10,11... | collective-permute-start | bytes 36872 | tf_op jit(solution)/shard_map/ppermute | solution.py:58
  63.5 2.0 %subtract_convert_fusion = bf16[512,2048]{1,0:T(8,128)(2,1)S(1)} fusion(bf16[512,768]{1,0:T(8,128)(2,1)S(1)} %pad_maximum_fusion, bf16[2048,768]{1,0:T(8,128)(2,1)S(1)} %bitcast.58, f32[2048]{0:T(1024)S(1)} %slice_bitcast_fusion, s32[2048]{0:T(1024)S(1)} %bitcast.67), kind=kOutput, calls=%fused_computation | convolution fusion | flops 1615855616 | bytes 6045696 | tf_op jit(solution)/shard_map/kd,rd->kr/dot_general | solution.py:70
  65.5 1.4 %fusion.5 = f16[384,768]{1,0:T(8,128)(2,1)S(1)} fusion(bf16[2048,768]{1,0:T(8,128)(2,1)S(1)} %bitcast.59, bf16[512,2048]{1,0:T(8,128)(2,1)S(1)} %subtract_convert_fusion), kind=kOutput, calls=%fused_computation.7 | convolution fusion | flops 1208549376 | bytes 5308416 | tf_op jit(solution)/shard_map/dot_general | solution.py:145
  68.6 2.1 %collective-permute-start.23 = (f16[128,768]{1,0:T(8,128)(2,1)S(1)}, f16[128,768]{1,0:T(8,128)(2,1)S(1)}, u32[]{:S(2)}, u32[]{:S(2)}) collective-permute-start(f16[128,768]{1,0:T(8,128)(2,1)S(1)} %get-tuple-element.81), channel_id=1, source_target_pairs={{0,128},{64,192},{128,0},{192,64},{1,129},{65,193},{129,1},{193,65... | collective-permute-start | bytes 589832 | tf_op jit(solution)/shard_map/ppermute | solution.py:149
  71.5 1.9 %collective-permute-start.25 = (f16[128,768]{1,0:T(8,128)(2,1)S(1)}, f16[128,768]{1,0:T(8,128)(2,1)S(1)}, u32[]{:S(2)}, u32[]{:S(2)}) collective-permute-start(f16[128,768]{1,0:T(8,128)(2,1)S(1)} %get-tuple-element.82), channel_id=1, source_target_pairs={{0,192},{64,0},{128,64},{192,128},{1,193},{65,1},{129,65},{193,129... | collective-permute-start | bytes 589832 | tf_op jit(solution)/shard_map/ppermute | solution.py:149
  74.0 1.7 %collective-permute-done.23 = f16[128,768]{1,0:T(8,128)(2,1)S(1)} collective-permute-done((f16[128,768]{1,0:T(8,128)(2,1)S(1)}, f16[128,768]{1,0:T(8,128)(2,1)S(1)}, u32[]{:S(2)}, u32[]{:S(2)}) %collective-permute-start.23) | collective-permute-done | bytes 196640 | tf_op jit(solution)/shard_map/ppermute | solution.py:149
  75.7 2.3 %collective-permute-start.28 = (f32[1,1]{1,0:T(1,128)}, f32[1,1]{1,0:T(1,128)}, u32[]{:S(2)}, u32[]{:S(2)}) collective-permute-start(f32[1,1]{1,0:T(1,128)} %bitcast.25), channel_id=1, source_target_pairs={{0,192},{64,0},{128,64},{192,128},{1,193},{65,1},{129,65},{193,129... | collective-permute-start | bytes 20 | tf_op jit(solution)/shard_map/ppermute | solution.py:157
  78.0 3.2 %collective-permute-done.24 = f16[128,768]{1,0:T(8,128)(2,1)S(1)} collective-permute-done((f16[128,768]{1,0:T(8,128)(2,1)S(1)}, f16[128,768]{1,0:T(8,128)(2,1)S(1)}, u32[]{:S(2)}, u32[]{:S(2)}) %collective-permute-start.24) | collective-permute-done | bytes 196640 | tf_op jit(solution)/shard_map/ppermute | solution.py:149
  81.2 1.2 %divide_subtract_fusion = (f32[128,768]{1,0:T(8,128)}, f32[128,768]{1,0:T(8,128)}, f32[128,768]{1,0:T(8,128)}) fusion(f32[128,768]{1,0:T(8,128)S(1)} %copy-done, f32[128,768]{1,0:T(8,128)S(1)} %fusion.8, f16[128,768]{1,0:T(8,128)(2,1)S(1)} %collective-permute-done.25, f16[128,768]{1,0:T(8,128)(2,1)S(1)} %collective-permute-done.24, ...), kind=kLoop, calls=%fused_computation.13 | loop fusion | flops 1769472 | bytes 3342336 | tf_op jit(solution)/shard_map/sub | solution.py:41
  (81 shorter events, 13.1 us)
Async XLA Ops:
  0.6 23.8 %copy-start.3 = (bf16[256,768]{1,0:T(8,128)(2,1)S(1)}, bf16[256,768]{1,0:T(8,128)(2,1)}, u32[]{:S(2)}) copy-start(bf16[256,768]{1,0:T(8,128)(2,1)} %param.5) | copy-start | bytes 1179652
  0.6 12.1 %collective-permute-start = (bf16[256,768]{1,0:T(8,128)(2,1)}, bf16[256,768]{1,0:T(8,128)(2,1)S(1)}, u32[]{:S(2)}, u32[]{:S(2)}) collective-permute-start(bf16[256,768]{1,0:T(8,128)(2,1)} %param.5), channel_id=1, source_target_pairs={{0,8},{1,57},{8,16},{9,1},{16,24},{17,9},{24,32},{25,17},{32,40},{... | collective-permute-start | bytes 1179656 | tf_op jit(solution)/shard_map/ppermute | solution.py:104
  8.1 9.0 %collective-permute-start.12 = (bf16[128,768]{1,0:T(8,128)(2,1)S(1)}, bf16[128,768]{1,0:T(8,128)(2,1)S(1)}, u32[]{:S(2)}, u32[]{:S(2)}) collective-permute-start(bf16[128,768]{1,0:T(8,128)(2,1)S(1)} %convert_element_type.81), channel_id=1, source_target_pairs={{0,192},{64,0},{128,64},{192,128},{1,193},{65,1},{129,65},{193,129... | collective-permute-start | bytes 589832 | tf_op jit(solution)/shard_map/ppermute | solution.py:128
  10.7 8.0 %collective-permute-start.13 = (bf16[128,768]{1,0:T(8,128)(2,1)S(1)}, bf16[128,768]{1,0:T(8,128)(2,1)S(1)}, u32[]{:S(2)}, u32[]{:S(2)}) collective-permute-start(bf16[128,768]{1,0:T(8,128)(2,1)S(1)} %convert_element_type.81), channel_id=1, source_target_pairs={{0,128},{64,192},{128,0},{192,64},{1,129},{65,193},{129,1},{193,65... | collective-permute-start | bytes 589832 | tf_op jit(solution)/shard_map/ppermute | solution.py:128
  11.2 9.6 %collective-permute-start.14 = (bf16[128,768]{1,0:T(8,128)(2,1)S(1)}, bf16[128,768]{1,0:T(8,128)(2,1)S(1)}, u32[]{:S(2)}, u32[]{:S(2)}) collective-permute-start(bf16[128,768]{1,0:T(8,128)(2,1)S(1)} %convert_element_type.81), channel_id=1, source_target_pairs={{0,64},{64,128},{128,192},{192,0},{1,65},{65,129},{129,193},{193,1... | collective-permute-start | bytes 589832 | tf_op jit(solution)/shard_map/ppermute | solution.py:128
  12.8 17.9 %collective-permute-start.1 = (bf16[256,768]{1,0:T(8,128)(2,1)S(1)}, bf16[256,768]{1,0:T(8,128)(2,1)S(1)}, u32[]{:S(2)}, u32[]{:S(2)}) collective-permute-start(bf16[256,768]{1,0:T(8,128)(2,1)S(1)} %collective-permute-done), channel_id=1, source_target_pairs={{0,1},{1,0},{2,3},{3,2},{4,5},{5,4},{6,7},{7,6},{8,9},{9,8},{10,11... | collective-permute-start | bytes 1179656 | tf_op jit(solution)/shard_map/ppermute | solution.py:108
  14.1 10.4 %collective-permute-start.2 = (bf16[128,768]{1,0:T(8,128)(2,1)S(1)}, bf16[128,768]{1,0:T(8,128)(2,1)S(1)}, u32[]{:S(2)}, u32[]{:S(2)}) collective-permute-start(bf16[128,768]{1,0:T(8,128)(2,1)S(1)} %get-tuple-element.85), channel_id=1, source_target_pairs={{0,8},{1,57},{8,16},{9,1},{16,24},{17,9},{24,32},{25,17},{32,40},{... | collective-permute-start | bytes 589832 | tf_op jit(solution)/shard_map/ppermute | solution.py:117
  20.9 5.8 %collective-permute-start.3 = (bf16[128,768]{1,0:T(8,128)(2,1)S(1)}, bf16[128,768]{1,0:T(8,128)(2,1)S(1)}, u32[]{:S(2)}, u32[]{:S(2)}) collective-permute-start(bf16[128,768]{1,0:T(8,128)(2,1)S(1)} %get-tuple-element.84), channel_id=1, source_target_pairs={{0,8},{1,57},{8,16},{9,1},{16,24},{17,9},{24,32},{25,17},{32,40},{... | collective-permute-start | bytes 589832 | tf_op jit(solution)/shard_map/ppermute | solution.py:117
  24.5 5.9 %collective-permute-start.6 = (bf16[128,768]{1,0:T(8,128)(2,1)S(1)}, bf16[128,768]{1,0:T(8,128)(2,1)S(1)}, u32[]{:S(2)}, u32[]{:S(2)}) collective-permute-start(bf16[128,768]{1,0:T(8,128)(2,1)S(1)} %collective-permute-done.2), channel_id=1, source_target_pairs={{0,8},{1,57},{8,16},{9,1},{16,24},{17,9},{24,32},{25,17},{32,40},{... | collective-permute-start | bytes 589832 | tf_op jit(solution)/shard_map/ppermute | solution.py:117
  26.7 5.7 %collective-permute-start.7 = (bf16[128,768]{1,0:T(8,128)(2,1)S(1)}, bf16[128,768]{1,0:T(8,128)(2,1)S(1)}, u32[]{:S(2)}, u32[]{:S(2)}) collective-permute-start(bf16[128,768]{1,0:T(8,128)(2,1)S(1)} %collective-permute-done.3), channel_id=1, source_target_pairs={{0,8},{1,57},{8,16},{9,1},{16,24},{17,9},{24,32},{25,17},{32,40},{... | collective-permute-start | bytes 589832 | tf_op jit(solution)/shard_map/ppermute | solution.py:117
  29.8 5.6 %collective-permute-start.4 = (bf16[128,768]{1,0:T(8,128)(2,1)S(1)}, bf16[128,768]{1,0:T(8,128)(2,1)S(1)}, u32[]{:S(2)}, u32[]{:S(2)}) collective-permute-start(bf16[128,768]{1,0:T(8,128)(2,1)S(1)} %collective-permute-done.2), channel_id=1, source_target_pairs={{0,1},{1,0},{2,3},{3,2},{4,5},{5,4},{6,7},{7,6},{8,9},{9,8},{10,11... | collective-permute-start | bytes 589832 | tf_op jit(solution)/shard_map/ppermute | solution.py:120
  29.8 5.7 %collective-permute-start.5 = (bf16[128,768]{1,0:T(8,128)(2,1)S(1)}, bf16[128,768]{1,0:T(8,128)(2,1)S(1)}, u32[]{:S(2)}, u32[]{:S(2)}) collective-permute-start(bf16[128,768]{1,0:T(8,128)(2,1)S(1)} %collective-permute-done.3), channel_id=1, source_target_pairs={{0,1},{1,0},{2,3},{3,2},{4,5},{5,4},{6,7},{7,6},{8,9},{9,8},{10,11... | collective-permute-start | bytes 589832 | tf_op jit(solution)/shard_map/ppermute | solution.py:120
  30.3 5.2 %collective-permute-start.8 = (bf16[128,768]{1,0:T(8,128)(2,1)S(1)}, bf16[128,768]{1,0:T(8,128)(2,1)S(1)}, u32[]{:S(2)}, u32[]{:S(2)}) collective-permute-start(bf16[128,768]{1,0:T(8,128)(2,1)S(1)} %collective-permute-done.6), channel_id=1, source_target_pairs={{0,1},{1,0},{2,3},{3,2},{4,5},{5,4},{6,7},{7,6},{8,9},{9,8},{10,11... | collective-permute-start | bytes 589832 | tf_op jit(solution)/shard_map/ppermute | solution.py:120
  30.6 8.8 %collective-permute-start.10 = (bf16[128,768]{1,0:T(8,128)(2,1)S(1)}, bf16[128,768]{1,0:T(8,128)(2,1)S(1)}, u32[]{:S(2)}, u32[]{:S(2)}) collective-permute-start(bf16[128,768]{1,0:T(8,128)(2,1)S(1)} %collective-permute-done.6), channel_id=1, source_target_pairs={{0,8},{1,57},{8,16},{9,1},{16,24},{17,9},{24,32},{25,17},{32,40},{... | collective-permute-start | bytes 589832 | tf_op jit(solution)/shard_map/ppermute | solution.py:122
  32.4 4.0 %collective-permute-start.9 = (bf16[128,768]{1,0:T(8,128)(2,1)S(1)}, bf16[128,768]{1,0:T(8,128)(2,1)S(1)}, u32[]{:S(2)}, u32[]{:S(2)}) collective-permute-start(bf16[128,768]{1,0:T(8,128)(2,1)S(1)} %collective-permute-done.7), channel_id=1, source_target_pairs={{0,1},{1,0},{2,3},{3,2},{4,5},{5,4},{6,7},{7,6},{8,9},{9,8},{10,11... | collective-permute-start | bytes 589832 | tf_op jit(solution)/shard_map/ppermute | solution.py:120
  39.4 1.5 %collective-permute-start.11 = (bf16[128,768]{1,0:T(8,128)(2,1)S(1)}, bf16[128,768]{1,0:T(8,128)(2,1)S(1)}, u32[]{:S(2)}, u32[]{:S(2)}) collective-permute-start(bf16[128,768]{1,0:T(8,128)(2,1)S(1)} %collective-permute-done.10), channel_id=1, source_target_pairs={{0,1},{1,0},{2,3},{3,2},{4,5},{5,4},{6,7},{7,6},{8,9},{9,8},{10,11... | collective-permute-start | bytes 589832 | tf_op jit(solution)/shard_map/ppermute | solution.py:123
  41.7 1.2 %collective-permute-start.15 = (f32[24,128]{1,0:T(8,128)S(1)}, f32[24,128]{1,0:T(8,128)S(1)}, u32[]{:S(2)}, u32[]{:S(2)}) collective-permute-start(f32[24,128]{1,0:T(8,128)S(1)} %maximum_maximum_fusion), channel_id=1, source_target_pairs={{0,1},{1,0},{2,3},{3,2},{4,5},{5,4},{6,7},{7,6},{8,9},{9,8},{10,11... | collective-permute-start | bytes 36872 | tf_op jit(solution)/shard_map/ppermute | solution.py:52
  43.0 2.6 %collective-permute-start.16 = (f32[24,128]{1,0:T(8,128)S(1)}, f32[24,128]{1,0:T(8,128)S(1)}, u32[]{:S(2)}, u32[]{:S(2)}) collective-permute-start(f32[24,128]{1,0:T(8,128)S(1)} %add_select_fusion.4), channel_id=1, source_target_pairs={{0,8},{1,57},{8,16},{9,1},{16,24},{17,9},{24,32},{25,17},{32,40},{... | collective-permute-start | bytes 36872 | tf_op jit(solution)/shard_map/ppermute | solution.py:53
  45.7 5.8 %collective-permute-start.17 = (f32[24,128]{1,0:T(8,128)S(1)}, f32[24,128]{1,0:T(8,128)S(1)}, u32[]{:S(2)}, u32[]{:S(2)}) collective-permute-start(f32[24,128]{1,0:T(8,128)S(1)} %add_select_fusion.3), channel_id=1, source_target_pairs={{0,16},{1,41},{8,24},{9,49},{16,32},{17,57},{24,40},{25,1},{32,48}... | collective-permute-start | bytes 36872 | tf_op jit(solution)/shard_map/ppermute | solution.py:54
  47.9 4.4 %collective-permute-start.18 = (f32[24,128]{1,0:T(8,128)S(1)}, f32[24,128]{1,0:T(8,128)S(1)}, u32[]{:S(2)}, u32[]{:S(2)}) collective-permute-start(f32[24,128]{1,0:T(8,128)S(1)} %add_select_fusion.3), channel_id=1, source_target_pairs={{1,57},{9,1},{17,9},{25,17},{33,25},{41,33},{49,41},{57,49},{3,59}... | collective-permute-start | bytes 36872 | tf_op jit(solution)/shard_map/ppermute | solution.py:55
  52.4 5.7 %collective-permute-start.19 = (f32[24,128]{1,0:T(8,128)S(1)}, f32[24,128]{1,0:T(8,128)S(1)}, u32[]{:S(2)}, u32[]{:S(2)}) collective-permute-start(f32[24,128]{1,0:T(8,128)S(1)} %add_select_fusion.2), channel_id=1, source_target_pairs={{0,4},{2,6},{4,0},{6,2},{1,5},{3,7},{5,1},{7,3},{8,12},{10,14},{12... | collective-permute-start | bytes 36872 | tf_op jit(solution)/shard_map/ppermute | solution.py:57
  55.4 3.8 %collective-permute-start.20 = (f32[24,128]{1,0:T(8,128)S(1)}, f32[24,128]{1,0:T(8,128)S(1)}, u32[]{:S(2)}, u32[]{:S(2)}) collective-permute-start(f32[24,128]{1,0:T(8,128)S(1)} %add_select_fusion.2), channel_id=1, source_target_pairs={{0,2},{2,4},{4,6},{6,0},{1,3},{3,5},{5,7},{7,1},{8,10},{10,12},{12... | collective-permute-start | bytes 36872 | tf_op jit(solution)/shard_map/ppermute | solution.py:57
  55.8 3.4 %collective-permute-start.21 = (f32[24,128]{1,0:T(8,128)S(1)}, f32[24,128]{1,0:T(8,128)S(1)}, u32[]{:S(2)}, u32[]{:S(2)}) collective-permute-start(f32[24,128]{1,0:T(8,128)S(1)} %add_select_fusion.2), channel_id=1, source_target_pairs={{0,6},{2,0},{4,2},{6,4},{1,7},{3,1},{5,3},{7,5},{8,14},{10,8},{12,... | collective-permute-start | bytes 36872 | tf_op jit(solution)/shard_map/ppermute | solution.py:57
  59.3 4.2 %collective-permute-start.22 = (f32[24,128]{1,0:T(8,128)S(1)}, f32[24,128]{1,0:T(8,128)S(1)}, u32[]{:S(2)}, u32[]{:S(2)}) collective-permute-start(f32[24,128]{1,0:T(8,128)S(1)} %add_select_fusion.1), channel_id=1, source_target_pairs={{0,1},{1,0},{2,3},{3,2},{4,5},{5,4},{6,7},{7,6},{8,9},{9,8},{10,11... | collective-permute-start | bytes 36872 | tf_op jit(solution)/shard_map/ppermute | solution.py:58
  66.9 14.3 %copy-start = (f32[128,768]{1,0:T(8,128)S(1)}, f32[128,768]{1,0:T(8,128)}, u32[]{:S(2)}) copy-start(f32[128,768]{1,0:T(8,128)} %param.7) | copy-start | bytes 1179652
  66.9 14.3 %copy-start.1 = (f32[128,768]{1,0:T(8,128)S(1)}, f32[128,768]{1,0:T(8,128)}, u32[]{:S(2)}) copy-start(f32[128,768]{1,0:T(8,128)} %param.8) | copy-start | bytes 1179652
  67.6 14.9 %collective-permute-start.26 = (f32[1,1]{1,0:T(1,128)}, f32[1,1]{1,0:T(1,128)}, u32[]{:S(2)}, u32[]{:S(2)}) collective-permute-start(f32[1,1]{1,0:T(1,128)} %bitcast.25), channel_id=1, source_target_pairs={{0,128},{64,192},{128,0},{192,64},{1,129},{65,193},{129,1},{193,65... | collective-permute-start | bytes 20 | tf_op jit(solution)/shard_map/ppermute | solution.py:157
  68.1 14.3 %collective-permute-start.27 = (f32[1,1]{1,0:T(1,128)}, f32[1,1]{1,0:T(1,128)}, u32[]{:S(2)}, u32[]{:S(2)}) collective-permute-start(f32[1,1]{1,0:T(1,128)} %bitcast.25), channel_id=1, source_target_pairs={{0,64},{64,128},{128,192},{192,0},{1,65},{65,129},{129,193},{193,1... | collective-permute-start | bytes 20 | tf_op jit(solution)/shard_map/ppermute | solution.py:157
  68.6 7.1 %collective-permute-start.23 = (f16[128,768]{1,0:T(8,128)(2,1)S(1)}, f16[128,768]{1,0:T(8,128)(2,1)S(1)}, u32[]{:S(2)}, u32[]{:S(2)}) collective-permute-start(f16[128,768]{1,0:T(8,128)(2,1)S(1)} %get-tuple-element.81), channel_id=1, source_target_pairs={{0,128},{64,192},{128,0},{192,64},{1,129},{65,193},{129,1},{193,65... | collective-permute-start | bytes 589832 | tf_op jit(solution)/shard_map/ppermute | solution.py:149
  70.7 10.4 %collective-permute-start.24 = (f16[128,768]{1,0:T(8,128)(2,1)S(1)}, f16[128,768]{1,0:T(8,128)(2,1)S(1)}, u32[]{:S(2)}, u32[]{:S(2)}) collective-permute-start(f16[128,768]{1,0:T(8,128)(2,1)S(1)} %get-tuple-element.83), channel_id=1, source_target_pairs={{0,64},{64,128},{128,192},{192,0},{1,65},{65,129},{129,193},{193,1... | collective-permute-start | bytes 589832 | tf_op jit(solution)/shard_map/ppermute | solution.py:149
  71.5 9.6 %collective-permute-start.25 = (f16[128,768]{1,0:T(8,128)(2,1)S(1)}, f16[128,768]{1,0:T(8,128)(2,1)S(1)}, u32[]{:S(2)}, u32[]{:S(2)}) collective-permute-start(f16[128,768]{1,0:T(8,128)(2,1)S(1)} %get-tuple-element.82), channel_id=1, source_target_pairs={{0,192},{64,0},{128,64},{192,128},{1,193},{65,1},{129,65},{193,129... | collective-permute-start | bytes 589832 | tf_op jit(solution)/shard_map/ppermute | solution.py:149
  75.7 6.7 %collective-permute-start.28 = (f32[1,1]{1,0:T(1,128)}, f32[1,1]{1,0:T(1,128)}, u32[]{:S(2)}, u32[]{:S(2)}) collective-permute-start(f32[1,1]{1,0:T(1,128)} %bitcast.25), channel_id=1, source_target_pairs={{0,192},{64,0},{128,64},{192,128},{1,193},{65,1},{129,65},{193,129... | collective-permute-start | bytes 20 | tf_op jit(solution)/shard_map/ppermute | solution.py:157
  (1 other events, 14.3 us)

commit v3 on v2

--- a/solution.py
+++ b/solution.py
@@ -20,6 +20,7 @@
 OWN = 128
 HOPS = (1, 2, 3, 0)
 ZERO = np.uint32(0)
+NOTHING = -1e30
 SCALE = 4.0
 
 
@@ -96,14 +97,21 @@
     four = [slot(4, core), slot(4, 1 - core)]
     own_base, x_at, cut, at_first = (z * 8 + y * 2 + core) * OWN, x.astype(jnp.uint32), core.astype(jnp.uint32), core == 0
 
-    targets = lax.dynamic_slice(positive_list.reshape(4, 2048), (x_at, ZERO), (1, 2048))[0] - own_base
-    place = (((targets >> 13) - x + 3) & 3) * OWN + (targets & (OWN - 1))
-    targets = jnp.where((targets & 8191) < OWN, place, -1)
-    late = [lax.dynamic_slice(targets.reshape(16, HALF), (row, ZERO), (1, HALF))[0] for row in four]
+    def places(base):
+        some = lax.dynamic_slice(positive_list.reshape(4, 2048), (x_at, ZERO), (1, 2048))[0] - base
+        place = (((some >> 13) - x + 3) & 3) * OWN + (some & (OWN - 1))
+        return jnp.where((some & 8191) < OWN, place, -1)
+
+    targets, other_targets = places(own_base), places((z * 8 + y * 2 + 1 - core) * OWN)
+    mine, others = three[:2] + four[:1], three[2:] + four[1:]
+    late = [
+        [lax.dynamic_slice(some.reshape(16, HALF), (row, ZERO), (1, HALF))[0] for some in (targets, other_targets)]
+        for row in mine
+    ]
 
     part = lax.ppermute(query_emb, ("z", "c"), OPPOSITE)
-    part, own_at, one, two, three, four, cut, at_first, targets, late = lax.optimization_barrier(
-        (part, own_at, one, two, three, four, cut, at_first, targets, late)
+    part, own_at, one, two, three, four, mine, others, cut, at_first, targets, late = lax.optimization_barrier(
+        (part, own_at, one, two, three, four, mine, others, cut, at_first, targets, late)
     )
     swapped = lax.ppermute(part, "c", SWAP)
     rows = jnp.zeros((16, HALF, width), query_emb.dtype)
@@ -121,18 +129,25 @@
         arrived.append(parts + swapped)
     last = lax.ppermute(parts[0], ("z", "c"), OPPOSITE)
     swapped = lax.ppermute(last, "c", SWAP)
-    for block, row in zip(arrived[0] + arrived[1], two + three):
+    for block, row in zip(arrived[0], two):
         rows = put(rows, block, row)
 
     half = centroids.astype(jnp.bfloat16)
     lists = jnp.concatenate([lax.ppermute(half, "x", turn(4, -hop)) if hop else half for hop in HOPS])
     lists = lax.optimization_barrier(lists)
+    other_lists = lax.ppermute(lists, "c", SWAP)
 
     state, hit = forward(rows.reshape(-1, width), lists, targets)
     at = lax.broadcasted_iota(jnp.uint32, (16, HALF), 0)
-    for i, (block, row) in enumerate(zip((last, swapped), four)):
-        local, more = forward(block, lists, late[i])
-        state, hit = jnp.where(at == row, local, state), hit + more
+    for i, (block, row) in enumerate(zip(arrived[1][:2] + [last], mine)):
+        local, more = forward(block, lists, late[i][0])
+        other_local, other_more = forward(block, other_lists, late[i][1])
+        top = jnp.maximum(local, other_local)
+        local = top + jnp.log(jnp.exp(local - top) + jnp.exp(other_local - top))
+        state, hit = jnp.where(at == row, local, state), hit + more + other_more
+    for row in others:
+        state = jnp.where(at == row, NOTHING, state)
+    for block, row in zip(arrived[1] + [last, swapped], three + four):
         rows = put(rows, block, row)
     state = jnp.concatenate([state, hit, jnp.zeros((7, HALF), jnp.float32)])
     rows = rows.reshape(-1, width)

time: 86.4 us -> 91.6 us (1.060)
  starting transfers between devices: 50.1 us -> 52.8 us
  matrix products: 6.51 us -> 8.04 us
    ppermute x1, starting transfers between devices: 0.4 us -> 4.05 us  [over_lists(): state = join(state, lax.ppermute(state, 'c', SWAP))]
    ppermute x4, starting transfers between devices: 3.75 us -> 0.52 us  [body(): swapped.append(lax.ppermute(parts[i], 'c', SWAP))]
    dot_general x4 -> x8, matrix products: 4.55 us -> 6.08 us  [logits_of(): jnp.einsum('kd,rd->kr', lists, rows, preferred_element_type=jnp.float32)]
    ppermute x4, starting transfers between devices: 8.94 us -> 10.4 us  [body(): parts[i] = lax.ppermute(parts[i], ('z', 'c'), OPPOSITE)]
    ppermute x1, starting transfers between devices: 3.34 us -> 2.41 us  [over_lists(): return join(state, lax.ppermute(state, 'c', SWAP))]
  transfers between devices with their start and end apart: 29 -> 30, of which waited for: 13 -> 11; matrix products, arithmetic and copies ran while one was open for 9% -> 11% of each run, Pallas kernels for 0% -> 0%
where the time goes in v3:
time: 91.6 us; the launch traced here: 91.1 us
  starting transfers between devices  52.8 us (58%)
  waiting for transfers between devices  18.6 us (20%)
  matrix products  8.04 us (9%)
  other arithmetic  5.4 us (6%)
  between operations  4.71 us (5%)
  local copies, waits for them, and re-layouts  1.59 us (2%)
    ppermute x4, starting transfers between devices, body(): parts[i] = lax.ppermute(parts[i], ('z', 'c'), OPPOSITE)  10.4 us
    dot_general x8, matrix products, logits_of(): jnp.einsum('kd,rd->kr', lists, rows, preferred_element_type=jnp.float32)  6.08 us
    ppermute x3, starting transfers between devices, over_lists(): lax.ppermute(state, 'y', turn(4, step))  5.63 us
    ppermute x1, starting transfers between devices, body(): part = lax.ppermute(query_emb, ('z', 'c'), OPPOSITE)  5.58 us
    ppermute x3, starting transfers between devices, body(): lax.ppermute(sent[some], 'x', turn(4, step)).astype(jnp.float32)  5.1 us
    ppermute x3, waiting for transfers between devices, body(): lax.ppermute(half, 'x', turn(4, -hop))  4.84 us
    ppermute x3, starting transfers between devices, body(): lax.ppermute(half, 'x', turn(4, -hop))  4.5 us
    ppermute x3, waiting for transfers between devices, body(): lax.ppermute(sent[some], 'x', turn(4, step)).astype(jnp.float32)  4.34 us
  transfers between devices with their start and end apart: 30, of which 11 were waited for; matrix products, arithmetic and copies ran while one was open for 11% of the time, Pallas kernels for 0%

profile of v3, /device:TPU:1, one launch (start us, length us, event | category | flops | bytes accessed | tf_op | source)
XLA Modules:
  0.0 91.1 jit_solution(2076246208209822189)
XLA Ops:
  0.6 1.1 %convert_element_type.81 = bf16[128,768]{1,0:T(8,128)(2,1)S(1)} convert(f32[128,768]{1,0:T(8,128)} %param.7) | non-fusion elementwise | flops 98304 | bytes 589824 | tf_op jit(solution)/shard_map/convert_element_type | solution.py:135
  1.7 3.4 %collective-permute-start.12 = (bf16[128,768]{1,0:T(8,128)(2,1)S(1)}, bf16[128,768]{1,0:T(8,128)(2,1)S(1)}, u32[]{:S(2)}, u32[]{:S(2)}) collective-permute-start(bf16[128,768]{1,0:T(8,128)(2,1)S(1)} %convert_element_type.81), channel_id=1, source_target_pairs={{0,192},{64,0},{128,64},{192,128},{1,193},{65,1},{129,65},{193,129... | collective-permute-start | bytes 589832 | tf_op jit(solution)/shard_map/ppermute | solution.py:136
  6.2 5.6 %collective-permute-start = (bf16[256,768]{1,0:T(8,128)(2,1)}, bf16[256,768]{1,0:T(8,128)(2,1)S(1)}, u32[]{:S(2)}, u32[]{:S(2)}) collective-permute-start(bf16[256,768]{1,0:T(8,128)(2,1)} %param.5), channel_id=1, source_target_pairs={{0,8},{1,57},{8,16},{9,1},{16,24},{17,9},{24,32},{25,17},{32,40},{... | collective-permute-start | bytes 1179656 | tf_op jit(solution)/shard_map/ppermute | solution.py:112
  12.8 4.8 %collective-permute-done.14 = bf16[128,768]{1,0:T(8,128)(2,1)S(1)} collective-permute-done((bf16[128,768]{1,0:T(8,128)(2,1)S(1)}, bf16[128,768]{1,0:T(8,128)(2,1)S(1)}, u32[]{:S(2)}, u32[]{:S(2)}) %collective-permute-start.14) | collective-permute-done | bytes 196640 | tf_op jit(solution)/shard_map/ppermute | solution.py:136
  18.3 1.3 %collective-permute-start.1 = (bf16[256,768]{1,0:T(8,128)(2,1)S(1)}, bf16[256,768]{1,0:T(8,128)(2,1)S(1)}, u32[]{:S(2)}, u32[]{:S(2)}) collective-permute-start(bf16[256,768]{1,0:T(8,128)(2,1)S(1)} %collective-permute-done), channel_id=1, source_target_pairs={{0,1},{1,0},{2,3},{3,2},{4,5},{5,4},{6,7},{7,6},{8,9},{9,8},{10,11... | collective-permute-start | bytes 1179656 | tf_op jit(solution)/shard_map/ppermute | solution.py:116
  19.6 4.5 %collective-permute-start.2 = (bf16[128,768]{1,0:T(8,128)(2,1)S(1)}, bf16[128,768]{1,0:T(8,128)(2,1)S(1)}, u32[]{:S(2)}, u32[]{:S(2)}) collective-permute-start(bf16[128,768]{1,0:T(8,128)(2,1)S(1)} %get-tuple-element.129), channel_id=1, source_target_pairs={{0,8},{1,57},{8,16},{9,1},{16,24},{17,9},{24,32},{25,17},{32,40},{... | collective-permute-start | bytes 589832 | tf_op jit(solution)/shard_map/ppermute | solution.py:125
  25.3 1.4 %collective-permute-done.2 = bf16[128,768]{1,0:T(8,128)(2,1)S(1)} collective-permute-done((bf16[128,768]{1,0:T(8,128)(2,1)S(1)}, bf16[128,768]{1,0:T(8,128)(2,1)S(1)}, u32[]{:S(2)}, u32[]{:S(2)}) %collective-permute-start.2) | collective-permute-done | bytes 196640 | tf_op jit(solution)/shard_map/ppermute | solution.py:125
  26.7 3.1 %collective-permute-start.6 = (bf16[128,768]{1,0:T(8,128)(2,1)S(1)}, bf16[128,768]{1,0:T(8,128)(2,1)S(1)}, u32[]{:S(2)}, u32[]{:S(2)}) collective-permute-start(bf16[128,768]{1,0:T(8,128)(2,1)S(1)} %collective-permute-done.2), channel_id=1, source_target_pairs={{0,8},{1,57},{8,16},{9,1},{16,24},{17,9},{24,32},{25,17},{32,40},{... | collective-permute-start | bytes 589832 | tf_op jit(solution)/shard_map/ppermute | solution.py:125
  29.8 2.1 %collective-permute-start.7 = (bf16[128,768]{1,0:T(8,128)(2,1)S(1)}, bf16[128,768]{1,0:T(8,128)(2,1)S(1)}, u32[]{:S(2)}, u32[]{:S(2)}) collective-permute-start(bf16[128,768]{1,0:T(8,128)(2,1)S(1)} %collective-permute-done.3), channel_id=1, source_target_pairs={{0,8},{1,57},{8,16},{9,1},{16,24},{17,9},{24,32},{25,17},{32,40},{... | collective-permute-start | bytes 589832 | tf_op jit(solution)/shard_map/ppermute | solution.py:125
  32.0 1.3 %collective-permute-done.5 = bf16[128,768]{1,0:T(8,128)(2,1)S(1)} collective-permute-done((bf16[128,768]{1,0:T(8,128)(2,1)S(1)}, bf16[128,768]{1,0:T(8,128)(2,1)S(1)}, u32[]{:S(2)}, u32[]{:S(2)}) %collective-permute-start.5) | collective-permute-done | bytes 196640 | tf_op jit(solution)/shard_map/ppermute | solution.py:128
  33.4 1.8 %fusion.37 = (f32[2048]{0:T(1024)S(1)}, f32[512,2048]{1,0:T(8,128)S(1)}) fusion(bf16[512,768]{1,0:T(8,128)(2,1)S(1)} %pad_maximum_fusion, bf16[2048,768]{1,0:T(8,128)(2,1)S(1)} %bitcast.82), kind=kOutput, calls=%fused_computation.111 | convolution fusion | flops 1611659264 | bytes 8134656 | tf_op jit(solution)/shard_map/kd,rd->kr/dot_general | solution.py:71
  36.0 2.5 %collective-permute-start.10 = (bf16[128,768]{1,0:T(8,128)(2,1)S(1)}, bf16[128,768]{1,0:T(8,128)(2,1)S(1)}, u32[]{:S(2)}, u32[]{:S(2)}) collective-permute-start(bf16[128,768]{1,0:T(8,128)(2,1)S(1)} %collective-permute-done.6), channel_id=1, source_target_pairs={{0,8},{1,57},{8,16},{9,1},{16,24},{17,9},{24,32},{25,17},{32,40},{... | collective-permute-start | bytes 589832 | tf_op jit(solution)/shard_map/ppermute | solution.py:130
  39.1 1.1 %exponential_reduce_fusion = (f32[2048]{0:T(1024)S(1)}, f32[2048]{0:T(1024)S(1)}) fusion(f32[512,2048]{1,0:T(8,128)S(1)} %get-tuple-element.90, f32[2048]{0:T(1024)S(1)} %get-tuple-element.89, s32[2048]{0:T(1024)S(1)} %bitcast.91), kind=kLoop, calls=%fused_computation.3 | loop fusion | flops 5238784 | bytes 4227072 | tf_op jit(solution)/shard_map/reduce_sum | solution.py:78
  43.3 4.0 %collective-permute-start.16 = (f32[24,128]{1,0:T(8,128)S(1)}, f32[24,128]{1,0:T(8,128)S(1)}, u32[]{:S(2)}, u32[]{:S(2)}) collective-permute-start(f32[24,128]{1,0:T(8,128)S(1)} %maximum_maximum_fusion), channel_id=1, source_target_pairs={{0,1},{1,0},{2,3},{3,2},{4,5},{5,4},{6,7},{7,6},{8,9},{9,8},{10,11... | collective-permute-start | bytes 36872 | tf_op jit(solution)/shard_map/ppermute | solution.py:53
  47.3 0.8 collective-permute-done.16
  48.8 2.1 %collective-permute-done.17 = f32[24,128]{1,0:T(8,128)S(1)} collective-permute-done((f32[24,128]{1,0:T(8,128)S(1)}, f32[24,128]{1,0:T(8,128)S(1)}, u32[]{:S(2)}, u32[]{:S(2)}) %collective-permute-start.17) | collective-permute-done | bytes 12320 | tf_op jit(solution)/shard_map/ppermute | solution.py:54
  50.9 2.9 %collective-permute-start.18 = (f32[24,128]{1,0:T(8,128)S(1)}, f32[24,128]{1,0:T(8,128)S(1)}, u32[]{:S(2)}, u32[]{:S(2)}) collective-permute-start(f32[24,128]{1,0:T(8,128)S(1)} %add_select_fusion.3), channel_id=1, source_target_pairs={{0,16},{1,41},{8,24},{9,49},{16,32},{17,57},{24,40},{25,1},{32,48}... | collective-permute-start | bytes 36872 | tf_op jit(solution)/shard_map/ppermute | solution.py:55
  53.8 3.6 %collective-permute-start.19 = (f32[24,128]{1,0:T(8,128)S(1)}, f32[24,128]{1,0:T(8,128)S(1)}, u32[]{:S(2)}, u32[]{:S(2)}) collective-permute-start(f32[24,128]{1,0:T(8,128)S(1)} %add_select_fusion.3), channel_id=1, source_target_pairs={{1,57},{9,1},{17,9},{25,17},{33,25},{41,33},{49,41},{57,49},{3,59}... | collective-permute-start | bytes 36872 | tf_op jit(solution)/shard_map/ppermute | solution.py:56
  57.5 1.1 %collective-permute-done.19 = f32[24,128]{1,0:T(8,128)S(1)} collective-permute-done((f32[24,128]{1,0:T(8,128)S(1)}, f32[24,128]{1,0:T(8,128)S(1)}, u32[]{:S(2)}, u32[]{:S(2)}) %collective-permute-start.19) | collective-permute-done | bytes 12320 | tf_op jit(solution)/shard_map/ppermute | solution.py:56
  58.6 3.0 %collective-permute-start.20 = (f32[24,128]{1,0:T(8,128)S(1)}, f32[24,128]{1,0:T(8,128)S(1)}, u32[]{:S(2)}, u32[]{:S(2)}) collective-permute-start(f32[24,128]{1,0:T(8,128)S(1)} %add_select_fusion.2), channel_id=1, source_target_pairs={{0,4},{2,6},{4,0},{6,2},{1,5},{3,7},{5,1},{7,3},{8,12},{10,14},{12... | collective-permute-start | bytes 36872 | tf_op jit(solution)/shard_map/ppermute | solution.py:58
  62.0 2.3 %collective-permute-start.22 = (f32[24,128]{1,0:T(8,128)S(1)}, f32[24,128]{1,0:T(8,128)S(1)}, u32[]{:S(2)}, u32[]{:S(2)}) collective-permute-start(f32[24,128]{1,0:T(8,128)S(1)} %add_select_fusion.2), channel_id=1, source_target_pairs={{0,6},{2,0},{4,2},{6,4},{1,7},{3,1},{5,3},{7,5},{8,14},{10,8},{12,... | collective-permute-start | bytes 36872 | tf_op jit(solution)/shard_map/ppermute | solution.py:58
  64.3 1.0 %collective-permute-done.21 = f32[24,128]{1,0:T(8,128)S(1)} collective-permute-done((f32[24,128]{1,0:T(8,128)S(1)}, f32[24,128]{1,0:T(8,128)S(1)}, u32[]{:S(2)}, u32[]{:S(2)}) %collective-permute-start.21) | collective-permute-done | bytes 12320 | tf_op jit(solution)/shard_map/ppermute | solution.py:58
  65.4 2.4 %collective-permute-start.23 = (f32[24,128]{1,0:T(8,128)S(1)}, f32[24,128]{1,0:T(8,128)S(1)}, u32[]{:S(2)}, u32[]{:S(2)}) collective-permute-start(f32[24,128]{1,0:T(8,128)S(1)} %add_select_fusion.1), channel_id=1, source_target_pairs={{0,1},{1,0},{2,3},{3,2},{4,5},{5,4},{6,7},{7,6},{8,9},{9,8},{10,11... | collective-permute-start | bytes 36872 | tf_op jit(solution)/shard_map/ppermute | solution.py:59
  67.9 0.8 collective-permute-done.23
  68.8 2.0 %subtract_convert_fusion = bf16[512,2048]{1,0:T(8,128)(2,1)S(1)} fusion(bf16[512,768]{1,0:T(8,128)(2,1)S(1)} %pad_maximum_fusion, bf16[2048,768]{1,0:T(8,128)(2,1)S(1)} %bitcast.83, f32[2048]{0:T(1024)S(1)} %slice_bitcast_fusion, s32[2048]{0:T(1024)S(1)} %bitcast.92), kind=kOutput, calls=%fused_computation | convolution fusion | flops 1615855616 | bytes 6045696 | tf_op jit(solution)/shard_map/kd,rd->kr/dot_general | solution.py:71
  70.7 1.4 %fusion.5 = f16[384,768]{1,0:T(8,128)(2,1)S(1)} fusion(bf16[2048,768]{1,0:T(8,128)(2,1)S(1)} %bitcast.84, bf16[512,2048]{1,0:T(8,128)(2,1)S(1)} %subtract_convert_fusion), kind=kOutput, calls=%fused_computation.7 | convolution fusion | flops 1208549376 | bytes 5308416 | tf_op jit(solution)/shard_map/dot_general | solution.py:160
  73.8 2.4 %collective-permute-start.24 = (f16[128,768]{1,0:T(8,128)(2,1)S(1)}, f16[128,768]{1,0:T(8,128)(2,1)S(1)}, u32[]{:S(2)}, u32[]{:S(2)}) collective-permute-start(f16[128,768]{1,0:T(8,128)(2,1)S(1)} %get-tuple-element.125), channel_id=1, source_target_pairs={{0,128},{64,192},{128,0},{192,64},{1,129},{65,193},{129,1},{193,65... | collective-permute-start | bytes 589832 | tf_op jit(solution)/shard_map/ppermute | solution.py:164
  76.8 2.1 %collective-permute-start.26 = (f16[128,768]{1,0:T(8,128)(2,1)S(1)}, f16[128,768]{1,0:T(8,128)(2,1)S(1)}, u32[]{:S(2)}, u32[]{:S(2)}) collective-permute-start(f16[128,768]{1,0:T(8,128)(2,1)S(1)} %get-tuple-element.126), channel_id=1, source_target_pairs={{0,192},{64,0},{128,64},{192,128},{1,193},{65,1},{129,65},{193,129... | collective-permute-start | bytes 589832 | tf_op jit(solution)/shard_map/ppermute | solution.py:164
  79.5 1.5 %collective-permute-done.24 = f16[128,768]{1,0:T(8,128)(2,1)S(1)} collective-permute-done((f16[128,768]{1,0:T(8,128)(2,1)S(1)}, f16[128,768]{1,0:T(8,128)(2,1)S(1)}, u32[]{:S(2)}, u32[]{:S(2)}) %collective-permute-start.24) | collective-permute-done | bytes 196640 | tf_op jit(solution)/shard_map/ppermute | solution.py:164
  81.0 2.3 %collective-permute-start.29 = (f32[1,1]{1,0:T(1,128)}, f32[1,1]{1,0:T(1,128)}, u32[]{:S(2)}, u32[]{:S(2)}) collective-permute-start(f32[1,1]{1,0:T(1,128)} %bitcast.30), channel_id=1, source_target_pairs={{0,192},{64,0},{128,64},{192,128},{1,193},{65,1},{129,65},{193,129... | collective-permute-start | bytes 20 | tf_op jit(solution)/shard_map/ppermute | solution.py:172
  83.3 2.9 %collective-permute-done.25 = f16[128,768]{1,0:T(8,128)(2,1)S(1)} collective-permute-done((f16[128,768]{1,0:T(8,128)(2,1)S(1)}, f16[128,768]{1,0:T(8,128)(2,1)S(1)}, u32[]{:S(2)}, u32[]{:S(2)}) %collective-permute-start.25) | collective-permute-done | bytes 196640 | tf_op jit(solution)/shard_map/ppermute | solution.py:164
  86.2 1.2 %divide_subtract_fusion = (f32[128,768]{1,0:T(8,128)}, f32[128,768]{1,0:T(8,128)}, f32[128,768]{1,0:T(8,128)}) fusion(f32[128,768]{1,0:T(8,128)S(1)} %copy-done, f32[128,768]{1,0:T(8,128)S(1)} %fusion.8, f16[128,768]{1,0:T(8,128)(2,1)S(1)} %collective-permute-done.26, f16[128,768]{1,0:T(8,128)(2,1)S(1)} %collective-permute-done.25, ...), kind=kLoop, calls=%fused_computation.13 | loop fusion | flops 1769472 | bytes 3342336 | tf_op jit(solution)/shard_map/sub | solution.py:42
  (98 shorter events, 12.6 us)
Async XLA Ops:
  0.6 24.5 %copy-start.3 = (bf16[256,768]{1,0:T(8,128)(2,1)S(1)}, bf16[256,768]{1,0:T(8,128)(2,1)}, u32[]{:S(2)}) copy-start(bf16[256,768]{1,0:T(8,128)(2,1)} %param.5) | copy-start | bytes 1179652
  1.7 11.1 %collective-permute-start.12 = (bf16[128,768]{1,0:T(8,128)(2,1)S(1)}, bf16[128,768]{1,0:T(8,128)(2,1)S(1)}, u32[]{:S(2)}, u32[]{:S(2)}) collective-permute-start(bf16[128,768]{1,0:T(8,128)(2,1)S(1)} %convert_element_type.81), channel_id=1, source_target_pairs={{0,192},{64,0},{128,64},{192,128},{1,193},{65,1},{129,65},{193,129... | collective-permute-start | bytes 589832 | tf_op jit(solution)/shard_map/ppermute | solution.py:136
  5.1 7.7 %collective-permute-start.13 = (bf16[128,768]{1,0:T(8,128)(2,1)S(1)}, bf16[128,768]{1,0:T(8,128)(2,1)S(1)}, u32[]{:S(2)}, u32[]{:S(2)}) collective-permute-start(bf16[128,768]{1,0:T(8,128)(2,1)S(1)} %convert_element_type.81), channel_id=1, source_target_pairs={{0,128},{64,192},{128,0},{192,64},{1,129},{65,193},{129,1},{193,65... | collective-permute-start | bytes 589832 | tf_op jit(solution)/shard_map/ppermute | solution.py:136
  5.6 12.0 %collective-permute-start.14 = (bf16[128,768]{1,0:T(8,128)(2,1)S(1)}, bf16[128,768]{1,0:T(8,128)(2,1)S(1)}, u32[]{:S(2)}, u32[]{:S(2)}) collective-permute-start(bf16[128,768]{1,0:T(8,128)(2,1)S(1)} %convert_element_type.81), channel_id=1, source_target_pairs={{0,64},{64,128},{128,192},{192,0},{1,65},{65,129},{129,193},{193,1... | collective-permute-start | bytes 589832 | tf_op jit(solution)/shard_map/ppermute | solution.py:136
  6.2 12.1 %collective-permute-start = (bf16[256,768]{1,0:T(8,128)(2,1)}, bf16[256,768]{1,0:T(8,128)(2,1)S(1)}, u32[]{:S(2)}, u32[]{:S(2)}) collective-permute-start(bf16[256,768]{1,0:T(8,128)(2,1)} %param.5), channel_id=1, source_target_pairs={{0,8},{1,57},{8,16},{9,1},{16,24},{17,9},{24,32},{25,17},{32,40},{... | collective-permute-start | bytes 1179656 | tf_op jit(solution)/shard_map/ppermute | solution.py:112
  17.7 23.4 %collective-permute-start.15 = (bf16[512,768]{1,0:T(8,128)(2,1)S(1)}, bf16[512,768]{1,0:T(8,128)(2,1)S(1)}, u32[]{:S(2)}, u32[]{:S(2)}) collective-permute-start(bf16[512,768]{1,0:T(8,128)(2,1)S(1)} %pad_maximum_fusion), channel_id=1, source_target_pairs={{0,1},{1,0},{2,3},{3,2},{4,5},{5,4},{6,7},{7,6},{8,9},{9,8},{10,11... | collective-permute-start | bytes 2359304 | tf_op jit(solution)/shard_map/ppermute | solution.py:138
  18.3 13.6 %collective-permute-start.1 = (bf16[256,768]{1,0:T(8,128)(2,1)S(1)}, bf16[256,768]{1,0:T(8,128)(2,1)S(1)}, u32[]{:S(2)}, u32[]{:S(2)}) collective-permute-start(bf16[256,768]{1,0:T(8,128)(2,1)S(1)} %collective-permute-done), channel_id=1, source_target_pairs={{0,1},{1,0},{2,3},{3,2},{4,5},{5,4},{6,7},{7,6},{8,9},{9,8},{10,11... | collective-permute-start | bytes 1179656 | tf_op jit(solution)/shard_map/ppermute | solution.py:116
  19.6 7.1 %collective-permute-start.2 = (bf16[128,768]{1,0:T(8,128)(2,1)S(1)}, bf16[128,768]{1,0:T(8,128)(2,1)S(1)}, u32[]{:S(2)}, u32[]{:S(2)}) collective-permute-start(bf16[128,768]{1,0:T(8,128)(2,1)S(1)} %get-tuple-element.129), channel_id=1, source_target_pairs={{0,8},{1,57},{8,16},{9,1},{16,24},{17,9},{24,32},{25,17},{32,40},{... | collective-permute-start | bytes 589832 | tf_op jit(solution)/shard_map/ppermute | solution.py:125
  24.1 5.7 %collective-permute-start.3 = (bf16[128,768]{1,0:T(8,128)(2,1)S(1)}, bf16[128,768]{1,0:T(8,128)(2,1)S(1)}, u32[]{:S(2)}, u32[]{:S(2)}) collective-permute-start(bf16[128,768]{1,0:T(8,128)(2,1)S(1)} %get-tuple-element.128), channel_id=1, source_target_pairs={{0,8},{1,57},{8,16},{9,1},{16,24},{17,9},{24,32},{25,17},{32,40},{... | collective-permute-start | bytes 589832 | tf_op jit(solution)/shard_map/ppermute | solution.py:125
  26.7 8.9 %collective-permute-start.6 = (bf16[128,768]{1,0:T(8,128)(2,1)S(1)}, bf16[128,768]{1,0:T(8,128)(2,1)S(1)}, u32[]{:S(2)}, u32[]{:S(2)}) collective-permute-start(bf16[128,768]{1,0:T(8,128)(2,1)S(1)} %collective-permute-done.2), channel_id=1, source_target_pairs={{0,8},{1,57},{8,16},{9,1},{16,24},{17,9},{24,32},{25,17},{32,40},{... | collective-permute-start | bytes 589832 | tf_op jit(solution)/shard_map/ppermute | solution.py:125
  29.8 2.2 %collective-permute-start.4 = (bf16[128,768]{1,0:T(8,128)(2,1)S(1)}, bf16[128,768]{1,0:T(8,128)(2,1)S(1)}, u32[]{:S(2)}, u32[]{:S(2)}) collective-permute-start(bf16[128,768]{1,0:T(8,128)(2,1)S(1)} %collective-permute-done.2), channel_id=1, source_target_pairs={{0,1},{1,0},{2,3},{3,2},{4,5},{5,4},{6,7},{7,6},{8,9},{9,8},{10,11... | collective-permute-start | bytes 589832 | tf_op jit(solution)/shard_map/ppermute | solution.py:128
  29.8 5.4 %collective-permute-start.7 = (bf16[128,768]{1,0:T(8,128)(2,1)S(1)}, bf16[128,768]{1,0:T(8,128)(2,1)S(1)}, u32[]{:S(2)}, u32[]{:S(2)}) collective-permute-start(bf16[128,768]{1,0:T(8,128)(2,1)S(1)} %collective-permute-done.3), channel_id=1, source_target_pairs={{0,8},{1,57},{8,16},{9,1},{16,24},{17,9},{24,32},{25,17},{32,40},{... | collective-permute-start | bytes 589832 | tf_op jit(solution)/shard_map/ppermute | solution.py:125
  31.9 1.4 %collective-permute-start.5 = (bf16[128,768]{1,0:T(8,128)(2,1)S(1)}, bf16[128,768]{1,0:T(8,128)(2,1)S(1)}, u32[]{:S(2)}, u32[]{:S(2)}) collective-permute-start(bf16[128,768]{1,0:T(8,128)(2,1)S(1)} %collective-permute-done.3), channel_id=1, source_target_pairs={{0,1},{1,0},{2,3},{3,2},{4,5},{5,4},{6,7},{7,6},{8,9},{9,8},{10,11... | collective-permute-start | bytes 589832 | tf_op jit(solution)/shard_map/ppermute | solution.py:128
  36.0 5.1 %collective-permute-start.10 = (bf16[128,768]{1,0:T(8,128)(2,1)S(1)}, bf16[128,768]{1,0:T(8,128)(2,1)S(1)}, u32[]{:S(2)}, u32[]{:S(2)}) collective-permute-start(bf16[128,768]{1,0:T(8,128)(2,1)S(1)} %collective-permute-done.6), channel_id=1, source_target_pairs={{0,8},{1,57},{8,16},{9,1},{16,24},{17,9},{24,32},{25,17},{32,40},{... | collective-permute-start | bytes 589832 | tf_op jit(solution)/shard_map/ppermute | solution.py:130
  38.5 19.0 %collective-permute-start.8 = (bf16[128,768]{1,0:T(8,128)(2,1)S(1)}, bf16[128,768]{1,0:T(8,128)(2,1)S(1)}, u32[]{:S(2)}, u32[]{:S(2)}) collective-permute-start(bf16[128,768]{1,0:T(8,128)(2,1)S(1)} %collective-permute-done.6), channel_id=1, source_target_pairs={{0,1},{1,0},{2,3},{3,2},{4,5},{5,4},{6,7},{7,6},{8,9},{9,8},{10,11... | collective-permute-start | bytes 589832 | tf_op jit(solution)/shard_map/ppermute | solution.py:128
  38.5 25.8 %collective-permute-start.9 = (bf16[128,768]{1,0:T(8,128)(2,1)S(1)}, bf16[128,768]{1,0:T(8,128)(2,1)S(1)}, u32[]{:S(2)}, u32[]{:S(2)}) collective-permute-start(bf16[128,768]{1,0:T(8,128)(2,1)S(1)} %collective-permute-done.7), channel_id=1, source_target_pairs={{0,1},{1,0},{2,3},{3,2},{4,5},{5,4},{6,7},{7,6},{8,9},{9,8},{10,11... | collective-permute-start | bytes 589832 | tf_op jit(solution)/shard_map/ppermute | solution.py:128
  43.3 4.9 %collective-permute-start.16 = (f32[24,128]{1,0:T(8,128)S(1)}, f32[24,128]{1,0:T(8,128)S(1)}, u32[]{:S(2)}, u32[]{:S(2)}) collective-permute-start(f32[24,128]{1,0:T(8,128)S(1)} %maximum_maximum_fusion), channel_id=1, source_target_pairs={{0,1},{1,0},{2,3},{3,2},{4,5},{5,4},{6,7},{7,6},{8,9},{9,8},{10,11... | collective-permute-start | bytes 36872 | tf_op jit(solution)/shard_map/ppermute | solution.py:53
  48.2 2.6 %collective-permute-start.17 = (f32[24,128]{1,0:T(8,128)S(1)}, f32[24,128]{1,0:T(8,128)S(1)}, u32[]{:S(2)}, u32[]{:S(2)}) collective-permute-start(f32[24,128]{1,0:T(8,128)S(1)} %add_select_fusion.4), channel_id=1, source_target_pairs={{0,8},{1,57},{8,16},{9,1},{16,24},{17,9},{24,32},{25,17},{32,40},{... | collective-permute-start | bytes 36872 | tf_op jit(solution)/shard_map/ppermute | solution.py:54
  48.4 20.4 %collective-permute-start.11 = (bf16[128,768]{1,0:T(8,128)(2,1)S(1)}, bf16[128,768]{1,0:T(8,128)(2,1)S(1)}, u32[]{:S(2)}, u32[]{:S(2)}) collective-permute-start(bf16[128,768]{1,0:T(8,128)(2,1)S(1)} %collective-permute-done.10), channel_id=1, source_target_pairs={{0,1},{1,0},{2,3},{3,2},{4,5},{5,4},{6,7},{7,6},{8,9},{9,8},{10,11... | collective-permute-start | bytes 589832 | tf_op jit(solution)/shard_map/ppermute | solution.py:131
  50.9 6.6 %collective-permute-start.18 = (f32[24,128]{1,0:T(8,128)S(1)}, f32[24,128]{1,0:T(8,128)S(1)}, u32[]{:S(2)}, u32[]{:S(2)}) collective-permute-start(f32[24,128]{1,0:T(8,128)S(1)} %add_select_fusion.3), channel_id=1, source_target_pairs={{0,16},{1,41},{8,24},{9,49},{16,32},{17,57},{24,40},{25,1},{32,48}... | collective-permute-start | bytes 36872 | tf_op jit(solution)/shard_map/ppermute | solution.py:55
  53.8 4.7 %collective-permute-start.19 = (f32[24,128]{1,0:T(8,128)S(1)}, f32[24,128]{1,0:T(8,128)S(1)}, u32[]{:S(2)}, u32[]{:S(2)}) collective-permute-start(f32[24,128]{1,0:T(8,128)S(1)} %add_select_fusion.3), channel_id=1, source_target_pairs={{1,57},{9,1},{17,9},{25,17},{33,25},{41,33},{49,41},{57,49},{3,59}... | collective-permute-start | bytes 36872 | tf_op jit(solution)/shard_map/ppermute | solution.py:56
  58.6 5.7 %collective-permute-start.20 = (f32[24,128]{1,0:T(8,128)S(1)}, f32[24,128]{1,0:T(8,128)S(1)}, u32[]{:S(2)}, u32[]{:S(2)}) collective-permute-start(f32[24,128]{1,0:T(8,128)S(1)} %add_select_fusion.2), channel_id=1, source_target_pairs={{0,4},{2,6},{4,0},{6,2},{1,5},{3,7},{5,1},{7,3},{8,12},{10,14},{12... | collective-permute-start | bytes 36872 | tf_op jit(solution)/shard_map/ppermute | solution.py:58
  61.6 3.8 %collective-permute-start.21 = (f32[24,128]{1,0:T(8,128)S(1)}, f32[24,128]{1,0:T(8,128)S(1)}, u32[]{:S(2)}, u32[]{:S(2)}) collective-permute-start(f32[24,128]{1,0:T(8,128)S(1)} %add_select_fusion.2), channel_id=1, source_target_pairs={{0,2},{2,4},{4,6},{6,0},{1,3},{3,5},{5,7},{7,1},{8,10},{10,12},{12... | collective-permute-start | bytes 36872 | tf_op jit(solution)/shard_map/ppermute | solution.py:58
  62.0 3.4 %collective-permute-start.22 = (f32[24,128]{1,0:T(8,128)S(1)}, f32[24,128]{1,0:T(8,128)S(1)}, u32[]{:S(2)}, u32[]{:S(2)}) collective-permute-start(f32[24,128]{1,0:T(8,128)S(1)} %add_select_fusion.2), channel_id=1, source_target_pairs={{0,6},{2,0},{4,2},{6,4},{1,7},{3,1},{5,3},{7,5},{8,14},{10,8},{12,... | collective-permute-start | bytes 36872 | tf_op jit(solution)/shard_map/ppermute | solution.py:58
  65.4 3.2 %collective-permute-start.23 = (f32[24,128]{1,0:T(8,128)S(1)}, f32[24,128]{1,0:T(8,128)S(1)}, u32[]{:S(2)}, u32[]{:S(2)}) collective-permute-start(f32[24,128]{1,0:T(8,128)S(1)} %add_select_fusion.1), channel_id=1, source_target_pairs={{0,1},{1,0},{2,3},{3,2},{4,5},{5,4},{6,7},{7,6},{8,9},{9,8},{10,11... | collective-permute-start | bytes 36872 | tf_op jit(solution)/shard_map/ppermute | solution.py:59
  72.1 14.0 %copy-start = (f32[128,768]{1,0:T(8,128)S(1)}, f32[128,768]{1,0:T(8,128)}, u32[]{:S(2)}) copy-start(f32[128,768]{1,0:T(8,128)} %param.7) | copy-start | bytes 1179652
  72.8 14.6 %collective-permute-start.27 = (f32[1,1]{1,0:T(1,128)}, f32[1,1]{1,0:T(1,128)}, u32[]{:S(2)}, u32[]{:S(2)}) collective-permute-start(f32[1,1]{1,0:T(1,128)} %bitcast.30), channel_id=1, source_target_pairs={{0,128},{64,192},{128,0},{192,64},{1,129},{65,193},{129,1},{193,65... | collective-permute-start | bytes 20 | tf_op jit(solution)/shard_map/ppermute | solution.py:172
  73.4 14.1 %collective-permute-start.28 = (f32[1,1]{1,0:T(1,128)}, f32[1,1]{1,0:T(1,128)}, u32[]{:S(2)}, u32[]{:S(2)}) collective-permute-start(f32[1,1]{1,0:T(1,128)} %bitcast.30), channel_id=1, source_target_pairs={{0,64},{64,128},{128,192},{192,0},{1,65},{65,129},{129,193},{193,1... | collective-permute-start | bytes 20 | tf_op jit(solution)/shard_map/ppermute | solution.py:172
  73.8 7.2 %collective-permute-start.24 = (f16[128,768]{1,0:T(8,128)(2,1)S(1)}, f16[128,768]{1,0:T(8,128)(2,1)S(1)}, u32[]{:S(2)}, u32[]{:S(2)}) collective-permute-start(f16[128,768]{1,0:T(8,128)(2,1)S(1)} %get-tuple-element.125), channel_id=1, source_target_pairs={{0,128},{64,192},{128,0},{192,64},{1,129},{65,193},{129,1},{193,65... | collective-permute-start | bytes 589832 | tf_op jit(solution)/shard_map/ppermute | solution.py:164
  76.3 9.9 %collective-permute-start.25 = (f16[128,768]{1,0:T(8,128)(2,1)S(1)}, f16[128,768]{1,0:T(8,128)(2,1)S(1)}, u32[]{:S(2)}, u32[]{:S(2)}) collective-permute-start(f16[128,768]{1,0:T(8,128)(2,1)S(1)} %get-tuple-element.127), channel_id=1, source_target_pairs={{0,64},{64,128},{128,192},{192,0},{1,65},{65,129},{129,193},{193,1... | collective-permute-start | bytes 589832 | tf_op jit(solution)/shard_map/ppermute | solution.py:164
  76.8 9.4 %collective-permute-start.26 = (f16[128,768]{1,0:T(8,128)(2,1)S(1)}, f16[128,768]{1,0:T(8,128)(2,1)S(1)}, u32[]{:S(2)}, u32[]{:S(2)}) collective-permute-start(f16[128,768]{1,0:T(8,128)(2,1)S(1)} %get-tuple-element.126), channel_id=1, source_target_pairs={{0,192},{64,0},{128,64},{192,128},{1,193},{65,1},{129,65},{193,129... | collective-permute-start | bytes 589832 | tf_op jit(solution)/shard_map/ppermute | solution.py:164
  81.0 6.4 %collective-permute-start.29 = (f32[1,1]{1,0:T(1,128)}, f32[1,1]{1,0:T(1,128)}, u32[]{:S(2)}, u32[]{:S(2)}) collective-permute-start(f32[1,1]{1,0:T(1,128)} %bitcast.30), channel_id=1, source_target_pairs={{0,192},{64,0},{128,64},{192,128},{1,193},{65,1},{129,65},{193,129... | collective-permute-start | bytes 20 | tf_op jit(solution)/shard_map/ppermute | solution.py:172
  (2 other events, 28.1 us)

commit v4 on v3

--- a/solution.py
+++ b/solution.py
@@ -92,8 +92,10 @@
     def slot(step, half):
         return ((((z + sign * step) & 7) * 2) + half).astype(jnp.uint32)
 
-    own_at, one = slot(0, 0), [slot(-1, 0), slot(1, 0)]
-    two, three = [[slot(step, half) for step, half in ((-k, core), (-k, 1 - core), (k, 1 - core), (k, core))] for k in (2, 3)]
+    own_at = slot(0, 0)
+    one, two, three = [
+        [slot(step, half) for step, half in ((-k, core), (-k, 1 - core), (k, 1 - core), (k, core))] for k in (1, 2, 3)
+    ]
     four = [slot(4, core), slot(4, 1 - core)]
     own_base, x_at, cut, at_first = (z * 8 + y * 2 + core) * OWN, x.astype(jnp.uint32), core.astype(jnp.uint32), core == 0
 
@@ -109,16 +111,19 @@
         for row in mine
     ]
 
-    part = lax.ppermute(query_emb, ("z", "c"), OPPOSITE)
-    part, own_at, one, two, three, four, mine, others, cut, at_first, targets, late = lax.optimization_barrier(
-        (part, own_at, one, two, three, four, mine, others, cut, at_first, targets, late)
+    parts = [lax.dynamic_slice(query_emb.reshape(2, HALF, width), (at, ZERO, ZERO), (1, HALF, width))[0] for at in (cut, 1 - cut)]
+    for i in range(2):
+        parts[i] = lax.ppermute(parts[i], ("z", "c"), OPPOSITE)
+    parts[0], own_at, one, two, three, four, mine, others, at_first = lax.optimization_barrier(
+        (parts[0], own_at, one, two, three, four, mine, others, at_first)
     )
-    swapped = lax.ppermute(part, "c", SWAP)
+    swapped = []
+    for i in range(2):
+        swapped.append(lax.ppermute(parts[i], "c", SWAP))
     rows = jnp.zeros((16, HALF, width), query_emb.dtype)
-    for block, row in zip((query_emb, part, swapped), [own_at] + one):
+    rows = put(rows, query_emb, own_at)
+    for block, row in zip(parts + swapped, one):
         rows = put(rows, block, row)
-    part = part.reshape(2, HALF, width)
-    parts = [lax.dynamic_slice(part, (at, ZERO, ZERO), (1, HALF, width))[0] for at in (cut, 1 - cut)]
     arrived = []
     for _ in range(2):
         for i in range(2):
@@ -133,7 +138,10 @@
         rows = put(rows, block, row)
 
     half = centroids.astype(jnp.bfloat16)
-    lists = jnp.concatenate([lax.ppermute(half, "x", turn(4, -hop)) if hop else half for hop in HOPS])
+    lists = []
+    for hop in HOPS[:3]:
+        lists.append(lax.ppermute(half, "x", turn(4, -hop)))
+    lists = jnp.concatenate(lists + [half])
     lists = lax.optimization_barrier(lists)
     other_lists = lax.ppermute(lists, "c", SWAP)
 

time: 91.6 us -> 90.9 us (level)
  waiting for transfers between devices: 18.6 us -> 15.2 us
  starting transfers between devices: 52.8 us -> 54.7 us
  local copies, waits for them, and re-layouts: 1.59 us -> 2.62 us
    ppermute x5 -> x3, starting transfers between devices: 11.4 us -> 4.5 us  [body(): lists.append(lax.ppermute(half, 'x', turn(4, -hop)))]
    ppermute x4 -> x6, starting transfers between devices: 0.52 us -> 6.42 us  [body(): swapped.append(lax.ppermute(parts[i], 'c', SWAP))]
    ppermute x5 -> x3, waiting for transfers between devices: 4.85 us -> 0.01 us  [body(): lists.append(lax.ppermute(half, 'x', turn(4, -hop)))]
    ppermute x4 -> x6, starting transfers between devices: 10.4 us -> 13.9 us  [body(): parts[i] = lax.ppermute(parts[i], ('z', 'c'), OPPOSITE)]
    ppermute x4 -> x6, waiting for transfers between devices: 1.32 us -> 0.02 us  [body(): swapped.append(lax.ppermute(parts[i], 'c', SWAP))]
    ppermute x1, waiting for transfers between devices: 0.8 us -> 1.99 us  [body(): last = lax.ppermute(parts[0], ('z', 'c'), OPPOSITE)]
    squeeze x2 -> x1, local copies, waits for them, and re-layouts: 0.04 us -> 1.05 us  [body(): lax.dynamic_slice(query_emb.reshape(2, HALF, width), (at, ZERO, ZERO), (1...]
    ppermute x4 -> x6, waiting for transfers between devices: 1.43 us -> 2.16 us  [body(): parts[i] = lax.ppermute(parts[i], ('z', 'c'), OPPOSITE)]
  transfers between devices with their start and end apart: 30 -> 32, of which waited for: 11 -> 10; matrix products, arithmetic and copies ran while one was open for 11% -> 12% of each run, Pallas kernels for 0% -> 0%
where the time goes in v4:
time: 90.9 us; the launch traced here: 90.6 us
  starting transfers between devices  54.7 us (60%)
  waiting for transfers between devices  15.2 us (17%)
  matrix products  8.03 us (9%)
  other arithmetic  5.4 us (6%)
  between operations  4.72 us (5%)
  local copies, waits for them, and re-layouts  2.62 us (3%)
    ppermute x6, starting transfers between devices, body(): parts[i] = lax.ppermute(parts[i], ('z', 'c'), OPPOSITE)  13.9 us
    ppermute x6, starting transfers between devices, body(): swapped.append(lax.ppermute(parts[i], 'c', SWAP))  6.42 us
    dot_general x8, matrix products, logits_of(): jnp.einsum('kd,rd->kr', lists, rows, preferred_element_type=jnp.float32)  6.07 us
    ppermute x3, starting transfers between devices, over_lists(): lax.ppermute(state, 'y', turn(4, step))  5.63 us
    ppermute x3, starting transfers between devices, body(): lax.ppermute(sent[some], 'x', turn(4, step)).astype(jnp.float32)  5.21 us
    ppermute x3, waiting for transfers between devices, body(): lax.ppermute(sent[some], 'x', turn(4, step)).astype(jnp.float32)  4.88 us
    ppermute x3, starting transfers between devices, body(): lists.append(lax.ppermute(half, 'x', turn(4, -hop)))  4.5 us
    ppermute x1, starting transfers between devices, over_lists(): state = join(state, lax.ppermute(state, 'c', SWAP))  3.71 us
  transfers between devices with their start and end apart: 32, of which 10 were waited for; matrix products, arithmetic and copies ran while one was open for 12% of the time, Pallas kernels for 0%

profile of v4, /device:TPU:1, one launch (start us, length us, event | category | flops | bytes accessed | tf_op | source)
XLA Modules:
  0.0 90.6 jit_solution(3658872676154224893)
XLA Ops:
  0.6 1.1 %convert_element_type.88 = bf16[128,768]{1,0:T(8,128)(2,1)S(1)} convert(f32[128,768]{1,0:T(8,128)} %param.7) | non-fusion elementwise | flops 98304 | bytes 589824 | tf_op jit(solution)/shard_map/convert_element_type | solution.py:140
  1.7 3.4 %collective-permute-start.14 = (bf16[128,768]{1,0:T(8,128)(2,1)S(1)}, bf16[128,768]{1,0:T(8,128)(2,1)S(1)}, u32[]{:S(2)}, u32[]{:S(2)}) collective-permute-start(bf16[128,768]{1,0:T(8,128)(2,1)S(1)} %convert_element_type.88), channel_id=1, source_target_pairs={{0,192},{64,0},{128,64},{192,128},{1,193},{65,1},{129,65},{193,129... | collective-permute-start | bytes 589832 | tf_op jit(solution)/shard_map/ppermute | solution.py:143
  6.2 1.0 %dynamic-slice_bitcast_fusion = (bf16[128,768]{1,0:T(8,128)(2,1)S(1)}, bf16[128,768]{1,0:T(8,128)(2,1)S(1)}) fusion(bf16[2,128,768]{2,1,0:T(8,128)(2,1)} %bitcast.92, u32[]{:T(128)S(6)} %sub.182, u32[]{:T(128)S(6)} %convert_element_type.72), kind=kLoop, calls=%fused_computation.48 | loop fusion | bytes 786440 | tf_op jit(solution)/shard_map/squeeze | solution.py:114
  7.3 5.7 %collective-permute-start = (bf16[128,768]{1,0:T(8,128)(2,1)S(1)}, bf16[128,768]{1,0:T(8,128)(2,1)S(1)}, u32[]{:S(2)}, u32[]{:S(2)}) collective-permute-start(bf16[128,768]{1,0:T(8,128)(2,1)S(1)} %get-tuple-element.117), channel_id=1, source_target_pairs={{0,8},{1,57},{8,16},{9,1},{16,24},{17,9},{24,32},{25,17},{32,40},{... | collective-permute-start | bytes 589832 | tf_op jit(solution)/shard_map/ppermute | solution.py:116
  15.5 2.8 %collective-permute-start.2 = (bf16[128,768]{1,0:T(8,128)(2,1)S(1)}, bf16[128,768]{1,0:T(8,128)(2,1)S(1)}, u32[]{:S(2)}, u32[]{:S(2)}) collective-permute-start(bf16[128,768]{1,0:T(8,128)(2,1)S(1)} %collective-permute-done), channel_id=1, source_target_pairs={{0,1},{1,0},{2,3},{3,2},{4,5},{5,4},{6,7},{7,6},{8,9},{9,8},{10,11... | collective-permute-start | bytes 589832 | tf_op jit(solution)/shard_map/ppermute | solution.py:122
  18.4 1.7 %collective-permute-start.4 = (bf16[128,768]{1,0:T(8,128)(2,1)S(1)}, bf16[128,768]{1,0:T(8,128)(2,1)S(1)}, u32[]{:S(2)}, u32[]{:S(2)}) collective-permute-start(bf16[128,768]{1,0:T(8,128)(2,1)S(1)} %collective-permute-done), channel_id=1, source_target_pairs={{0,8},{1,57},{8,16},{9,1},{16,24},{17,9},{24,32},{25,17},{32,40},{... | collective-permute-start | bytes 589832 | tf_op jit(solution)/shard_map/ppermute | solution.py:130
  21.3 3.2 %collective-permute-start.5 = (bf16[128,768]{1,0:T(8,128)(2,1)S(1)}, bf16[128,768]{1,0:T(8,128)(2,1)S(1)}, u32[]{:S(2)}, u32[]{:S(2)}) collective-permute-start(bf16[128,768]{1,0:T(8,128)(2,1)S(1)} %collective-permute-done.1), channel_id=1, source_target_pairs={{0,8},{1,57},{8,16},{9,1},{16,24},{17,9},{24,32},{25,17},{32,40},{... | collective-permute-start | bytes 589832 | tf_op jit(solution)/shard_map/ppermute | solution.py:130
  25.8 1.2 %collective-permute-done.5 = bf16[128,768]{1,0:T(8,128)(2,1)S(1)} collective-permute-done((bf16[128,768]{1,0:T(8,128)(2,1)S(1)}, bf16[128,768]{1,0:T(8,128)(2,1)S(1)}, u32[]{:S(2)}, u32[]{:S(2)}) %collective-permute-start.5) | collective-permute-done | bytes 196640 | tf_op jit(solution)/shard_map/ppermute | solution.py:130
  27.1 1.7 %collective-permute-start.7 = (bf16[128,768]{1,0:T(8,128)(2,1)S(1)}, bf16[128,768]{1,0:T(8,128)(2,1)S(1)}, u32[]{:S(2)}, u32[]{:S(2)}) collective-permute-start(bf16[128,768]{1,0:T(8,128)(2,1)S(1)} %collective-permute-done.5), channel_id=1, source_target_pairs={{0,1},{1,0},{2,3},{3,2},{4,5},{5,4},{6,7},{7,6},{8,9},{9,8},{10,11... | collective-permute-start | bytes 589832 | tf_op jit(solution)/shard_map/ppermute | solution.py:133
  28.8 2.0 %collective-permute-start.9 = (bf16[128,768]{1,0:T(8,128)(2,1)S(1)}, bf16[128,768]{1,0:T(8,128)(2,1)S(1)}, u32[]{:S(2)}, u32[]{:S(2)}) collective-permute-start(bf16[128,768]{1,0:T(8,128)(2,1)S(1)} %collective-permute-done.5), channel_id=1, source_target_pairs={{0,8},{1,57},{8,16},{9,1},{16,24},{17,9},{24,32},{25,17},{32,40},{... | collective-permute-start | bytes 589832 | tf_op jit(solution)/shard_map/ppermute | solution.py:130
  31.0 1.8 %fusion.37 = (f32[2048]{0:T(1024)S(1)}, f32[512,2048]{1,0:T(8,128)S(1)}) fusion(bf16[512,768]{1,0:T(8,128)(2,1)S(1)} %pad_maximum_fusion, bf16[2048,768]{1,0:T(8,128)(2,1)S(1)} %bitcast.88), kind=kOutput, calls=%fused_computation.113 | convolution fusion | flops 1611659264 | bytes 8134656 | tf_op jit(solution)/shard_map/kd,rd->kr/dot_general | solution.py:71
  32.8 1.1 %exponential_reduce_fusion = (f32[2048]{0:T(1024)S(1)}, f32[2048]{0:T(1024)S(1)}) fusion(f32[512,2048]{1,0:T(8,128)S(1)} %get-tuple-element.85, f32[2048]{0:T(1024)S(1)} %get-tuple-element.84, s32[2048]{0:T(1024)S(1)} %bitcast.95), kind=kLoop, calls=%fused_computation.3 | loop fusion | flops 5238784 | bytes 4227072 | tf_op jit(solution)/shard_map/reduce_sum | solution.py:78
  34.8 2.2 %collective-permute-start.12 = (bf16[128,768]{1,0:T(8,128)(2,1)S(1)}, bf16[128,768]{1,0:T(8,128)(2,1)S(1)}, u32[]{:S(2)}, u32[]{:S(2)}) collective-permute-start(bf16[128,768]{1,0:T(8,128)(2,1)S(1)} %collective-permute-done.8), channel_id=1, source_target_pairs={{0,8},{1,57},{8,16},{9,1},{16,24},{17,9},{24,32},{25,17},{32,40},{... | collective-permute-start | bytes 589832 | tf_op jit(solution)/shard_map/ppermute | solution.py:135
  37.7 2.0 %collective-permute-done.12 = bf16[128,768]{1,0:T(8,128)(2,1)S(1)} collective-permute-done((bf16[128,768]{1,0:T(8,128)(2,1)S(1)}, bf16[128,768]{1,0:T(8,128)(2,1)S(1)}, u32[]{:S(2)}, u32[]{:S(2)}) %collective-permute-start.12) | collective-permute-done | bytes 196640 | tf_op jit(solution)/shard_map/ppermute | solution.py:135
  41.8 3.7 %collective-permute-start.18 = (f32[24,128]{1,0:T(8,128)S(1)}, f32[24,128]{1,0:T(8,128)S(1)}, u32[]{:S(2)}, u32[]{:S(2)}) collective-permute-start(f32[24,128]{1,0:T(8,128)S(1)} %maximum_maximum_fusion), channel_id=1, source_target_pairs={{0,1},{1,0},{2,3},{3,2},{4,5},{5,4},{6,7},{7,6},{8,9},{9,8},{10,11... | collective-permute-start | bytes 36872 | tf_op jit(solution)/shard_map/ppermute | solution.py:53
  46.6 2.5 %collective-permute-done.19 = f32[24,128]{1,0:T(8,128)S(1)} collective-permute-done((f32[24,128]{1,0:T(8,128)S(1)}, f32[24,128]{1,0:T(8,128)S(1)}, u32[]{:S(2)}, u32[]{:S(2)}) %collective-permute-start.19) | collective-permute-done | bytes 12320 | tf_op jit(solution)/shard_map/ppermute | solution.py:54
  49.2 2.9 %collective-permute-start.20 = (f32[24,128]{1,0:T(8,128)S(1)}, f32[24,128]{1,0:T(8,128)S(1)}, u32[]{:S(2)}, u32[]{:S(2)}) collective-permute-start(f32[24,128]{1,0:T(8,128)S(1)} %add_select_fusion.3), channel_id=1, source_target_pairs={{0,16},{1,41},{8,24},{9,49},{16,32},{17,57},{24,40},{25,1},{32,48}... | collective-permute-start | bytes 36872 | tf_op jit(solution)/shard_map/ppermute | solution.py:55
  52.0 3.6 %collective-permute-start.21 = (f32[24,128]{1,0:T(8,128)S(1)}, f32[24,128]{1,0:T(8,128)S(1)}, u32[]{:S(2)}, u32[]{:S(2)}) collective-permute-start(f32[24,128]{1,0:T(8,128)S(1)} %add_select_fusion.3), channel_id=1, source_target_pairs={{1,57},{9,1},{17,9},{25,17},{33,25},{41,33},{49,41},{57,49},{3,59}... | collective-permute-start | bytes 36872 | tf_op jit(solution)/shard_map/ppermute | solution.py:56
  55.7 1.1 %collective-permute-done.21 = f32[24,128]{1,0:T(8,128)S(1)} collective-permute-done((f32[24,128]{1,0:T(8,128)S(1)}, f32[24,128]{1,0:T(8,128)S(1)}, u32[]{:S(2)}, u32[]{:S(2)}) %collective-permute-start.21) | collective-permute-done | bytes 12320 | tf_op jit(solution)/shard_map/ppermute | solution.py:56
  56.8 3.0 %collective-permute-start.22 = (f32[24,128]{1,0:T(8,128)S(1)}, f32[24,128]{1,0:T(8,128)S(1)}, u32[]{:S(2)}, u32[]{:S(2)}) collective-permute-start(f32[24,128]{1,0:T(8,128)S(1)} %add_select_fusion.2), channel_id=1, source_target_pairs={{0,4},{2,6},{4,0},{6,2},{1,5},{3,7},{5,1},{7,3},{8,12},{10,14},{12... | collective-permute-start | bytes 36872 | tf_op jit(solution)/shard_map/ppermute | solution.py:58
  60.2 2.3 %collective-permute-start.24 = (f32[24,128]{1,0:T(8,128)S(1)}, f32[24,128]{1,0:T(8,128)S(1)}, u32[]{:S(2)}, u32[]{:S(2)}) collective-permute-start(f32[24,128]{1,0:T(8,128)S(1)} %add_select_fusion.2), channel_id=1, source_target_pairs={{0,6},{2,0},{4,2},{6,4},{1,7},{3,1},{5,3},{7,5},{8,14},{10,8},{12,... | collective-permute-start | bytes 36872 | tf_op jit(solution)/shard_map/ppermute | solution.py:58
  62.5 1.1 %collective-permute-done.23 = f32[24,128]{1,0:T(8,128)S(1)} collective-permute-done((f32[24,128]{1,0:T(8,128)S(1)}, f32[24,128]{1,0:T(8,128)S(1)}, u32[]{:S(2)}, u32[]{:S(2)}) %collective-permute-start.23) | collective-permute-done | bytes 12320 | tf_op jit(solution)/shard_map/ppermute | solution.py:58
  63.6 2.6 %collective-permute-start.25 = (f32[24,128]{1,0:T(8,128)S(1)}, f32[24,128]{1,0:T(8,128)S(1)}, u32[]{:S(2)}, u32[]{:S(2)}) collective-permute-start(f32[24,128]{1,0:T(8,128)S(1)} %add_select_fusion.1), channel_id=1, source_target_pairs={{0,1},{1,0},{2,3},{3,2},{4,5},{5,4},{6,7},{7,6},{8,9},{9,8},{10,11... | collective-permute-start | bytes 36872 | tf_op jit(solution)/shard_map/ppermute | solution.py:59
  67.2 2.0 %subtract_convert_fusion = bf16[512,2048]{1,0:T(8,128)(2,1)S(1)} fusion(bf16[512,768]{1,0:T(8,128)(2,1)S(1)} %pad_maximum_fusion, bf16[2048,768]{1,0:T(8,128)(2,1)S(1)} %bitcast.89, f32[2048]{0:T(1024)S(1)} %slice_bitcast_fusion, s32[2048]{0:T(1024)S(1)} %bitcast.96), kind=kOutput, calls=%fused_computation | convolution fusion | flops 1615855616 | bytes 6045696 | tf_op jit(solution)/shard_map/kd,rd->kr/dot_general | solution.py:71
  69.1 1.4 %fusion.5 = f16[384,768]{1,0:T(8,128)(2,1)S(1)} fusion(bf16[2048,768]{1,0:T(8,128)(2,1)S(1)} %bitcast.90, bf16[512,2048]{1,0:T(8,128)(2,1)S(1)} %subtract_convert_fusion), kind=kOutput, calls=%fused_computation.7 | convolution fusion | flops 1208549376 | bytes 5308416 | tf_op jit(solution)/shard_map/dot_general | solution.py:168
  72.3 1.1 %collective-permute-start.30 = (f32[1,1]{1,0:T(1,128)}, f32[1,1]{1,0:T(1,128)}, u32[]{:S(2)}, u32[]{:S(2)}) collective-permute-start(f32[1,1]{1,0:T(1,128)} %bitcast.32), channel_id=1, source_target_pairs={{0,64},{64,128},{128,192},{192,0},{1,65},{65,129},{129,193},{193,1... | collective-permute-start | bytes 20 | tf_op jit(solution)/shard_map/ppermute | solution.py:180
  73.5 2.5 %collective-permute-start.26 = (f16[128,768]{1,0:T(8,128)(2,1)S(1)}, f16[128,768]{1,0:T(8,128)(2,1)S(1)}, u32[]{:S(2)}, u32[]{:S(2)}) collective-permute-start(f16[128,768]{1,0:T(8,128)(2,1)S(1)} %get-tuple-element.113), channel_id=1, source_target_pairs={{0,128},{64,192},{128,0},{192,64},{1,129},{65,193},{129,1},{193,65... | collective-permute-start | bytes 589832 | tf_op jit(solution)/shard_map/ppermute | solution.py:172
  76.0 2.7 %collective-permute-start.28 = (f16[128,768]{1,0:T(8,128)(2,1)S(1)}, f16[128,768]{1,0:T(8,128)(2,1)S(1)}, u32[]{:S(2)}, u32[]{:S(2)}) collective-permute-start(f16[128,768]{1,0:T(8,128)(2,1)S(1)} %get-tuple-element.114), channel_id=1, source_target_pairs={{0,192},{64,0},{128,64},{192,128},{1,193},{65,1},{129,65},{193,129... | collective-permute-start | bytes 589832 | tf_op jit(solution)/shard_map/ppermute | solution.py:172
  79.2 1.4 %collective-permute-done.26 = f16[128,768]{1,0:T(8,128)(2,1)S(1)} collective-permute-done((f16[128,768]{1,0:T(8,128)(2,1)S(1)}, f16[128,768]{1,0:T(8,128)(2,1)S(1)}, u32[]{:S(2)}, u32[]{:S(2)}) %collective-permute-start.26) | collective-permute-done | bytes 196640 | tf_op jit(solution)/shard_map/ppermute | solution.py:172
  80.6 1.6 %collective-permute-start.31 = (f32[1,1]{1,0:T(1,128)}, f32[1,1]{1,0:T(1,128)}, u32[]{:S(2)}, u32[]{:S(2)}) collective-permute-start(f32[1,1]{1,0:T(1,128)} %bitcast.32), channel_id=1, source_target_pairs={{0,192},{64,0},{128,64},{192,128},{1,193},{65,1},{129,65},{193,129... | collective-permute-start | bytes 20 | tf_op jit(solution)/shard_map/ppermute | solution.py:180
  82.2 3.5 %collective-permute-done.27 = f16[128,768]{1,0:T(8,128)(2,1)S(1)} collective-permute-done((f16[128,768]{1,0:T(8,128)(2,1)S(1)}, f16[128,768]{1,0:T(8,128)(2,1)S(1)}, u32[]{:S(2)}, u32[]{:S(2)}) %collective-permute-start.27) | collective-permute-done | bytes 196640 | tf_op jit(solution)/shard_map/ppermute | solution.py:172
  85.7 1.2 %divide_subtract_fusion = (f32[128,768]{1,0:T(8,128)}, f32[128,768]{1,0:T(8,128)}, f32[128,768]{1,0:T(8,128)}) fusion(f32[128,768]{1,0:T(8,128)S(1)} %copy-done, f32[128,768]{1,0:T(8,128)S(1)} %fusion.8, f16[128,768]{1,0:T(8,128)(2,1)S(1)} %collective-permute-done.28, f16[128,768]{1,0:T(8,128)(2,1)S(1)} %collective-permute-done.27, ...), kind=kLoop, calls=%fused_computation.13 | loop fusion | flops 1769472 | bytes 3342336 | tf_op jit(solution)/shard_map/sub | solution.py:42
  (101 shorter events, 15.0 us)
Async XLA Ops:
  1.7 16.7 %collective-permute-start.14 = (bf16[128,768]{1,0:T(8,128)(2,1)S(1)}, bf16[128,768]{1,0:T(8,128)(2,1)S(1)}, u32[]{:S(2)}, u32[]{:S(2)}) collective-permute-start(bf16[128,768]{1,0:T(8,128)(2,1)S(1)} %convert_element_type.88), channel_id=1, source_target_pairs={{0,192},{64,0},{128,64},{192,128},{1,193},{65,1},{129,65},{193,129... | collective-permute-start | bytes 589832 | tf_op jit(solution)/shard_map/ppermute | solution.py:143
  5.1 15.0 %collective-permute-start.15 = (bf16[128,768]{1,0:T(8,128)(2,1)S(1)}, bf16[128,768]{1,0:T(8,128)(2,1)S(1)}, u32[]{:S(2)}, u32[]{:S(2)}) collective-permute-start(bf16[128,768]{1,0:T(8,128)(2,1)S(1)} %convert_element_type.88), channel_id=1, source_target_pairs={{0,128},{64,192},{128,0},{192,64},{1,129},{65,193},{129,1},{193,65... | collective-permute-start | bytes 589832 | tf_op jit(solution)/shard_map/ppermute | solution.py:143
  5.6 14.5 %collective-permute-start.16 = (bf16[128,768]{1,0:T(8,128)(2,1)S(1)}, bf16[128,768]{1,0:T(8,128)(2,1)S(1)}, u32[]{:S(2)}, u32[]{:S(2)}) collective-permute-start(bf16[128,768]{1,0:T(8,128)(2,1)S(1)} %convert_element_type.88), channel_id=1, source_target_pairs={{0,64},{64,128},{128,192},{192,0},{1,65},{65,129},{129,193},{193,1... | collective-permute-start | bytes 589832 | tf_op jit(solution)/shard_map/ppermute | solution.py:143
  7.3 8.3 %collective-permute-start = (bf16[128,768]{1,0:T(8,128)(2,1)S(1)}, bf16[128,768]{1,0:T(8,128)(2,1)S(1)}, u32[]{:S(2)}, u32[]{:S(2)}) collective-permute-start(bf16[128,768]{1,0:T(8,128)(2,1)S(1)} %get-tuple-element.117), channel_id=1, source_target_pairs={{0,8},{1,57},{8,16},{9,1},{16,24},{17,9},{24,32},{25,17},{32,40},{... | collective-permute-start | bytes 589832 | tf_op jit(solution)/shard_map/ppermute | solution.py:116
  12.9 7.8 %collective-permute-start.1 = (bf16[128,768]{1,0:T(8,128)(2,1)S(1)}, bf16[128,768]{1,0:T(8,128)(2,1)S(1)}, u32[]{:S(2)}, u32[]{:S(2)}) collective-permute-start(bf16[128,768]{1,0:T(8,128)(2,1)S(1)} %get-tuple-element.116), channel_id=1, source_target_pairs={{0,8},{1,57},{8,16},{9,1},{16,24},{17,9},{24,32},{25,17},{32,40},{... | collective-permute-start | bytes 589832 | tf_op jit(solution)/shard_map/ppermute | solution.py:116
  15.5 9.7 %collective-permute-start.2 = (bf16[128,768]{1,0:T(8,128)(2,1)S(1)}, bf16[128,768]{1,0:T(8,128)(2,1)S(1)}, u32[]{:S(2)}, u32[]{:S(2)}) collective-permute-start(bf16[128,768]{1,0:T(8,128)(2,1)S(1)} %collective-permute-done), channel_id=1, source_target_pairs={{0,1},{1,0},{2,3},{3,2},{4,5},{5,4},{6,7},{7,6},{8,9},{9,8},{10,11... | collective-permute-start | bytes 589832 | tf_op jit(solution)/shard_map/ppermute | solution.py:122
  18.4 6.1 %collective-permute-start.4 = (bf16[128,768]{1,0:T(8,128)(2,1)S(1)}, bf16[128,768]{1,0:T(8,128)(2,1)S(1)}, u32[]{:S(2)}, u32[]{:S(2)}) collective-permute-start(bf16[128,768]{1,0:T(8,128)(2,1)S(1)} %collective-permute-done), channel_id=1, source_target_pairs={{0,8},{1,57},{8,16},{9,1},{16,24},{17,9},{24,32},{25,17},{32,40},{... | collective-permute-start | bytes 589832 | tf_op jit(solution)/shard_map/ppermute | solution.py:130
  20.2 20.0 %collective-permute-start.17 = (bf16[512,768]{1,0:T(8,128)(2,1)S(1)}, bf16[512,768]{1,0:T(8,128)(2,1)S(1)}, u32[]{:S(2)}, u32[]{:S(2)}) collective-permute-start(bf16[512,768]{1,0:T(8,128)(2,1)S(1)} %pad_maximum_fusion), channel_id=1, source_target_pairs={{0,1},{1,0},{2,3},{3,2},{4,5},{5,4},{6,7},{7,6},{8,9},{9,8},{10,11... | collective-permute-start | bytes 2359304 | tf_op jit(solution)/shard_map/ppermute | solution.py:146
  20.7 8.1 %collective-permute-start.3 = (bf16[128,768]{1,0:T(8,128)(2,1)S(1)}, bf16[128,768]{1,0:T(8,128)(2,1)S(1)}, u32[]{:S(2)}, u32[]{:S(2)}) collective-permute-start(bf16[128,768]{1,0:T(8,128)(2,1)S(1)} %collective-permute-done.1), channel_id=1, source_target_pairs={{0,1},{1,0},{2,3},{3,2},{4,5},{5,4},{6,7},{7,6},{8,9},{9,8},{10,11... | collective-permute-start | bytes 589832 | tf_op jit(solution)/shard_map/ppermute | solution.py:122
  21.3 5.8 %collective-permute-start.5 = (bf16[128,768]{1,0:T(8,128)(2,1)S(1)}, bf16[128,768]{1,0:T(8,128)(2,1)S(1)}, u32[]{:S(2)}, u32[]{:S(2)}) collective-permute-start(bf16[128,768]{1,0:T(8,128)(2,1)S(1)} %collective-permute-done.1), channel_id=1, source_target_pairs={{0,8},{1,57},{8,16},{9,1},{16,24},{17,9},{24,32},{25,17},{32,40},{... | collective-permute-start | bytes 589832 | tf_op jit(solution)/shard_map/ppermute | solution.py:130
  24.5 6.4 %collective-permute-start.6 = (bf16[128,768]{1,0:T(8,128)(2,1)S(1)}, bf16[128,768]{1,0:T(8,128)(2,1)S(1)}, u32[]{:S(2)}, u32[]{:S(2)}) collective-permute-start(bf16[128,768]{1,0:T(8,128)(2,1)S(1)} %collective-permute-done.4), channel_id=1, source_target_pairs={{0,1},{1,0},{2,3},{3,2},{4,5},{5,4},{6,7},{7,6},{8,9},{9,8},{10,11... | collective-permute-start | bytes 589832 | tf_op jit(solution)/shard_map/ppermute | solution.py:133
  25.3 8.7 %collective-permute-start.8 = (bf16[128,768]{1,0:T(8,128)(2,1)S(1)}, bf16[128,768]{1,0:T(8,128)(2,1)S(1)}, u32[]{:S(2)}, u32[]{:S(2)}) collective-permute-start(bf16[128,768]{1,0:T(8,128)(2,1)S(1)} %collective-permute-done.4), channel_id=1, source_target_pairs={{0,8},{1,57},{8,16},{9,1},{16,24},{17,9},{24,32},{25,17},{32,40},{... | collective-permute-start | bytes 589832 | tf_op jit(solution)/shard_map/ppermute | solution.py:130
  27.1 3.9 %collective-permute-start.7 = (bf16[128,768]{1,0:T(8,128)(2,1)S(1)}, bf16[128,768]{1,0:T(8,128)(2,1)S(1)}, u32[]{:S(2)}, u32[]{:S(2)}) collective-permute-start(bf16[128,768]{1,0:T(8,128)(2,1)S(1)} %collective-permute-done.5), channel_id=1, source_target_pairs={{0,1},{1,0},{2,3},{3,2},{4,5},{5,4},{6,7},{7,6},{8,9},{9,8},{10,11... | collective-permute-start | bytes 589832 | tf_op jit(solution)/shard_map/ppermute | solution.py:133
  28.8 5.6 %collective-permute-start.9 = (bf16[128,768]{1,0:T(8,128)(2,1)S(1)}, bf16[128,768]{1,0:T(8,128)(2,1)S(1)}, u32[]{:S(2)}, u32[]{:S(2)}) collective-permute-start(bf16[128,768]{1,0:T(8,128)(2,1)S(1)} %collective-permute-done.5), channel_id=1, source_target_pairs={{0,8},{1,57},{8,16},{9,1},{16,24},{17,9},{24,32},{25,17},{32,40},{... | collective-permute-start | bytes 589832 | tf_op jit(solution)/shard_map/ppermute | solution.py:130
  34.8 4.8 %collective-permute-start.12 = (bf16[128,768]{1,0:T(8,128)(2,1)S(1)}, bf16[128,768]{1,0:T(8,128)(2,1)S(1)}, u32[]{:S(2)}, u32[]{:S(2)}) collective-permute-start(bf16[128,768]{1,0:T(8,128)(2,1)S(1)} %collective-permute-done.8), channel_id=1, source_target_pairs={{0,8},{1,57},{8,16},{9,1},{16,24},{17,9},{24,32},{25,17},{32,40},{... | collective-permute-start | bytes 589832 | tf_op jit(solution)/shard_map/ppermute | solution.py:135
  37.0 9.5 %collective-permute-start.10 = (bf16[128,768]{1,0:T(8,128)(2,1)S(1)}, bf16[128,768]{1,0:T(8,128)(2,1)S(1)}, u32[]{:S(2)}, u32[]{:S(2)}) collective-permute-start(bf16[128,768]{1,0:T(8,128)(2,1)S(1)} %collective-permute-done.8), channel_id=1, source_target_pairs={{0,1},{1,0},{2,3},{3,2},{4,5},{5,4},{6,7},{7,6},{8,9},{9,8},{10,11... | collective-permute-start | bytes 589832 | tf_op jit(solution)/shard_map/ppermute | solution.py:133
  37.0 18.6 %collective-permute-start.11 = (bf16[128,768]{1,0:T(8,128)(2,1)S(1)}, bf16[128,768]{1,0:T(8,128)(2,1)S(1)}, u32[]{:S(2)}, u32[]{:S(2)}) collective-permute-start(bf16[128,768]{1,0:T(8,128)(2,1)S(1)} %collective-permute-done.9), channel_id=1, source_target_pairs={{0,1},{1,0},{2,3},{3,2},{4,5},{5,4},{6,7},{7,6},{8,9},{9,8},{10,11... | collective-permute-start | bytes 589832 | tf_op jit(solution)/shard_map/ppermute | solution.py:133
  41.8 4.5 %collective-permute-start.18 = (f32[24,128]{1,0:T(8,128)S(1)}, f32[24,128]{1,0:T(8,128)S(1)}, u32[]{:S(2)}, u32[]{:S(2)}) collective-permute-start(f32[24,128]{1,0:T(8,128)S(1)} %maximum_maximum_fusion), channel_id=1, source_target_pairs={{0,1},{1,0},{2,3},{3,2},{4,5},{5,4},{6,7},{7,6},{8,9},{9,8},{10,11... | collective-permute-start | bytes 36872 | tf_op jit(solution)/shard_map/ppermute | solution.py:53
  45.5 20.7 %collective-permute-start.13 = (bf16[128,768]{1,0:T(8,128)(2,1)S(1)}, bf16[128,768]{1,0:T(8,128)(2,1)S(1)}, u32[]{:S(2)}, u32[]{:S(2)}) collective-permute-start(bf16[128,768]{1,0:T(8,128)(2,1)S(1)} %collective-permute-done.12), channel_id=1, source_target_pairs={{0,1},{1,0},{2,3},{3,2},{4,5},{5,4},{6,7},{7,6},{8,9},{9,8},{10,11... | collective-permute-start | bytes 589832 | tf_op jit(solution)/shard_map/ppermute | solution.py:136
  46.5 2.6 %collective-permute-start.19 = (f32[24,128]{1,0:T(8,128)S(1)}, f32[24,128]{1,0:T(8,128)S(1)}, u32[]{:S(2)}, u32[]{:S(2)}) collective-permute-start(f32[24,128]{1,0:T(8,128)S(1)} %add_select_fusion.4), channel_id=1, source_target_pairs={{0,8},{1,57},{8,16},{9,1},{16,24},{17,9},{24,32},{25,17},{32,40},{... | collective-permute-start | bytes 36872 | tf_op jit(solution)/shard_map/ppermute | solution.py:54
  49.2 6.6 %collective-permute-start.20 = (f32[24,128]{1,0:T(8,128)S(1)}, f32[24,128]{1,0:T(8,128)S(1)}, u32[]{:S(2)}, u32[]{:S(2)}) collective-permute-start(f32[24,128]{1,0:T(8,128)S(1)} %add_select_fusion.3), channel_id=1, source_target_pairs={{0,16},{1,41},{8,24},{9,49},{16,32},{17,57},{24,40},{25,1},{32,48}... | collective-permute-start | bytes 36872 | tf_op jit(solution)/shard_map/ppermute | solution.py:55
  52.0 4.7 %collective-permute-start.21 = (f32[24,128]{1,0:T(8,128)S(1)}, f32[24,128]{1,0:T(8,128)S(1)}, u32[]{:S(2)}, u32[]{:S(2)}) collective-permute-start(f32[24,128]{1,0:T(8,128)S(1)} %add_select_fusion.3), channel_id=1, source_target_pairs={{1,57},{9,1},{17,9},{25,17},{33,25},{41,33},{49,41},{57,49},{3,59}... | collective-permute-start | bytes 36872 | tf_op jit(solution)/shard_map/ppermute | solution.py:56
  56.8 5.7 %collective-permute-start.22 = (f32[24,128]{1,0:T(8,128)S(1)}, f32[24,128]{1,0:T(8,128)S(1)}, u32[]{:S(2)}, u32[]{:S(2)}) collective-permute-start(f32[24,128]{1,0:T(8,128)S(1)} %add_select_fusion.2), channel_id=1, source_target_pairs={{0,4},{2,6},{4,0},{6,2},{1,5},{3,7},{5,1},{7,3},{8,12},{10,14},{12... | collective-permute-start | bytes 36872 | tf_op jit(solution)/shard_map/ppermute | solution.py:58
  59.8 3.8 %collective-permute-start.23 = (f32[24,128]{1,0:T(8,128)S(1)}, f32[24,128]{1,0:T(8,128)S(1)}, u32[]{:S(2)}, u32[]{:S(2)}) collective-permute-start(f32[24,128]{1,0:T(8,128)S(1)} %add_select_fusion.2), channel_id=1, source_target_pairs={{0,2},{2,4},{4,6},{6,0},{1,3},{3,5},{5,7},{7,1},{8,10},{10,12},{12... | collective-permute-start | bytes 36872 | tf_op jit(solution)/shard_map/ppermute | solution.py:58
  60.2 3.4 %collective-permute-start.24 = (f32[24,128]{1,0:T(8,128)S(1)}, f32[24,128]{1,0:T(8,128)S(1)}, u32[]{:S(2)}, u32[]{:S(2)}) collective-permute-start(f32[24,128]{1,0:T(8,128)S(1)} %add_select_fusion.2), channel_id=1, source_target_pairs={{0,6},{2,0},{4,2},{6,4},{1,7},{3,1},{5,3},{7,5},{8,14},{10,8},{12,... | collective-permute-start | bytes 36872 | tf_op jit(solution)/shard_map/ppermute | solution.py:58
  63.6 3.5 %collective-permute-start.25 = (f32[24,128]{1,0:T(8,128)S(1)}, f32[24,128]{1,0:T(8,128)S(1)}, u32[]{:S(2)}, u32[]{:S(2)}) collective-permute-start(f32[24,128]{1,0:T(8,128)S(1)} %add_select_fusion.1), channel_id=1, source_target_pairs={{0,1},{1,0},{2,3},{3,2},{4,5},{5,4},{6,7},{7,6},{8,9},{9,8},{10,11... | collective-permute-start | bytes 36872 | tf_op jit(solution)/shard_map/ppermute | solution.py:59
  71.2 15.7 %collective-permute-start.29 = (f32[1,1]{1,0:T(1,128)}, f32[1,1]{1,0:T(1,128)}, u32[]{:S(2)}, u32[]{:S(2)}) collective-permute-start(f32[1,1]{1,0:T(1,128)} %bitcast.32), channel_id=1, source_target_pairs={{0,128},{64,192},{128,0},{192,64},{1,129},{65,193},{129,1},{193,65... | collective-permute-start | bytes 20 | tf_op jit(solution)/shard_map/ppermute | solution.py:180
  72.3 14.7 %collective-permute-start.30 = (f32[1,1]{1,0:T(1,128)}, f32[1,1]{1,0:T(1,128)}, u32[]{:S(2)}, u32[]{:S(2)}) collective-permute-start(f32[1,1]{1,0:T(1,128)} %bitcast.32), channel_id=1, source_target_pairs={{0,64},{64,128},{128,192},{192,0},{1,65},{65,129},{129,193},{193,1... | collective-permute-start | bytes 20 | tf_op jit(solution)/shard_map/ppermute | solution.py:180
  73.5 7.2 %collective-permute-start.26 = (f16[128,768]{1,0:T(8,128)(2,1)S(1)}, f16[128,768]{1,0:T(8,128)(2,1)S(1)}, u32[]{:S(2)}, u32[]{:S(2)}) collective-permute-start(f16[128,768]{1,0:T(8,128)(2,1)S(1)} %get-tuple-element.113), channel_id=1, source_target_pairs={{0,128},{64,192},{128,0},{192,64},{1,129},{65,193},{129,1},{193,65... | collective-permute-start | bytes 589832 | tf_op jit(solution)/shard_map/ppermute | solution.py:172
  76.0 9.7 %collective-permute-start.27 = (f16[128,768]{1,0:T(8,128)(2,1)S(1)}, f16[128,768]{1,0:T(8,128)(2,1)S(1)}, u32[]{:S(2)}, u32[]{:S(2)}) collective-permute-start(f16[128,768]{1,0:T(8,128)(2,1)S(1)} %get-tuple-element.115), channel_id=1, source_target_pairs={{0,64},{64,128},{128,192},{192,0},{1,65},{65,129},{129,193},{193,1... | collective-permute-start | bytes 589832 | tf_op jit(solution)/shard_map/ppermute | solution.py:172
  76.0 9.7 %collective-permute-start.28 = (f16[128,768]{1,0:T(8,128)(2,1)S(1)}, f16[128,768]{1,0:T(8,128)(2,1)S(1)}, u32[]{:S(2)}, u32[]{:S(2)}) collective-permute-start(f16[128,768]{1,0:T(8,128)(2,1)S(1)} %get-tuple-element.114), channel_id=1, source_target_pairs={{0,192},{64,0},{128,64},{192,128},{1,193},{65,1},{129,65},{193,129... | collective-permute-start | bytes 589832 | tf_op jit(solution)/shard_map/ppermute | solution.py:172
  80.6 6.4 %collective-permute-start.31 = (f32[1,1]{1,0:T(1,128)}, f32[1,1]{1,0:T(1,128)}, u32[]{:S(2)}, u32[]{:S(2)}) collective-permute-start(f32[1,1]{1,0:T(1,128)} %bitcast.32), channel_id=1, source_target_pairs={{0,192},{64,0},{128,64},{192,128},{1,193},{65,1},{129,65},{193,129... | collective-permute-start | bytes 20 | tf_op jit(solution)/shard_map/ppermute | solution.py:180
  (4 other events, 65.5 us)

commit v5 on v4

--- a/solution.py
+++ b/solution.py
@@ -159,11 +159,12 @@
         rows = put(rows, block, row)
     state = jnp.concatenate([state, hit, jnp.zeros((7, HALF), jnp.float32)])
     rows = rows.reshape(-1, width)
+    logits = lax.optimization_barrier(logits_of(rows, lists))
     state = over_lists(state, at_first)
 
-    rows, lists, log_norm = lax.optimization_barrier((rows, lists, state[:16].reshape(-1)))
+    rows, log_norm = lax.optimization_barrier((rows, state[:16].reshape(-1)))
     hot = is_target(targets).astype(jnp.float32)
-    weights = (jnp.exp(logits_of(rows, lists) - log_norm[None, :]) - hot).astype(jnp.bfloat16)
+    weights = (jnp.exp(logits - log_norm[None, :]) - hot).astype(jnp.bfloat16)
     weights = lax.optimization_barrier(weights)
     sent = jnp.dot(weights[: 3 * OWN], rows, preferred_element_type=jnp.float32)
     sent = (sent * SCALE).astype(jnp.float16)

time: 90.9 us -> 94 us (1.034)
  the two profiles are of different devices: /device:TPU:1 before, /device:TPU:30 now
where the time goes in v5:
time: 94 us; the launch traced here: 93.7 us
  waiting for transfers between devices  48.5 us (52%)
  starting transfers between devices  23.5 us (25%)
  matrix products  7.9 us (8%)
  other arithmetic  6.41 us (7%)
  between operations  4.79 us (5%)
  local copies, waits for them, and re-layouts  2.63 us (3%)
    ppermute x6, waiting for transfers between devices, body(): parts[i] = lax.ppermute(parts[i], ('z', 'c'), OPPOSITE)  14.3 us
    ppermute x3, waiting for transfers between devices, body(): lax.ppermute(sent[some], 'x', turn(4, step)).astype(jnp.float32)  7.14 us
    ppermute x1, waiting for transfers between devices, body(): last = lax.ppermute(parts[0], ('z', 'c'), OPPOSITE)  6.34 us
    dot_general x8, matrix products, logits_of(): jnp.einsum('kd,rd->kr', lists, rows, preferred_element_type=jnp.float32)  5.94 us
    ppermute x3, waiting for transfers between devices, over_lists(): lax.ppermute(state, 'y', turn(4, step))  5.14 us
    ppermute x1, waiting for transfers between devices, over_lists(): lax.ppermute(pair, ('z', 'c'), [(z * 2 + c, (z + (2, -3)[c]) % 8 * 2 + c)...  5.09 us
    ppermute x1, waiting for transfers between devices, over_lists(): pair = join(state, lax.ppermute(state, ('z', 'c'), OPPOSITE))  4.85 us
    ppermute x3, starting transfers between devices, body(): lax.ppermute(sent[some], 'x', turn(4, step)).astype(jnp.float32)  4.45 us
  transfers between devices with their start and end apart: 32, of which 13 were waited for; matrix products, arithmetic and copies ran while one was open for 13% of the time, Pallas kernels for 0%

profile of v5, /device:TPU:30, one launch (start us, length us, event | category | flops | bytes accessed | tf_op | source)
XLA Modules:
  0.0 93.7 jit_solution(5537262638595019958)
XLA Ops:
  0.6 1.1 %convert_element_type.72 = bf16[128,768]{1,0:T(8,128)(2,1)S(1)} convert(f32[128,768]{1,0:T(8,128)} %param.7) | non-fusion elementwise | flops 98304 | bytes 589824 | tf_op jit(solution)/shard_map/convert_element_type | solution.py:140
  2.3 2.4 %collective-permute-start.1 = (bf16[128,768]{1,0:T(8,128)(2,1)S(1)}, bf16[128,768]{1,0:T(8,128)(2,1)S(1)}, u32[]{:S(2)}, u32[]{:S(2)}) collective-permute-start(bf16[128,768]{1,0:T(8,128)(2,1)S(1)} %convert_element_type.72), channel_id=1, source_target_pairs={{0,128},{64,192},{128,0},{192,64},{1,129},{65,193},{129,1},{193,65... | collective-permute-start | bytes 589832 | tf_op jit(solution)/shard_map/ppermute | solution.py:143
  4.7 1.0 %dynamic-slice_bitcast_fusion = (bf16[128,768]{1,0:T(8,128)(2,1)S(1)}, bf16[128,768]{1,0:T(8,128)(2,1)S(1)}) fusion(bf16[2,128,768]{2,1,0:T(8,128)(2,1)} %bitcast.92, u32[]{:T(128)S(6)} %sub.182, u32[]{:T(128)S(6)} %convert_element_type.73), kind=kLoop, calls=%fused_computation.48 | loop fusion | bytes 786440 | tf_op jit(solution)/shard_map/squeeze | solution.py:114
  5.7 2.0 %collective-permute-start.3 = (bf16[128,768]{1,0:T(8,128)(2,1)S(1)}, bf16[128,768]{1,0:T(8,128)(2,1)S(1)}, u32[]{:S(2)}, u32[]{:S(2)}) collective-permute-start(bf16[128,768]{1,0:T(8,128)(2,1)S(1)} %get-tuple-element.115), channel_id=1, source_target_pairs={{0,8},{1,57},{8,16},{9,1},{16,24},{17,9},{24,32},{25,17},{32,40},{... | collective-permute-start | bytes 589832 | tf_op jit(solution)/shard_map/ppermute | solution.py:116
  7.7 1.9 %collective-permute-start.4 = (bf16[128,768]{1,0:T(8,128)(2,1)S(1)}, bf16[128,768]{1,0:T(8,128)(2,1)S(1)}, u32[]{:S(2)}, u32[]{:S(2)}) collective-permute-start(bf16[128,768]{1,0:T(8,128)(2,1)S(1)} %get-tuple-element.114), channel_id=1, source_target_pairs={{0,8},{1,57},{8,16},{9,1},{16,24},{17,9},{24,32},{25,17},{32,40},{... | collective-permute-start | bytes 589832 | tf_op jit(solution)/shard_map/ppermute | solution.py:116
  9.7 0.8 reshape.249
  10.6 4.7 %collective-permute-done.3 = bf16[128,768]{1,0:T(8,128)(2,1)S(1)} collective-permute-done((bf16[128,768]{1,0:T(8,128)(2,1)S(1)}, bf16[128,768]{1,0:T(8,128)(2,1)S(1)}, u32[]{:S(2)}, u32[]{:S(2)}) %collective-permute-start.3) | collective-permute-done | bytes 196640 | tf_op jit(solution)/shard_map/ppermute | solution.py:116
  15.4 2.3 %collective-permute-start.17 = (bf16[512,768]{1,0:T(8,128)(2,1)S(1)}, bf16[512,768]{1,0:T(8,128)(2,1)S(1)}, u32[]{:S(2)}, u32[]{:S(2)}) collective-permute-start(bf16[512,768]{1,0:T(8,128)(2,1)S(1)} %pad_maximum_fusion), channel_id=1, source_target_pairs={{0,1},{1,0},{2,3},{3,2},{4,5},{5,4},{6,7},{7,6},{8,9},{9,8},{10,11... | collective-permute-start | bytes 2359304 | tf_op jit(solution)/shard_map/ppermute | solution.py:146
  18.4 3.8 %collective-permute-done.7 = bf16[128,768]{1,0:T(8,128)(2,1)S(1)} collective-permute-done((bf16[128,768]{1,0:T(8,128)(2,1)S(1)}, bf16[128,768]{1,0:T(8,128)(2,1)S(1)}, u32[]{:S(2)}, u32[]{:S(2)}) %collective-permute-start.7) | collective-permute-done | bytes 196640 | tf_op jit(solution)/shard_map/ppermute | solution.py:130
  22.2 3.0 %collective-permute-done.8 = bf16[128,768]{1,0:T(8,128)(2,1)S(1)} collective-permute-done((bf16[128,768]{1,0:T(8,128)(2,1)S(1)}, bf16[128,768]{1,0:T(8,128)(2,1)S(1)}, u32[]{:S(2)}, u32[]{:S(2)}) %collective-permute-start.8) | collective-permute-done | bytes 196640 | tf_op jit(solution)/shard_map/ppermute | solution.py:130
  25.7 1.0 %collective-permute-done.10 = bf16[128,768]{1,0:T(8,128)(2,1)S(1)} collective-permute-done((bf16[128,768]{1,0:T(8,128)(2,1)S(1)}, bf16[128,768]{1,0:T(8,128)(2,1)S(1)}, u32[]{:S(2)}, u32[]{:S(2)}) %collective-permute-start.10) | collective-permute-done | bytes 196640 | tf_op jit(solution)/shard_map/ppermute | solution.py:133
  26.7 1.8 %fusion.37 = (f32[2048]{0:T(1024)S(1)}, f32[512,2048]{1,0:T(8,128)S(1)}) fusion(bf16[512,768]{1,0:T(8,128)(2,1)S(1)} %pad_maximum_fusion, bf16[2048,768]{1,0:T(8,128)(2,1)S(1)} %bitcast.88), kind=kOutput, calls=%fused_computation.113 | convolution fusion | flops 1611659264 | bytes 8134656 | tf_op jit(solution)/shard_map/kd,rd->kr/dot_general | solution.py:71
  28.5 1.1 %exponential_reduce_fusion = (f32[2048]{0:T(1024)S(1)}, f32[2048]{0:T(1024)S(1)}) fusion(f32[512,2048]{1,0:T(8,128)S(1)} %get-tuple-element.84, f32[2048]{0:T(1024)S(1)} %get-tuple-element.83, s32[2048]{0:T(1024)S(1)} %bitcast.95), kind=kLoop, calls=%fused_computation.3 | loop fusion | flops 5238784 | bytes 4227072 | tf_op jit(solution)/shard_map/reduce_sum | solution.py:78
  29.6 2.8 %collective-permute-done.12 = bf16[128,768]{1,0:T(8,128)(2,1)S(1)} collective-permute-done((bf16[128,768]{1,0:T(8,128)(2,1)S(1)}, bf16[128,768]{1,0:T(8,128)(2,1)S(1)}, u32[]{:S(2)}, u32[]{:S(2)}) %collective-permute-start.12) | collective-permute-done | bytes 196640 | tf_op jit(solution)/shard_map/ppermute | solution.py:130
  34.1 6.3 %collective-permute-done.15 = bf16[128,768]{1,0:T(8,128)(2,1)S(1)} collective-permute-done((bf16[128,768]{1,0:T(8,128)(2,1)S(1)}, bf16[128,768]{1,0:T(8,128)(2,1)S(1)}, u32[]{:S(2)}, u32[]{:S(2)}) %collective-permute-start.15) | collective-permute-done | bytes 196640 | tf_op jit(solution)/shard_map/ppermute | solution.py:135
  43.3 0.8 collective-permute-done.18
  44.3 4.9 %collective-permute-done.19 = f32[24,128]{1,0:T(8,128)S(1)} collective-permute-done((f32[24,128]{1,0:T(8,128)S(1)}, f32[24,128]{1,0:T(8,128)S(1)}, u32[]{:S(2)}, u32[]{:S(2)}) %collective-permute-start.19) | collective-permute-done | bytes 12320 | tf_op jit(solution)/shard_map/ppermute | solution.py:54
  50.0 5.1 %collective-permute-done.20 = f32[24,128]{1,0:T(8,128)S(1)} collective-permute-done((f32[24,128]{1,0:T(8,128)S(1)}, f32[24,128]{1,0:T(8,128)S(1)}, u32[]{:S(2)}, u32[]{:S(2)}) %collective-permute-start.20) | collective-permute-done | bytes 12320 | tf_op jit(solution)/shard_map/ppermute | solution.py:55
  55.1 0.8 collective-permute-start.24
  55.9 2.5 %collective-permute-start.23 = (f32[24,128]{1,0:T(8,128)S(1)}, f32[24,128]{1,0:T(8,128)S(1)}, u32[]{:S(2)}, u32[]{:S(2)}) collective-permute-start(f32[24,128]{1,0:T(8,128)S(1)} %add_select_fusion.2), channel_id=1, source_target_pairs={{0,2},{2,4},{4,6},{6,0},{1,3},{3,5},{5,7},{7,1},{8,10},{10,12},{12... | collective-permute-start | bytes 36872 | tf_op jit(solution)/shard_map/ppermute | solution.py:58
  58.5 1.6 %collective-permute-done.24 = f32[24,128]{1,0:T(8,128)S(1)} collective-permute-done((f32[24,128]{1,0:T(8,128)S(1)}, f32[24,128]{1,0:T(8,128)S(1)}, u32[]{:S(2)}, u32[]{:S(2)}) %collective-permute-start.24) | collective-permute-done | bytes 12320 | tf_op jit(solution)/shard_map/ppermute | solution.py:58
  60.1 3.5 %collective-permute-done.22 = f32[24,128]{1,0:T(8,128)S(1)} collective-permute-done((f32[24,128]{1,0:T(8,128)S(1)}, f32[24,128]{1,0:T(8,128)S(1)}, u32[]{:S(2)}, u32[]{:S(2)}) %collective-permute-start.22) | collective-permute-done | bytes 12320 | tf_op jit(solution)/shard_map/ppermute | solution.py:58
  64.0 1.8 %fusion.39 = f32[512,2048]{1,0:T(8,128)S(1)} fusion(bf16[512,768]{1,0:T(8,128)(2,1)S(1)} %pad_maximum_fusion, bf16[2048,768]{1,0:T(8,128)(2,1)S(1)} %bitcast.89), kind=kOutput, calls=%fused_computation.115 | convolution fusion | flops 1610612736 | bytes 8126464 | tf_op jit(solution)/shard_map/kd,rd->kr/dot_general | solution.py:71
  65.9 1.0 %subtract_convert_fusion = bf16[512,2048]{1,0:T(8,128)(2,1)S(1)} fusion(f32[512,2048]{1,0:T(8,128)S(1)} %fusion.39, f32[2048]{0:T(1024)S(1)} %slice_bitcast_fusion, s32[2048]{0:T(1024)S(1)} %bitcast.96), kind=kLoop, calls=%fused_computation | loop fusion | flops 5242880 | bytes 6307840 | tf_op jit(solution)/shard_map/convert_element_type | solution.py:167
  66.9 1.4 %fusion.5 = f16[384,768]{1,0:T(8,128)(2,1)S(1)} fusion(bf16[2048,768]{1,0:T(8,128)(2,1)S(1)} %bitcast.90, bf16[512,2048]{1,0:T(8,128)(2,1)S(1)} %subtract_convert_fusion), kind=kOutput, calls=%fused_computation.7 | convolution fusion | flops 1208549376 | bytes 5308416 | tf_op jit(solution)/shard_map/dot_general | solution.py:169
  69.1 3.3 %collective-permute-start.29 = (f32[1,1]{1,0:T(1,128)}, f32[1,1]{1,0:T(1,128)}, u32[]{:S(2)}, u32[]{:S(2)}) collective-permute-start(f32[1,1]{1,0:T(1,128)} %bitcast.32), channel_id=1, source_target_pairs={{0,128},{64,192},{128,0},{192,64},{1,129},{65,193},{129,1},{193,65... | collective-permute-start | bytes 20 | tf_op jit(solution)/shard_map/ppermute | solution.py:181
  72.9 1.5 %collective-permute-start.28 = (f16[128,768]{1,0:T(8,128)(2,1)S(1)}, f16[128,768]{1,0:T(8,128)(2,1)S(1)}, u32[]{:S(2)}, u32[]{:S(2)}) collective-permute-start(f16[128,768]{1,0:T(8,128)(2,1)S(1)} %get-tuple-element.112), channel_id=1, source_target_pairs={{0,192},{64,0},{128,64},{192,128},{1,193},{65,1},{129,65},{193,129... | collective-permute-start | bytes 589832 | tf_op jit(solution)/shard_map/ppermute | solution.py:173
  74.4 1.7 %collective-permute-start.27 = (f16[128,768]{1,0:T(8,128)(2,1)S(1)}, f16[128,768]{1,0:T(8,128)(2,1)S(1)}, u32[]{:S(2)}, u32[]{:S(2)}) collective-permute-start(f16[128,768]{1,0:T(8,128)(2,1)S(1)} %get-tuple-element.113), channel_id=1, source_target_pairs={{0,64},{64,128},{128,192},{192,0},{1,65},{65,129},{129,193},{193,1... | collective-permute-start | bytes 589832 | tf_op jit(solution)/shard_map/ppermute | solution.py:173
  76.1 1.2 %collective-permute-start.26 = (f16[128,768]{1,0:T(8,128)(2,1)S(1)}, f16[128,768]{1,0:T(8,128)(2,1)S(1)}, u32[]{:S(2)}, u32[]{:S(2)}) collective-permute-start(f16[128,768]{1,0:T(8,128)(2,1)S(1)} %get-tuple-element.111), channel_id=1, source_target_pairs={{0,128},{64,192},{128,0},{192,64},{1,129},{65,193},{129,1},{193,65... | collective-permute-start | bytes 589832 | tf_op jit(solution)/shard_map/ppermute | solution.py:173
  77.9 7.1 %collective-permute-done.28 = f16[128,768]{1,0:T(8,128)(2,1)S(1)} collective-permute-done((f16[128,768]{1,0:T(8,128)(2,1)S(1)}, f16[128,768]{1,0:T(8,128)(2,1)S(1)}, u32[]{:S(2)}, u32[]{:S(2)}) %collective-permute-start.28) | collective-permute-done | bytes 196640 | tf_op jit(solution)/shard_map/ppermute | solution.py:173
  85.1 1.2 %divide_subtract_fusion = (f32[128,768]{1,0:T(8,128)}, f32[128,768]{1,0:T(8,128)}, f32[128,768]{1,0:T(8,128)}) fusion(f32[128,768]{1,0:T(8,128)S(1)} %copy-done, f32[128,768]{1,0:T(8,128)S(1)} %fusion.8, f16[128,768]{1,0:T(8,128)(2,1)S(1)} %collective-permute-done.28, f16[128,768]{1,0:T(8,128)(2,1)S(1)} %collective-permute-done.27, ...), kind=kLoop, calls=%fused_computation.13 | loop fusion | flops 1769472 | bytes 3342336 | tf_op jit(solution)/shard_map/sub | solution.py:42
  86.3 3.8 %collective-permute-done.31 = f32[1,1]{1,0:T(1,128)} collective-permute-done((f32[1,1]{1,0:T(1,128)}, f32[1,1]{1,0:T(1,128)}, u32[]{:S(2)}, u32[]{:S(2)}) %collective-permute-start.31) | collective-permute-done | bytes 36 | tf_op jit(solution)/shard_map/ppermute | solution.py:181
  (102 shorter events, 9.6 us)
Async XLA Ops:
  1.7 13.6 %collective-permute-start.2 = (bf16[128,768]{1,0:T(8,128)(2,1)S(1)}, bf16[128,768]{1,0:T(8,128)(2,1)S(1)}, u32[]{:S(2)}, u32[]{:S(2)}) collective-permute-start(bf16[128,768]{1,0:T(8,128)(2,1)S(1)} %convert_element_type.72), channel_id=1, source_target_pairs={{0,64},{64,128},{128,192},{192,0},{1,65},{65,129},{129,193},{193,1... | collective-permute-start | bytes 589832 | tf_op jit(solution)/shard_map/ppermute | solution.py:143
  2.3 13.1 %collective-permute-start.1 = (bf16[128,768]{1,0:T(8,128)(2,1)S(1)}, bf16[128,768]{1,0:T(8,128)(2,1)S(1)}, u32[]{:S(2)}, u32[]{:S(2)}) collective-permute-start(bf16[128,768]{1,0:T(8,128)(2,1)S(1)} %convert_element_type.72), channel_id=1, source_target_pairs={{0,128},{64,192},{128,0},{192,64},{1,129},{65,193},{129,1},{193,65... | collective-permute-start | bytes 589832 | tf_op jit(solution)/shard_map/ppermute | solution.py:143
  4.7 10.7 %collective-permute-start = (bf16[128,768]{1,0:T(8,128)(2,1)S(1)}, bf16[128,768]{1,0:T(8,128)(2,1)S(1)}, u32[]{:S(2)}, u32[]{:S(2)}) collective-permute-start(bf16[128,768]{1,0:T(8,128)(2,1)S(1)} %convert_element_type.72), channel_id=1, source_target_pairs={{0,192},{64,0},{128,64},{192,128},{1,193},{65,1},{129,65},{193,129... | collective-permute-start | bytes 589832 | tf_op jit(solution)/shard_map/ppermute | solution.py:143
  5.7 9.6 %collective-permute-start.3 = (bf16[128,768]{1,0:T(8,128)(2,1)S(1)}, bf16[128,768]{1,0:T(8,128)(2,1)S(1)}, u32[]{:S(2)}, u32[]{:S(2)}) collective-permute-start(bf16[128,768]{1,0:T(8,128)(2,1)S(1)} %get-tuple-element.115), channel_id=1, source_target_pairs={{0,8},{1,57},{8,16},{9,1},{16,24},{17,9},{24,32},{25,17},{32,40},{... | collective-permute-start | bytes 589832 | tf_op jit(solution)/shard_map/ppermute | solution.py:116
  7.7 10.4 %collective-permute-start.4 = (bf16[128,768]{1,0:T(8,128)(2,1)S(1)}, bf16[128,768]{1,0:T(8,128)(2,1)S(1)}, u32[]{:S(2)}, u32[]{:S(2)}) collective-permute-start(bf16[128,768]{1,0:T(8,128)(2,1)S(1)} %get-tuple-element.114), channel_id=1, source_target_pairs={{0,8},{1,57},{8,16},{9,1},{16,24},{17,9},{24,32},{25,17},{32,40},{... | collective-permute-start | bytes 589832 | tf_op jit(solution)/shard_map/ppermute | solution.py:116
  15.3 6.9 %collective-permute-start.5 = (bf16[128,768]{1,0:T(8,128)(2,1)S(1)}, bf16[128,768]{1,0:T(8,128)(2,1)S(1)}, u32[]{:S(2)}, u32[]{:S(2)}) collective-permute-start(bf16[128,768]{1,0:T(8,128)(2,1)S(1)} %collective-permute-done.3), channel_id=1, source_target_pairs={{0,1},{1,0},{2,3},{3,2},{4,5},{5,4},{6,7},{7,6},{8,9},{9,8},{10,11... | collective-permute-start | bytes 589832 | tf_op jit(solution)/shard_map/ppermute | solution.py:122
  15.3 6.9 %collective-permute-start.7 = (bf16[128,768]{1,0:T(8,128)(2,1)S(1)}, bf16[128,768]{1,0:T(8,128)(2,1)S(1)}, u32[]{:S(2)}, u32[]{:S(2)}) collective-permute-start(bf16[128,768]{1,0:T(8,128)(2,1)S(1)} %collective-permute-done.3), channel_id=1, source_target_pairs={{0,8},{1,57},{8,16},{9,1},{16,24},{17,9},{24,32},{25,17},{32,40},{... | collective-permute-start | bytes 589832 | tf_op jit(solution)/shard_map/ppermute | solution.py:130
  15.4 25.6 %collective-permute-start.17 = (bf16[512,768]{1,0:T(8,128)(2,1)S(1)}, bf16[512,768]{1,0:T(8,128)(2,1)S(1)}, u32[]{:S(2)}, u32[]{:S(2)}) collective-permute-start(bf16[512,768]{1,0:T(8,128)(2,1)S(1)} %pad_maximum_fusion), channel_id=1, source_target_pairs={{0,1},{1,0},{2,3},{3,2},{4,5},{5,4},{6,7},{7,6},{8,9},{9,8},{10,11... | collective-permute-start | bytes 2359304 | tf_op jit(solution)/shard_map/ppermute | solution.py:146
  18.2 7.1 %collective-permute-start.6 = (bf16[128,768]{1,0:T(8,128)(2,1)S(1)}, bf16[128,768]{1,0:T(8,128)(2,1)S(1)}, u32[]{:S(2)}, u32[]{:S(2)}) collective-permute-start(bf16[128,768]{1,0:T(8,128)(2,1)S(1)} %collective-permute-done.4), channel_id=1, source_target_pairs={{0,1},{1,0},{2,3},{3,2},{4,5},{5,4},{6,7},{7,6},{8,9},{9,8},{10,11... | collective-permute-start | bytes 589832 | tf_op jit(solution)/shard_map/ppermute | solution.py:122
  18.3 7.0 %collective-permute-start.8 = (bf16[128,768]{1,0:T(8,128)(2,1)S(1)}, bf16[128,768]{1,0:T(8,128)(2,1)S(1)}, u32[]{:S(2)}, u32[]{:S(2)}) collective-permute-start(bf16[128,768]{1,0:T(8,128)(2,1)S(1)} %collective-permute-done.4), channel_id=1, source_target_pairs={{0,8},{1,57},{8,16},{9,1},{16,24},{17,9},{24,32},{25,17},{32,40},{... | collective-permute-start | bytes 589832 | tf_op jit(solution)/shard_map/ppermute | solution.py:130
  22.2 3.4 %collective-permute-start.9 = (bf16[128,768]{1,0:T(8,128)(2,1)S(1)}, bf16[128,768]{1,0:T(8,128)(2,1)S(1)}, u32[]{:S(2)}, u32[]{:S(2)}) collective-permute-start(bf16[128,768]{1,0:T(8,128)(2,1)S(1)} %collective-permute-done.7), channel_id=1, source_target_pairs={{0,1},{1,0},{2,3},{3,2},{4,5},{5,4},{6,7},{7,6},{8,9},{9,8},{10,11... | collective-permute-start | bytes 589832 | tf_op jit(solution)/shard_map/ppermute | solution.py:133
  22.2 10.8 %collective-permute-start.11 = (bf16[128,768]{1,0:T(8,128)(2,1)S(1)}, bf16[128,768]{1,0:T(8,128)(2,1)S(1)}, u32[]{:S(2)}, u32[]{:S(2)}) collective-permute-start(bf16[128,768]{1,0:T(8,128)(2,1)S(1)} %collective-permute-done.7), channel_id=1, source_target_pairs={{0,8},{1,57},{8,16},{9,1},{16,24},{17,9},{24,32},{25,17},{32,40},{... | collective-permute-start | bytes 589832 | tf_op jit(solution)/shard_map/ppermute | solution.py:130
  25.2 1.4 %collective-permute-start.10 = (bf16[128,768]{1,0:T(8,128)(2,1)S(1)}, bf16[128,768]{1,0:T(8,128)(2,1)S(1)}, u32[]{:S(2)}, u32[]{:S(2)}) collective-permute-start(bf16[128,768]{1,0:T(8,128)(2,1)S(1)} %collective-permute-done.8), channel_id=1, source_target_pairs={{0,1},{1,0},{2,3},{3,2},{4,5},{5,4},{6,7},{7,6},{8,9},{9,8},{10,11... | collective-permute-start | bytes 589832 | tf_op jit(solution)/shard_map/ppermute | solution.py:133
  25.3 7.1 %collective-permute-start.12 = (bf16[128,768]{1,0:T(8,128)(2,1)S(1)}, bf16[128,768]{1,0:T(8,128)(2,1)S(1)}, u32[]{:S(2)}, u32[]{:S(2)}) collective-permute-start(bf16[128,768]{1,0:T(8,128)(2,1)S(1)} %collective-permute-done.8), channel_id=1, source_target_pairs={{0,8},{1,57},{8,16},{9,1},{16,24},{17,9},{24,32},{25,17},{32,40},{... | collective-permute-start | bytes 589832 | tf_op jit(solution)/shard_map/ppermute | solution.py:130
  32.8 11.5 %collective-permute-start.14 = (bf16[128,768]{1,0:T(8,128)(2,1)S(1)}, bf16[128,768]{1,0:T(8,128)(2,1)S(1)}, u32[]{:S(2)}, u32[]{:S(2)}) collective-permute-start(bf16[128,768]{1,0:T(8,128)(2,1)S(1)} %collective-permute-done.12), channel_id=1, source_target_pairs={{0,1},{1,0},{2,3},{3,2},{4,5},{5,4},{6,7},{7,6},{8,9},{9,8},{10,11... | collective-permute-start | bytes 589832 | tf_op jit(solution)/shard_map/ppermute | solution.py:133
  33.0 10.3 %collective-permute-start.13 = (bf16[128,768]{1,0:T(8,128)(2,1)S(1)}, bf16[128,768]{1,0:T(8,128)(2,1)S(1)}, u32[]{:S(2)}, u32[]{:S(2)}) collective-permute-start(bf16[128,768]{1,0:T(8,128)(2,1)S(1)} %collective-permute-done.11), channel_id=1, source_target_pairs={{0,1},{1,0},{2,3},{3,2},{4,5},{5,4},{6,7},{7,6},{8,9},{9,8},{10,11... | collective-permute-start | bytes 589832 | tf_op jit(solution)/shard_map/ppermute | solution.py:133
  33.6 6.9 %collective-permute-start.15 = (bf16[128,768]{1,0:T(8,128)(2,1)S(1)}, bf16[128,768]{1,0:T(8,128)(2,1)S(1)}, u32[]{:S(2)}, u32[]{:S(2)}) collective-permute-start(bf16[128,768]{1,0:T(8,128)(2,1)S(1)} %collective-permute-done.11), channel_id=1, source_target_pairs={{0,8},{1,57},{8,16},{9,1},{16,24},{17,9},{24,32},{25,17},{32,40},{... | collective-permute-start | bytes 589832 | tf_op jit(solution)/shard_map/ppermute | solution.py:135
  40.8 17.6 %collective-permute-start.16 = (bf16[128,768]{1,0:T(8,128)(2,1)S(1)}, bf16[128,768]{1,0:T(8,128)(2,1)S(1)}, u32[]{:S(2)}, u32[]{:S(2)}) collective-permute-start(bf16[128,768]{1,0:T(8,128)(2,1)S(1)} %collective-permute-done.15), channel_id=1, source_target_pairs={{0,1},{1,0},{2,3},{3,2},{4,5},{5,4},{6,7},{7,6},{8,9},{9,8},{10,11... | collective-permute-start | bytes 589832 | tf_op jit(solution)/shard_map/ppermute | solution.py:136
  42.7 1.4 %collective-permute-start.18 = (f32[24,128]{1,0:T(8,128)S(1)}, f32[24,128]{1,0:T(8,128)S(1)}, u32[]{:S(2)}, u32[]{:S(2)}) collective-permute-start(f32[24,128]{1,0:T(8,128)S(1)} %maximum_maximum_fusion), channel_id=1, source_target_pairs={{0,1},{1,0},{2,3},{3,2},{4,5},{5,4},{6,7},{7,6},{8,9},{9,8},{10,11... | collective-permute-start | bytes 36872 | tf_op jit(solution)/shard_map/ppermute | solution.py:53
  44.2 5.0 %collective-permute-start.19 = (f32[24,128]{1,0:T(8,128)S(1)}, f32[24,128]{1,0:T(8,128)S(1)}, u32[]{:S(2)}, u32[]{:S(2)}) collective-permute-start(f32[24,128]{1,0:T(8,128)S(1)} %add_select_fusion.4), channel_id=1, source_target_pairs={{0,8},{1,57},{8,16},{9,1},{16,24},{17,9},{24,32},{25,17},{32,40},{... | collective-permute-start | bytes 36872 | tf_op jit(solution)/shard_map/ppermute | solution.py:54
  49.2 5.8 %collective-permute-start.20 = (f32[24,128]{1,0:T(8,128)S(1)}, f32[24,128]{1,0:T(8,128)S(1)}, u32[]{:S(2)}, u32[]{:S(2)}) collective-permute-start(f32[24,128]{1,0:T(8,128)S(1)} %add_select_fusion.3), channel_id=1, source_target_pairs={{0,16},{1,41},{8,24},{9,49},{16,32},{17,57},{24,40},{25,1},{32,48}... | collective-permute-start | bytes 36872 | tf_op jit(solution)/shard_map/ppermute | solution.py:55
  49.3 5.8 %collective-permute-start.21 = (f32[24,128]{1,0:T(8,128)S(1)}, f32[24,128]{1,0:T(8,128)S(1)}, u32[]{:S(2)}, u32[]{:S(2)}) collective-permute-start(f32[24,128]{1,0:T(8,128)S(1)} %add_select_fusion.3), channel_id=1, source_target_pairs={{1,57},{9,1},{17,9},{25,17},{33,25},{41,33},{49,41},{57,49},{3,59}... | collective-permute-start | bytes 36872 | tf_op jit(solution)/shard_map/ppermute | solution.py:56
  55.1 4.9 %collective-permute-start.24 = (f32[24,128]{1,0:T(8,128)S(1)}, f32[24,128]{1,0:T(8,128)S(1)}, u32[]{:S(2)}, u32[]{:S(2)}) collective-permute-start(f32[24,128]{1,0:T(8,128)S(1)} %add_select_fusion.2), channel_id=1, source_target_pairs={{0,6},{2,0},{4,2},{6,4},{1,7},{3,1},{5,3},{7,5},{8,14},{10,8},{12,... | collective-permute-start | bytes 36872 | tf_op jit(solution)/shard_map/ppermute | solution.py:58
  55.9 4.2 %collective-permute-start.23 = (f32[24,128]{1,0:T(8,128)S(1)}, f32[24,128]{1,0:T(8,128)S(1)}, u32[]{:S(2)}, u32[]{:S(2)}) collective-permute-start(f32[24,128]{1,0:T(8,128)S(1)} %add_select_fusion.2), channel_id=1, source_target_pairs={{0,2},{2,4},{4,6},{6,0},{1,3},{3,5},{5,7},{7,1},{8,10},{10,12},{12... | collective-permute-start | bytes 36872 | tf_op jit(solution)/shard_map/ppermute | solution.py:58
  58.4 5.2 %collective-permute-start.22 = (f32[24,128]{1,0:T(8,128)S(1)}, f32[24,128]{1,0:T(8,128)S(1)}, u32[]{:S(2)}, u32[]{:S(2)}) collective-permute-start(f32[24,128]{1,0:T(8,128)S(1)} %add_select_fusion.2), channel_id=1, source_target_pairs={{0,4},{2,6},{4,0},{6,2},{1,5},{3,7},{5,1},{7,3},{8,12},{10,14},{12... | collective-permute-start | bytes 36872 | tf_op jit(solution)/shard_map/ppermute | solution.py:58
  63.7 2.1 %collective-permute-start.25 = (f32[24,128]{1,0:T(8,128)S(1)}, f32[24,128]{1,0:T(8,128)S(1)}, u32[]{:S(2)}, u32[]{:S(2)}) collective-permute-start(f32[24,128]{1,0:T(8,128)S(1)} %add_select_fusion.1), channel_id=1, source_target_pairs={{0,1},{1,0},{2,3},{3,2},{4,5},{5,4},{6,7},{7,6},{8,9},{9,8},{10,11... | collective-permute-start | bytes 36872 | tf_op jit(solution)/shard_map/ppermute | solution.py:59
  69.1 17.2 %collective-permute-start.29 = (f32[1,1]{1,0:T(1,128)}, f32[1,1]{1,0:T(1,128)}, u32[]{:S(2)}, u32[]{:S(2)}) collective-permute-start(f32[1,1]{1,0:T(1,128)} %bitcast.32), channel_id=1, source_target_pairs={{0,128},{64,192},{128,0},{192,64},{1,129},{65,193},{129,1},{193,65... | collective-permute-start | bytes 20 | tf_op jit(solution)/shard_map/ppermute | solution.py:181
  72.4 13.9 %collective-permute-start.30 = (f32[1,1]{1,0:T(1,128)}, f32[1,1]{1,0:T(1,128)}, u32[]{:S(2)}, u32[]{:S(2)}) collective-permute-start(f32[1,1]{1,0:T(1,128)} %bitcast.32), channel_id=1, source_target_pairs={{0,64},{64,128},{128,192},{192,0},{1,65},{65,129},{129,193},{193,1... | collective-permute-start | bytes 20 | tf_op jit(solution)/shard_map/ppermute | solution.py:181
  72.9 12.2 %collective-permute-start.28 = (f16[128,768]{1,0:T(8,128)(2,1)S(1)}, f16[128,768]{1,0:T(8,128)(2,1)S(1)}, u32[]{:S(2)}, u32[]{:S(2)}) collective-permute-start(f16[128,768]{1,0:T(8,128)(2,1)S(1)} %get-tuple-element.112), channel_id=1, source_target_pairs={{0,192},{64,0},{128,64},{192,128},{1,193},{65,1},{129,65},{193,129... | collective-permute-start | bytes 589832 | tf_op jit(solution)/shard_map/ppermute | solution.py:173
  74.4 10.6 %collective-permute-start.27 = (f16[128,768]{1,0:T(8,128)(2,1)S(1)}, f16[128,768]{1,0:T(8,128)(2,1)S(1)}, u32[]{:S(2)}, u32[]{:S(2)}) collective-permute-start(f16[128,768]{1,0:T(8,128)(2,1)S(1)} %get-tuple-element.113), channel_id=1, source_target_pairs={{0,64},{64,128},{128,192},{192,0},{1,65},{65,129},{129,193},{193,1... | collective-permute-start | bytes 589832 | tf_op jit(solution)/shard_map/ppermute | solution.py:173
  76.1 8.9 %collective-permute-start.26 = (f16[128,768]{1,0:T(8,128)(2,1)S(1)}, f16[128,768]{1,0:T(8,128)(2,1)S(1)}, u32[]{:S(2)}, u32[]{:S(2)}) collective-permute-start(f16[128,768]{1,0:T(8,128)(2,1)S(1)} %get-tuple-element.111), channel_id=1, source_target_pairs={{0,128},{64,192},{128,0},{192,64},{1,129},{65,193},{129,1},{193,65... | collective-permute-start | bytes 589832 | tf_op jit(solution)/shard_map/ppermute | solution.py:173
  85.0 5.0 %collective-permute-start.31 = (f32[1,1]{1,0:T(1,128)}, f32[1,1]{1,0:T(1,128)}, u32[]{:S(2)}, u32[]{:S(2)}) collective-permute-start(f32[1,1]{1,0:T(1,128)} %bitcast.32), channel_id=1, source_target_pairs={{0,192},{64,0},{128,64},{192,128},{1,193},{65,1},{129,65},{193,129... | collective-permute-start | bytes 20 | tf_op jit(solution)/shard_map/ppermute | solution.py:181
  (4 other events, 67.6 us)
